TPU v7x, 32 devices: a whole 2x2x4 slice. The times are simulated.
32 devices in a mesh: dp: 8 (over y, x, core), expert: 4 (over z).
Axes of the slice: x: 2, y: 2, z: 4, core: 2. Of those that a mesh axis runs over, the one named last changes fastest.
Arguments:
- layer_input: bfloat16 [10240, 2048], P(('dp', 'expert')), may hold values from -6 to 6
- cotangent: bfloat16 [10240, 2048], P(('dp', 'expert')), may hold values from -6 to 6
- cont_ids: int32 [10240], P('dp'), may hold values from 0 to 2, as said below
- attn_routes: int32 [10240, 2], P('dp'), may hold values from 0 to 3, all different within a row; in each aligned block of 320 rows (0 to 319, 320 to 639, ...) at most 180 rows name the same one
- attn_gates: float32 [10240, 2], P(('dp', 'expert')), may hold values from 0.25 to 1
- mlp_routes: int32 [10240, 2], P(('dp', 'expert')), may hold values from 0 to 3, all different within a row; in each aligned block of 320 rows (0 to 319, 320 to 639, ...) at most 180 rows name the same one
- mlp_gates: float32 [10240, 2], P(('dp', 'expert')), may hold values from 0.25 to 1
- gain_attn: bfloat16 [2048], P(('dp', 'expert')), may hold values from 0.5 to 1.5
- gain_mlp: bfloat16 [2048], P(('dp', 'expert')), may hold values from 0.5 to 1.5
- kv_weight: bfloat16 [2048, 4096], P(('dp', 'expert')), may hold values from -0.125 to 0.125
- query_weight: bfloat16 [2048, 4, 2048], P('dp', 'expert'), may hold values from -0.125 to 0.125
- output_weight: bfloat16 [2048, 4, 2048], P('dp', 'expert'), may hold values from -0.5 to 0.5
- mlp_weight: bfloat16 [5632, 4, 3, 2048], P('dp', 'expert'), may hold values from -0.125 to 0.125
Outputs:
- output: bfloat16 [10240, 2048], P(('dp', 'expert'))
- grad_input: float32 [10240, 2048], P(('dp', 'expert'))
- grad_gain_attn: float32 [2048], P(('dp', 'expert'))
- grad_gain_mlp: float32 [2048], P(('dp', 'expert'))
- grad_kv_weight: float32 [2048, 4096], P(('dp', 'expert'))
- grad_query_weight: float32 [2048, 4, 2048], P('dp', 'expert')
- grad_output_weight: float32 [2048, 4, 2048], P('dp', 'expert')
- grad_mlp_weight: float32 [5632, 4, 3, 2048], P('dp', 'expert')
Inputs may be any that keep to these rules, and one draw needn't show every extreme that they name: `cont_ids`: in each group of 1280 consecutive rows the first 1024 have id 0 and ids 1 to 2 follow in order; continuation 1 starts at place 1024, and continuation c > 1 at place 1024 + (c - 1) * 128 plus a shift drawn evenly from -64 to 63. `attn_routes`: each row names 2 different experts; in the rows of one device no expert is named by more than 180 rows, a bound that some block reaches. `mlp_routes`: each row names 2 different experts; in the rows of one device no expert is named by more than 180 rows, a bound that some block reaches.
All inputs are finite; a program needn't handle non-finite values.
Results may differ from a plain program's by a relative error of at most 0.02.
Values may be sent and summed in bfloat16 or wider, within the bound.
A program may use at most 640 MiB of HBM per device.

v0:
```python
import math

import jax
import jax.numpy as jnp
from jax import lax
from jax.sharding import PartitionSpec as P

HEAD = 128
PROMPT = 1024
CONTS = 2
GROUP_TOK = 1280


norm_eps = 1e-06
rope_base = 10000.0
neg_fill = -1e30
contract_last = (((1,), (1,)), ((), ()))
contract_first = (((0,), (0,)), ((), ()))


def rope_angles(positions, head_size):
    half_size = head_size // 2
    freq_steps = jnp.arange(half_size, dtype=jnp.float32)
    inverse_freq = jnp.exp(-math.log(rope_base) * 2.0 * freq_steps / head_size)
    angle_table = positions.astype(jnp.float32)[:, None] * inverse_freq[None, :]
    return (jnp.cos(angle_table), jnp.sin(angle_table))


def rotate(values, cosine, sine):
    half_size = cosine.shape[1]
    head_count = values.shape[1] // (2 * half_size)
    shaped = values.reshape(values.shape[0], head_count, 2 * half_size)
    first_half = shaped[:, :, :half_size]
    second_half = shaped[:, :, half_size:]
    cos_part = cosine[:, None, :]
    sin_part = sine[:, None, :]
    turned = jnp.concatenate(
        [
            first_half * cos_part - second_half * sin_part,
            second_half * cos_part + first_half * sin_part,
        ],
        axis=2,
    )
    return turned.reshape(values.shape)


def token_positions(cont_ids):
    row_count = cont_ids.shape[0]
    group_count = row_count // GROUP_TOK
    places = jnp.arange(row_count, dtype=jnp.int32) % GROUP_TOK
    labels = jnp.arange(CONTS + 1, dtype=jnp.int32)
    one_hot = (cont_ids[:, None] == labels[None, :]).astype(jnp.int32)
    counts = jnp.sum(one_hot.reshape(group_count, GROUP_TOK, CONTS + 1), axis=1)
    starts = jnp.cumsum(counts, axis=1) - counts
    starts_tok = jnp.broadcast_to(starts[:, None, :], (group_count, GROUP_TOK, CONTS + 1)).reshape(
        row_count, CONTS + 1
    )
    start_of = jnp.sum(starts_tok * one_hot, axis=1)
    return (places, places - start_of + PROMPT * (cont_ids > 0).astype(jnp.int32))


def rms_parts(values):
    row_scale = lax.rsqrt(jnp.mean(values * values, axis=-1, keepdims=True) + norm_eps)
    return (values * row_scale, row_scale)


def rms_back(grad_out, normed, row_scale, gain_vec):
    through = grad_out * gain_vec
    grad_gain = jnp.sum(grad_out * normed, axis=0)
    grad_in = row_scale * (through - normed * jnp.mean(through * normed, axis=-1, keepdims=True))
    return (grad_in, grad_gain)


def ranks_of(route_block, experts):
    flat_ids = route_block.reshape(-1)
    labels = jnp.arange(experts, dtype=jnp.int32)
    one_hot = (flat_ids[:, None] == labels[None, :]).astype(jnp.int32)
    slot_rank = jnp.sum((jnp.cumsum(one_hot, axis=0) - one_hot) * one_hot, axis=1)
    return (flat_ids, slot_rank)


def slot_table(flat_ids, slot_rank, targets, capacity):
    slot_ids = jnp.arange(capacity, dtype=jnp.int32)
    match = (
        (flat_ids[None, :, None] == targets[:, None, None])
        & (slot_rank[None, :, None] == slot_ids[None, None, :])
    ).astype(jnp.int32)
    places = jnp.arange(flat_ids.shape[0], dtype=jnp.int32)
    assign = jnp.sum(match * places[None, :, None], axis=1)
    live = jnp.sum(match, axis=1)
    return (assign, live)


def unit_block(rows_in, rows_grad, piece):
    gate_rows = piece[:, 0, 0, :]
    up_rows = piece[:, 0, 1, :]
    down_rows = piece[:, 0, 2, :]
    gate_val = lax.dot_general(
        rows_in, gate_rows, contract_last, preferred_element_type=jnp.float32
    )
    up_val = lax.dot_general(rows_in, up_rows, contract_last, preferred_element_type=jnp.float32)
    sigma = jax.nn.sigmoid(gate_val)
    active = gate_val * sigma
    hidden = (active * up_val).astype(jnp.bfloat16)
    out_term = jnp.dot(hidden, down_rows, preferred_element_type=jnp.float32)
    grad_hidden = lax.dot_general(
        rows_grad, down_rows, contract_last, preferred_element_type=jnp.float32
    )
    grad_gate = (grad_hidden * up_val * sigma * (1.0 + gate_val * (1.0 - sigma))).astype(
        jnp.bfloat16
    )
    grad_up = (grad_hidden * active).astype(jnp.bfloat16)
    in_term = jnp.dot(grad_gate, gate_rows, preferred_element_type=jnp.float32) + jnp.dot(
        grad_up, up_rows, preferred_element_type=jnp.float32
    )
    return (out_term, in_term, hidden, grad_gate, grad_up)


def unit_grads(rows_in, rows_grad, hidden, grad_gate, grad_up):
    gate_term = lax.dot_general(
        grad_gate, rows_in, contract_first, preferred_element_type=jnp.float32
    )
    up_term = lax.dot_general(grad_up, rows_in, contract_first, preferred_element_type=jnp.float32)
    down_term = lax.dot_general(
        hidden, rows_grad, contract_first, preferred_element_type=jnp.float32
    )
    return jnp.stack([gate_term, up_term, down_term], axis=1)[:, None, :, :]


def local(
    layer_input,
    cotangent,
    cont_ids,
    attn_routes,
    attn_gates,
    mlp_routes,
    mlp_gates,
    gain_attn,
    gain_mlp,
    kv_weight,
    query_weight,
    output_weight,
    mlp_weight,
):
    experts = lax.axis_size("expert")
    expert_id = lax.axis_index("expert")
    tok_dev = layer_input.shape[0]
    width = layer_input.shape[1]
    per_token = attn_routes.shape[1]
    capacity = tok_dev * per_token * 9 // (8 * experts)
    slot_total = experts * capacity
    score_scale = 1.0 / math.sqrt(HEAD)
    expert_ids = jnp.arange(experts, dtype=jnp.int32)
    gain_one, gain_two, kv_full = (
        lax.all_gather(gain_attn, ("dp", "expert"), axis=0, tiled=True),
        lax.all_gather(gain_mlp, ("dp", "expert"), axis=0, tiled=True),
        lax.all_gather(kv_weight, ("dp", "expert"), axis=0, tiled=True),
    )
    query_full, output_full = (
        lax.all_gather(query_weight, "dp", axis=0, tiled=True),
        lax.all_gather(output_weight, "dp", axis=0, tiled=True),
    )
    query_full = query_full[:, 0, :]
    output_full = output_full[:, 0, :]
    features = query_full.shape[1]
    head_count = features // HEAD
    places_row, positions_row = token_positions(cont_ids)
    groups_row = jnp.arange(cont_ids.shape[0], dtype=jnp.int32) // GROUP_TOK
    first_row = expert_id * tok_dev
    positions_mine = lax.dynamic_slice_in_dim(positions_row, first_row, tok_dev)
    cos_mine, sin_mine = rope_angles(positions_mine, HEAD)
    input_f32 = layer_input.astype(jnp.float32)
    normed_one, scale_one = rms_parts(input_f32)
    gain_one_f = gain_one.astype(jnp.float32)
    hidden_low = (normed_one * gain_one_f).astype(jnp.bfloat16)
    kv_proj = jnp.dot(hidden_low, kv_full, preferred_element_type=jnp.float32)
    keys_low = rotate(kv_proj[:, :features], cos_mine, sin_mine).astype(jnp.bfloat16)
    values_low = kv_proj[:, features:].astype(jnp.bfloat16)
    kv_low = jnp.concatenate([keys_low, values_low], axis=1)
    routes_mine = lax.dynamic_slice_in_dim(attn_routes, first_row, tok_dev)
    attn_flat, attn_rank = ranks_of(routes_mine, experts)
    attn_assign, attn_live = slot_table(attn_flat, attn_rank, expert_ids, capacity)
    attn_rows = attn_assign // per_token
    attn_back = (attn_flat * capacity + attn_rank).reshape(tok_dev, per_token)
    picked = hidden_low[attn_rows] * attn_live.astype(jnp.bfloat16)[:, :, None]
    kv_copies = jnp.broadcast_to(kv_low[None], (experts,) + kv_low.shape)
    got_rows, got_kv = (
        lax.all_to_all(picked, "expert", split_axis=0, concat_axis=0, tiled=True),
        lax.all_to_all(kv_copies, "expert", split_axis=0, concat_axis=0, tiled=True),
    )
    query_rows = got_rows.reshape(slot_total, width)
    kv_all = got_kv.reshape(-1, 2 * features)

    def owner_block(block_routes):
        block_flat, block_rank = ranks_of(block_routes, experts)
        block_assign, block_live = slot_table(
            block_flat, block_rank, jnp.reshape(expert_id, (1,)), capacity
        )
        return block_assign[0]

    owner_assign = jax.vmap(owner_block)(attn_routes.reshape(experts, tok_dev, per_token))
    owner_rows = (owner_assign // per_token + expert_ids[:, None] * tok_dev).reshape(-1)
    query_pos = positions_row[owner_rows]
    query_place = places_row[owner_rows]
    query_group = groups_row[owner_rows]
    query_cont = cont_ids[owner_rows]
    allowed = (
        (query_group[:, None] == groups_row[None, :])
        & (places_row[None, :] <= query_place[:, None])
        & ((cont_ids[None, :] == 0) | (cont_ids[None, :] == query_cont[:, None]))
    )
    query_pre = jnp.dot(query_rows, query_full, preferred_element_type=jnp.float32)
    cos_query, sin_query = rope_angles(query_pos, HEAD)
    query_low = rotate(query_pre, cos_query, sin_query).astype(jnp.bfloat16)
    query_heads = query_low.reshape(slot_total, head_count, HEAD).transpose(1, 0, 2)
    key_heads = kv_all[:, :features].reshape(-1, head_count, HEAD).transpose(1, 0, 2)
    value_heads = kv_all[:, features:].reshape(-1, head_count, HEAD).transpose(1, 0, 2)

    def head_forward(operands):
        query_one, key_one, value_one = operands
        scores = (
            lax.dot_general(query_one, key_one, contract_last, preferred_element_type=jnp.float32)
            * score_scale
        )
        scores = jnp.where(allowed, scores, neg_fill)
        row_peak = jnp.max(scores, axis=1, keepdims=True)
        weights = jnp.exp(scores - row_peak)
        totals = jnp.sum(weights, axis=1, keepdims=True)
        prob_low = (weights / totals).astype(jnp.bfloat16)
        return (
            jnp.dot(prob_low, value_one, preferred_element_type=jnp.float32),
            (row_peak + jnp.log(totals))[:, 0],
        )

    attended, log_totals = lax.map(head_forward, (query_heads, key_heads, value_heads))
    attn_low = attended.transpose(1, 0, 2).reshape(slot_total, features).astype(jnp.bfloat16)
    result_low = jnp.dot(attn_low, output_full, preferred_element_type=jnp.float32).astype(
        jnp.bfloat16
    )
    result_back = lax.all_to_all(
        result_low.reshape(experts, capacity, width),
        "expert",
        split_axis=0,
        concat_axis=0,
        tiled=True,
    )
    result_tok = result_back.reshape(slot_total, width)[attn_back].astype(jnp.float32)
    residual = input_f32 + jnp.sum(attn_gates[:, :, None] * result_tok, axis=1)
    normed_two, scale_two = rms_parts(residual)
    gain_two_f = gain_two.astype(jnp.float32)
    second_low = (normed_two * gain_two_f).astype(jnp.bfloat16)
    mlp_flat, mlp_rank = ranks_of(mlp_routes, experts)
    mlp_assign, mlp_live = slot_table(mlp_flat, mlp_rank, expert_ids, capacity)
    mlp_rows = mlp_assign // per_token
    mlp_back = (mlp_flat * capacity + mlp_rank).reshape(tok_dev, per_token)
    slot_gate = mlp_gates.reshape(-1)[mlp_assign] * mlp_live.astype(jnp.float32)
    cot_f32 = cotangent.astype(jnp.float32)
    send_in = second_low[mlp_rows] * mlp_live.astype(jnp.bfloat16)[:, :, None]
    send_grad = (slot_gate[:, :, None] * cot_f32[mlp_rows]).astype(jnp.bfloat16)
    got_in, got_grad = (
        lax.all_to_all(send_in, "expert", split_axis=0, concat_axis=0, tiled=True),
        lax.all_to_all(send_grad, "expert", split_axis=0, concat_axis=0, tiled=True),
    )
    owner_in = got_in.reshape(slot_total, width)
    owner_grad = got_grad.reshape(slot_total, width)
    out_term, in_term, hidden_piece, gate_piece, up_piece = unit_block(
        owner_in, owner_grad, lax.all_gather(mlp_weight, "dp", axis=0, tiled=True)
    )
    grad_mlp_weight = lax.psum_scatter(
        unit_grads(owner_in, owner_grad, hidden_piece, gate_piece, up_piece).astype(jnp.bfloat16),
        "dp",
        scatter_dimension=0,
        tiled=True,
    ).astype(jnp.float32)
    mixed_back, in_back = (
        lax.all_to_all(
            out_term.astype(jnp.bfloat16).reshape(experts, capacity, width),
            "expert",
            split_axis=0,
            concat_axis=0,
            tiled=True,
        ),
        lax.all_to_all(
            in_term.astype(jnp.bfloat16).reshape(experts, capacity, width),
            "expert",
            split_axis=0,
            concat_axis=0,
            tiled=True,
        ),
    )
    mixed_tok = mixed_back.reshape(slot_total, width)[mlp_back].astype(jnp.float32)
    final = residual + jnp.sum(mlp_gates[:, :, None] * mixed_tok, axis=1)
    output = final.astype(jnp.bfloat16)
    grad_second = jnp.sum(in_back.reshape(slot_total, width)[mlp_back].astype(jnp.float32), axis=1)
    grad_resid_part, grad_gain_two = rms_back(grad_second, normed_two, scale_two, gain_two_f)
    grad_resid = cot_f32 + grad_resid_part
    attn_slot_gate = attn_gates.reshape(-1)[attn_assign] * attn_live.astype(jnp.float32)
    send_cot = (attn_slot_gate[:, :, None] * grad_resid[attn_rows]).astype(jnp.bfloat16)
    got_cot = lax.all_to_all(send_cot, "expert", split_axis=0, concat_axis=0, tiled=True)
    grad_result = got_cot.reshape(slot_total, width)
    grad_attn = lax.dot_general(
        grad_result, output_full, contract_last, preferred_element_type=jnp.float32
    ).astype(jnp.bfloat16)
    grad_heads = grad_attn.reshape(slot_total, head_count, HEAD).transpose(1, 0, 2)

    def head_backward(operands):
        query_one, key_one, value_one, log_one, grad_one = operands
        scores = (
            lax.dot_general(query_one, key_one, contract_last, preferred_element_type=jnp.float32)
            * score_scale
        )
        scores = jnp.where(allowed, scores, neg_fill)
        prob_full = jnp.exp(scores - log_one[:, None])
        grad_prob = lax.dot_general(
            grad_one, value_one, contract_last, preferred_element_type=jnp.float32
        )
        row_inner = jnp.sum(prob_full * grad_prob, axis=1, keepdims=True)
        grad_scores = (prob_full * (grad_prob - row_inner)).astype(jnp.bfloat16)
        grad_query_one = (
            jnp.dot(grad_scores, key_one, preferred_element_type=jnp.float32) * score_scale
        )
        grad_key_one = (
            lax.dot_general(
                grad_scores, query_one, contract_first, preferred_element_type=jnp.float32
            )
            * score_scale
        )
        grad_value_one = lax.dot_general(
            prob_full.astype(jnp.bfloat16),
            grad_one,
            contract_first,
            preferred_element_type=jnp.float32,
        )
        return (grad_query_one, grad_key_one, grad_value_one)

    grad_query_heads, grad_key_heads, grad_value_heads = lax.map(
        head_backward, (query_heads, key_heads, value_heads, log_totals, grad_heads)
    )
    grad_query = grad_query_heads.transpose(1, 0, 2).reshape(slot_total, features)
    grad_query_low = rotate(grad_query, cos_query, -sin_query).astype(jnp.bfloat16)
    grad_rows = (
        lax.dot_general(
            grad_query_low, query_full, contract_last, preferred_element_type=jnp.float32
        )
        .astype(jnp.bfloat16)
        .astype(jnp.float32)
    )
    grad_keys = grad_key_heads.transpose(1, 0, 2).reshape(-1, features)
    grad_values = grad_value_heads.transpose(1, 0, 2).reshape(-1, features)
    grad_kv_term = jnp.concatenate([grad_keys, grad_values], axis=1).reshape(
        experts, tok_dev, 2 * features
    )
    rows_back, kv_parts = (
        lax.all_to_all(
            grad_rows.reshape(experts, capacity, width).astype(jnp.bfloat16),
            "expert",
            split_axis=0,
            concat_axis=0,
            tiled=True,
        ).astype(jnp.float32),
        lax.all_to_all(
            grad_kv_term.astype(jnp.bfloat16), "expert", split_axis=0, concat_axis=0, tiled=True
        ).astype(grad_kv_term.dtype),
    )
    kv_sum = jnp.sum(kv_parts, axis=0)
    grad_kv_low = jnp.concatenate(
        [
            rotate(kv_sum[:, :features], cos_mine, -sin_mine).astype(jnp.bfloat16),
            kv_sum[:, features:].astype(jnp.bfloat16),
        ],
        axis=1,
    )
    grad_first = lax.dot_general(
        grad_kv_low, kv_full, contract_last, preferred_element_type=jnp.float32
    )
    grad_first = grad_first + jnp.sum(rows_back.reshape(slot_total, width)[attn_back], axis=1)
    grad_in_part, grad_gain_one = rms_back(grad_first, normed_one, scale_one, gain_one_f)
    grad_input = grad_resid + grad_in_part
    grad_kv_local = lax.dot_general(
        hidden_low, grad_kv_low, contract_first, preferred_element_type=jnp.float32
    )
    grad_gain_attn, grad_gain_mlp, grad_kv_weight = (
        lax.psum_scatter(grad_gain_one, ("dp", "expert"), scatter_dimension=0, tiled=True),
        lax.psum_scatter(grad_gain_two, ("dp", "expert"), scatter_dimension=0, tiled=True),
        lax.psum_scatter(grad_kv_local, ("dp", "expert"), scatter_dimension=0, tiled=True),
    )
    query_term = lax.dot_general(
        query_rows, grad_query_low, contract_first, preferred_element_type=jnp.float32
    )
    output_term = lax.dot_general(
        attn_low, grad_result, contract_first, preferred_element_type=jnp.float32
    )
    attn_terms = lax.psum_scatter(
        jnp.stack([query_term, output_term], axis=1)[:, None, :, :].astype(jnp.bfloat16),
        "dp",
        scatter_dimension=0,
        tiled=True,
    ).astype(jnp.float32)
    grad_query_weight = attn_terms[:, :, 0, :]
    grad_output_weight = attn_terms[:, :, 1, :]
    return (
        output,
        grad_input,
        grad_gain_attn,
        grad_gain_mlp,
        grad_kv_weight,
        grad_query_weight,
        grad_output_weight,
        grad_mlp_weight,
    )


def solution(mesh):
    placed = (
        P(("dp", "expert"), None),
        P(("dp", "expert"), None),
        P("dp"),
        P("dp", None),
        P(("dp", "expert"), None),
        P(("dp", "expert"), None),
        P(("dp", "expert"), None),
        P(("dp", "expert")),
        P(("dp", "expert")),
        P(("dp", "expert"), None),
        P("dp", "expert", None),
        P("dp", "expert", None),
        P("dp", "expert", None, None),
    )
    return jax.shard_map(
        local,
        mesh=mesh,
        in_specs=placed,
        out_specs=(
            P(("dp", "expert"), None),
            P(("dp", "expert"), None),
            P(("dp", "expert")),
            P(("dp", "expert")),
            P(("dp", "expert"), None),
            P("dp", "expert", None),
            P("dp", "expert", None),
            P("dp", "expert", None, None),
        ),
        check_vma=False,
    )
```

profile of v0, /device:TPU:0, one launch (start us, length us, event | category | flops | bytes accessed | tf_op | source)
XLA Modules:
  0.0 2700.5 jit_solution(13206879504461205156)
XLA Ops:
  11.2 43.5 %all-reduce.5 = (bf16[2048]{0:T(1024)(128)(2,1)S(1)}, bf16[2048]{0:T(1024)(128)(2,1)}) all-reduce(bf16[2048]{0:T(1024)(128)(2,1)S(1)} %dynamic-update-slice, bf16[2048]{0:T(1024)(128)(2,1)S(1)} %dynamic-update-slice.1), channel_id=1, replica_groups=mesh['dp'=8,'expert'=4] {'dp','expert'}, use_global_device_ids=true, to_apply=%add | all-reduce | flops 4096 | bytes 16384
  84.0 94.4 %all-gather.7.cloned.1.call-done = bf16[2048,4096]{1,0:T(8,128)(2,1)} async-done(((bf16[64,4096]{1,0:T(8,128)(2,1)}), bf16[2048,4096]{1,0:T(8,128)(2,1)}) %all-gather.7.cloned.1.call-update) | async-done | bytes 16777232 | tf_op jit(solution)/shard_map/all_gather | solution.py:157
  266.5 165.4 %all-to-all-done.1 = bf16[4,320,4096]{2,1,0:T(8,128)(2,1)} async-done(((bf16[4,320,4096]{2,1,0:T(8,128)(2,1)}), bf16[4,320,4096]{2,1,0:T(8,128)(2,1)}, u32[]{:S(2)}, u32[]{:S(2)}) %all-to-all-start.1) | async-done | bytes 10485792 | tf_op jit(solution)/shard_map/all_to_all | solution.py:189
  473.6 119.9 %while.30 = (s32[]{:T(128)}, bf16[16,720,128]{2,1,0:T(8,128)(2,1)}, f32[16,720]{1,0:T(8,128)}, bf16[16,720,128]{2,1,0:T(8,128)(2,1)}, bf16[16,1280,128]{2,1,0:T(...) while((s32[]{:T(128)}, bf16[16,720,128]{2,1,0:T(8,128)(2,1)}, ...), condition=%wide.region_16.17_spmd.clone.clone, body=%wide.region_13.16_spmd.clone.sunk.clone | while | flops 484760896 | bytes 12324417 | solution.py:235
  642.3 38.7 %all-to-all-done.2 = bf16[4,180,2048]{2,1,0:T(8,128)(2,1)} async-done(((bf16[4,180,2048]{2,1,0:T(8,128)(2,1)}), bf16[4,180,2048]{2,1,0:T(8,128)(2,1)}, u32[]{:S(2)}, u32[]{:S(2)}) %all-to-all-start.2) | async-done | bytes 2949152 | tf_op jit(solution)/shard_map/all_to_all | solution.py:240
  699.6 12.5 multiply_reduce_fusion.2
  724.5 29.1 %all-to-all-done.5 = bf16[4,180,2048]{2,1,0:T(8,128)(2,1)} async-done(((bf16[4,180,2048]{2,1,0:T(8,128)(2,1)}), bf16[4,180,2048]{2,1,0:T(8,128)(2,1)}, u32[]{:S(2)}, u32[]{:S(2)}) %all-to-all-start.5) | async-done | bytes 2949152 | tf_op jit(solution)/shard_map/all_to_all | solution.py:262
  760.5 64.1 %all-to-all-done.3 = bf16[4,180,2048]{2,1,0:T(8,128)(2,1)S(1)} async-done(((bf16[4,180,2048]{2,1,0:T(8,128)(2,1)}), bf16[4,180,2048]{2,1,0:T(8,128)(2,1)S(1)}, u32[]{:S(2)}, u32[]{:S(2)}) %all-to-all-start.3) | async-done | bytes 2949152 | tf_op jit(solution)/shard_map/all_to_all | solution.py:261
  826.5 24.7 fusion.51
  851.2 23.9 fusion.53
  875.2 33.7 %multiply_convert_fusion.1 = (bf16[720,5632]{1,0:T(8,128)(2,1)}, bf16[720,5632]{1,0:T(8,128)(2,1)}, bf16[720,5632]{1,0:T(8,128)(2,1)}) fusion(f32[720,5632]{1,0:T(8,128)} %fusion.51, f32[720,5632]{1,0:T(8,128)} %fusion.53, bf16[720,2048]{1,0:T(8,128)(2,1)S(1)} %copy-done.19, bf16[5632,1,3,2048]{3,0,2,1:T(8,128)(2,1)} %all-gather.11.cloned.1.call-done), kind=kOutput, calls=%fused_computation.90 | convolution fusion | flops 16670269440 | bytes 82788352 | tf_op jit(solution)/shard_map/dot_general | solution.py:106
  908.8 22.5 fusion.50
  931.4 20.1 add_convert_fusion.1
  957.1 23.3 fusion.76
  983.7 40.8 %all-to-all-done.6 = bf16[4,180,2048]{2,1,0:T(8,128)(2,1)S(1)} async-done(((bf16[4,180,2048]{2,1,0:T(8,128)(2,1)}), bf16[4,180,2048]{2,1,0:T(8,128)(2,1)S(1)}, u32[]{:S(2)}, u32[]{:S(2)}) %all-to-all-start.6) | async-done | bytes 2949152 | tf_op jit(solution)/shard_map/all_to_all | solution.py:283
  1060.4 36.6 %all-to-all-done.4 = bf16[4,180,2048]{2,1,0:T(8,128)(2,1)} async-done(((bf16[4,180,2048]{2,1,0:T(8,128)(2,1)}), bf16[4,180,2048]{2,1,0:T(8,128)(2,1)}, u32[]{:S(2)}, u32[]{:S(2)}) %all-to-all-start.4) | async-done | bytes 2949152 | tf_op jit(solution)/shard_map/all_to_all | solution.py:276
  1110.2 12.4 multiply_reduce_fusion.1
  1149.6 64.0 %all-to-all-done.7 = bf16[4,180,2048]{2,1,0:T(8,128)(2,1)S(1)} async-done(((bf16[4,180,2048]{2,1,0:T(8,128)(2,1)}), bf16[4,180,2048]{2,1,0:T(8,128)(2,1)S(1)}, u32[]{:S(2)}, u32[]{:S(2)}) %all-to-all-start.7) | async-done | bytes 2949152 | tf_op jit(solution)/shard_map/all_to_all | solution.py:299
  1236.6 200.5 %while.31 = (s32[]{:T(128)}, f32[16,720,128]{2,1,0:T(8,128)}, bf16[16,1280,128]{2,1,0:T(8,128)(2,1)}, bf16[16,1280,128]{2,1,0:T(8,128)(2,1)}, bf16[16,720,128]{2...) while((s32[]{:T(128)}, f32[16,720,128]{2,1,0:T(8,128)}, ...), condition=%wide.region_29.30_spmd.clone.clone, body=%wide.region_27.29_spmd.clone.sunk.clone | while | flops 1193727232 | bytes 31087512 | solution.py:336
  1458.7 25.4 convert_bitcast_fusion
  1484.1 26.8 convert_bitcast_fusion.1
  1510.9 25.1 convert_bitcast_fusion.2
  1536.0 46.7 %pad_maximum_fusion = bf16[5632,1,3,2048]{3,0,2,1:T(8,128)(2,1)} fusion(bf16[5632,1,1,2048]{3,0,2,1:T(8,128)(2,1)} %convert_bitcast_fusion, bf16[5632,1,1,2048]{3,0,2,1:T(8,128)(2,1)} %convert_bitcast_fusion.1, bf16[5632,1,1,2048]{3,0,2,1:T(8,128)(2,1)} %convert_bitcast_fusion.2), kind=kLoop, calls=%fused_computation.75 | loop fusion | flops 69206016 | bytes 138412032 | tf_op jit(solution)/shard_map/stack | solution.py:127
  1582.8 16.1 copy.202
  1608.2 16.9 copy.201
  1641.2 231.7 %all_to_all.50 = bf16[4,320,4096]{2,1,0:T(8,128)(2,1)} all-to-all(bf16[4,320,4096]{2,1,0:T(8,128)(2,1)S(1)} %pad_maximum_fusion.2), channel_id=1, replica_groups=mesh['dp'=8,'expert'=4] {'expert'}, dimensions={0} | all-to-all | bytes 20971520 | tf_op jit(solution)/shard_map/all_to_all | solution.py:361
  1890.4 16.4 fusion.100
  1927.2 87.9 %all-to-all-done.9 = bf16[4,180,2048]{2,1,0:T(8,128)(2,1)S(1)} async-done(((bf16[4,180,2048]{2,1,0:T(8,128)(2,1)}), bf16[4,180,2048]{2,1,0:T(8,128)(2,1)S(1)}, u32[]{:S(2)}, u32[]{:S(2)}) %all-to-all-start.9) | async-done | bytes 2949152 | tf_op jit(solution)/shard_map/all_to_all | solution.py:354
  2045.3 12.6 fusion.86
  2057.9 43.2 %all-reduce.4 = (f32[2048]{0:T(1024)S(1)}, f32[2048]{0:T(1024)S(1)}) all-reduce(f32[2048]{0:T(1024)S(1)} %get-tuple-element.395, f32[2048]{0:T(1024)S(1)} %copy-done.49), channel_id=2, replica_groups=mesh['dp'=8,'expert'=4] {'dp','expert'}, use_global_device_ids=true, to_apply=%region_34.35.clone | all-reduce | flops 4096 | bytes 32768
  2116.0 16.0 copy.206
  2132.0 561.2 %reduce-scatter.4.cloned.1.call-done = f32[64,4096]{1,0:T(8,128)} async-done(((f32[2048,4096]{1,0:T(8,128)}), f32[64,4096]{1,0:T(8,128)}) %reduce-scatter.4.cloned.1.call-update) | async-done | bytes 1048592 | tf_op jit(solution)/shard_map/reduce_scatter | solution.py:385
  (582 shorter events, 808.2 us)
Async XLA Ops:
  7.2 171.2 %all-gather.7.cloned.1.call-start = ((), (), s32[]{:S(2)}) async-start(), calls=%async_computation.14 | async-start | bytes 17301504 | tf_op jit(solution)/shard_map/all_gather | solution.py:157
  7.9 231.1 %all-gather.5.cloned.1.call-start = ((), (), s32[]{:S(2)}) async-start(), calls=%async_computation.13 | async-start | bytes 9437184 | tf_op jit(solution)/shard_map/all_gather | solution.py:160
  8.7 584.8 %all-gather.9.cloned.1.call-start = ((), (), s32[]{:S(2)}) async-start(), calls=%async_computation.15 | async-start | bytes 9437184 | tf_op jit(solution)/shard_map/all_gather | solution.py:161
  9.4 817.1 %all-gather.11.cloned.1.call-start = ((), (), s32[]{:S(2)}) async-start(), calls=%async_computation.16 | async-start | bytes 77856768 | tf_op jit(solution)/shard_map/all_gather | solution.py:267
  10.0 54.1 %copy-start.12 = (bf16[320,2048]{1,0:T(8,128)(2,1)S(1)}, bf16[320,2048]{1,0:T(8,128)(2,1)}, u32[]{:S(2)}) copy-start(bf16[320,2048]{1,0:T(8,128)(2,1)} %param.17) | copy-start | bytes 3932164
  64.8 113.5 %copy-start.6 = (bf16[320,2048]{1,0:T(8,128)(2,1)}, bf16[320,2048]{1,0:T(8,128)(2,1)S(1)}, u32[]{:S(2)}) copy-start(bf16[320,2048]{1,0:T(8,128)(2,1)S(1)} %fusion.81) | copy-start | bytes 3932164
  77.1 114.3 %all-to-all-start = ((bf16[4,180,2048]{2,1,0:T(8,128)(2,1)}), bf16[4,180,2048]{2,1,0:T(8,128)(2,1)}, u32[]{:S(2)}, u32[]{:S(2)}) async-start(bf16[4,180,2048]{2,1,0:T(8,128)(2,1)} %broadcast_multiply_fusion.1), calls=%async_computation | async-start | bytes 6029312 | tf_op jit(solution)/shard_map/all_to_all | solution.py:188
  84.0 104.5 %copy-start.32 = (f32[320,64]{1,0:T(8,128)}, f32[320,64]{1,0:T(8,128)S(1)}, u32[]{:S(2)}) copy-start(f32[320,64]{1,0:T(8,128)S(1)} %get-tuple-element.491) | copy-start | bytes 245764
  196.8 235.1 %all-to-all-start.1 = ((bf16[4,320,4096]{2,1,0:T(8,128)(2,1)}), bf16[4,320,4096]{2,1,0:T(8,128)(2,1)}, u32[]{:S(2)}, u32[]{:S(2)}) async-start(bf16[4,320,4096]{2,1,0:T(8,128)(2,1)} %broadcast_in_dim.28), calls=%async_computation.1 | async-start | bytes 20971520 | tf_op jit(solution)/shard_map/all_to_all | solution.py:189
  235.5 25.5 copy-start.17
  608.2 72.8 %all-to-all-start.2 = ((bf16[4,180,2048]{2,1,0:T(8,128)(2,1)}), bf16[4,180,2048]{2,1,0:T(8,128)(2,1)}, u32[]{:S(2)}, u32[]{:S(2)}) async-start(bf16[4,180,2048]{2,1,0:T(8,128)(2,1)} %reshape.924), calls=%async_computation.2 | async-start | bytes 6029312 | tf_op jit(solution)/shard_map/all_to_all | solution.py:240
  642.3 43.7 %copy-start.44 = (s32[640]{0:T(1024)S(1)}, s32[640]{0:T(1024)}, u32[]{:S(2)}) copy-start(s32[640]{0:T(1024)} %copy-done.43) | copy-start | bytes 7684
  642.3 44.1 %copy-start.65 = (f32[320,2]{0,1:T(2,128)S(1)}, f32[320,2]{0,1:T(2,128)}, u32[]{:S(2)}) copy-start(f32[320,2]{0,1:T(2,128)} %param.21) | copy-start | bytes 7684
  642.3 44.3 %copy-start.57 = (bf16[2048]{0:T(1024)(128)(2,1)S(1)}, bf16[2048]{0:T(1024)(128)(2,1)}, u32[]{:S(2)}) copy-start(bf16[2048]{0:T(1024)(128)(2,1)} %get-tuple-element.458) | copy-start | bytes 12292
  681.0 72.5 %all-to-all-start.5 = ((bf16[4,180,2048]{2,1,0:T(8,128)(2,1)}), bf16[4,180,2048]{2,1,0:T(8,128)(2,1)}, u32[]{:S(2)}, u32[]{:S(2)}) async-start(bf16[4,180,2048]{2,1,0:T(8,128)(2,1)} %multiply_convert_fusion.5), calls=%async_computation.5 | async-start | bytes 6029312 | tf_op jit(solution)/shard_map/all_to_all | solution.py:262
  686.6 27.8 %copy-start.37 = (f32[2048]{0:T(1024)}, f32[2048]{0:T(1024)S(1)}, u32[]{:S(2)}) copy-start(f32[2048]{0:T(1024)S(1)} %convert_element_type.234) | copy-start | bytes 24580
  753.5 71.1 %all-to-all-start.3 = ((bf16[4,180,2048]{2,1,0:T(8,128)(2,1)}), bf16[4,180,2048]{2,1,0:T(8,128)(2,1)S(1)}, u32[]{:S(2)}, u32[]{:S(2)}) async-start(bf16[4,180,2048]{2,1,0:T(8,128)(2,1)} %broadcast_multiply_fusion), calls=%async_computation.3 | async-start | bytes 6029312 | tf_op jit(solution)/shard_map/all_to_all | solution.py:261
  953.4 71.1 %all-to-all-start.6 = ((bf16[4,180,2048]{2,1,0:T(8,128)(2,1)}), bf16[4,180,2048]{2,1,0:T(8,128)(2,1)S(1)}, u32[]{:S(2)}, u32[]{:S(2)}) async-start(bf16[4,180,2048]{2,1,0:T(8,128)(2,1)} %reshape.932), calls=%async_computation.6 | async-start | bytes 6029312 | tf_op jit(solution)/shard_map/all_to_all | solution.py:283
  983.7 45.8 %copy-start.46 = (s32[640]{0:T(1024)S(1)}, s32[640]{0:T(1024)}, u32[]{:S(2)}) copy-start(s32[640]{0:T(1024)} %copy-done.45) | copy-start | bytes 7684
  983.7 46.0 %copy-start.31 = (f32[320,2]{1,0:T(8,128)S(1)}, f32[320,2]{1,0:T(8,128)}, u32[]{:S(2)}) copy-start(f32[320,2]{1,0:T(8,128)} %copy-done.30) | copy-start | bytes 7684
  983.7 46.2 %copy-start.55 = (s32[320,2]{0,1:T(2,128)S(1)}, s32[320,2]{0,1:T(2,128)}, u32[]{:S(2)}) copy-start(s32[320,2]{0,1:T(2,128)} %param.22) | copy-start | bytes 7684
  983.7 46.5 %copy-start.36 = (s32[4,180,1]{0,1,2:T(8,128)S(1)}, s32[4,180,1]{0,1,2:T(8,128)}, u32[]{:S(2)}) copy-start(s32[4,180,1]{0,1,2:T(8,128)} %get-tuple-element.482) | copy-start | bytes 8644
  1024.5 72.5 %all-to-all-start.4 = ((bf16[4,180,2048]{2,1,0:T(8,128)(2,1)}), bf16[4,180,2048]{2,1,0:T(8,128)(2,1)}, u32[]{:S(2)}, u32[]{:S(2)}) async-start(bf16[4,180,2048]{2,1,0:T(8,128)(2,1)} %reshape.928), calls=%async_computation.4 | async-start | bytes 6029312 | tf_op jit(solution)/shard_map/all_to_all | solution.py:276
  1142.6 71.1 %all-to-all-start.7 = ((bf16[4,180,2048]{2,1,0:T(8,128)(2,1)}), bf16[4,180,2048]{2,1,0:T(8,128)(2,1)S(1)}, u32[]{:S(2)}, u32[]{:S(2)}) async-start(bf16[4,180,2048]{2,1,0:T(8,128)(2,1)} %multiply_convert_fusion.4), calls=%async_computation.7 | async-start | bytes 6029312 | tf_op jit(solution)/shard_map/all_to_all | solution.py:299
  1146.3 960.4 %reduce-scatter.6.cloned.1.call-start = ((), (), s32[]{:S(2)}) async-start(), calls=%async_computation.18 | async-start | bytes 18874368 | tf_op jit(solution)/shard_map/reduce_scatter | solution.py:393
  1236.6 200.5 %copy-start.18 = (f32[720,64]{1,0:T(8,128)S(1)}, f32[720,64]{1,0:T(8,128)}, u32[]{:S(2)}) copy-start(f32[720,64]{1,0:T(8,128)} %copy-done.17) | copy-start | bytes 552964
  1456.9 659.1 %reduce-scatter.8.cloned.1.call-start = ((), (), s32[]{:S(2)}) async-start(), calls=%async_computation.19 | async-start | bytes 77856768 | tf_op jit(solution)/shard_map/reduce_scatter | solution.py:269
  1484.1 26.8 copy-start.22
  1582.7 1110.5 %reduce-scatter.4.cloned.1.call-start = ((), (), s32[]{:S(2)}) async-start(), calls=%async_computation.17 | async-start | bytes 34603008 | tf_op jit(solution)/shard_map/reduce_scatter | solution.py:385
  1923.5 91.6 %all-to-all-start.9 = ((bf16[4,180,2048]{2,1,0:T(8,128)(2,1)}), bf16[4,180,2048]{2,1,0:T(8,128)(2,1)S(1)}, u32[]{:S(2)}, u32[]{:S(2)}) async-start(bf16[4,180,2048]{2,1,0:T(8,128)(2,1)} %convert_element_type.258), calls=%async_computation.9 | async-start | bytes 6029312 | tf_op jit(solution)/shard_map/all_to_all | solution.py:354
  1927.2 90.6 %copy-start.11 = (s32[1024]{0:T(1024)S(1)}, s32[1024]{0:T(1024)}, u32[]{:S(2)}) copy-start(s32[1024]{0:T(1024)} %copy-done.10) | copy-start | bytes 12292
  2045.3 56.9 %copy-start.5 = (f32[320,2048]{1,0:T(8,128)S(1)}, f32[320,2048]{1,0:T(8,128)}, u32[]{:S(2)}) copy-start(f32[320,2048]{1,0:T(8,128)} %copy-done.4) | copy-start | bytes 7864324
  (57 other events, 384.2 us)
Sparse Core Ops, SparseCore 0:
  11.0 167.3 all-gather.6
  180.2 53.4 all-gather.4
  235.6 54.2 all-gather.8
  291.7 311.6 all-gather.10
  1457.1 115.4 reduce-scatter.5
  1582.9 393.5 reduce-scatter.7
  1979.3 713.8 reduce-scatter.3
where the time goes:
time: 2720 us; the launch traced here: 2700 us
  waiting for transfers between devices  1180 us (43%)
  matrix products  591 us (22%)
  local copies, waits for them, and re-layouts  333 us (12%)
  blocking collectives  318 us (12%)
  other arithmetic  214 us (8%)
  starting transfers between devices  41.5 us (2%)
    reduce_scatter x1, waiting for transfers between devices, local(): lax.psum_scatter(grad_kv_local, ('dp', 'expert'), scatter_dimension=0, ti...  561 us
    all_to_all x1, blocking collectives, local(): lax.all_to_all(grad_kv_term.astype(jnp.bfloat16), 'expert', split_axis=0,...  232 us
    all_to_all x1, waiting for transfers between devices, local(): lax.all_to_all(kv_copies, 'expert', split_axis=0, concat_axis=0, tiled=True)  165 us
    all_gather x1, waiting for transfers between devices, local(): lax.all_gather(kv_weight, ('dp', 'expert'), axis=0, tiled=True)  94.4 us
    all_to_all x1, waiting for transfers between devices, local(): lax.all_to_all(grad_rows.reshape(experts, capacity, width).astype(jnp.bfl...  87.9 us
    unnamed x2, blocking collectives  86.6 us
    all_to_all x1, waiting for transfers between devices, local(): lax.all_to_all(send_in, 'expert', split_axis=0, concat_axis=0, tiled=True)  64.1 us
    all_to_all x1, waiting for transfers between devices, local(): lax.all_to_all(send_cot, 'expert', split_axis=0, concat_axis=0, tiled=True)  64 us
  transfers between devices with their start and end apart: 16, of which 10 were waited for; matrix products, arithmetic and copies ran while one was open for 26% of the time, Pallas kernels for 0%

commit v1 on v0

v1 whole, which is shorter than its diff:
```python
import functools
import math

import jax
import jax.numpy as jnp
from jax import lax
from jax.experimental import pallas as pl
from jax.experimental.pallas import tpu as pltpu
from jax.sharding import PartitionSpec as P


HEAD = 128
PROMPT = 1024
CONTS = 2
GROUP_TOK = 1280
MLP_FIRST = 0.4

norm_eps = 1e-06
rope_base = 10000.0
neg_fill = -1e30
log2e = 1.4426950408889634
MESH = pl.DeviceIdType.MESH
contract_last = (((1,), (1,)), ((), ()))
contract_first = (((0,), (0,)), ((), ()))
f32 = jnp.float32
bf16 = jnp.bfloat16


def rope_tables(positions):
    half_size = HEAD // 2
    freq_steps = jnp.arange(half_size, dtype=f32)
    inverse_freq = jnp.exp(-math.log(rope_base) * 2.0 * freq_steps / HEAD)
    angles = positions.astype(f32)[:, None] * inverse_freq[None, :]
    cosine, sine = jnp.cos(angles), jnp.sin(angles)
    return (
        jnp.concatenate([cosine, cosine], axis=1),
        jnp.concatenate([-sine, sine], axis=1),
    )


def token_positions(cont_ids):
    row_count = cont_ids.shape[0]
    group_count = row_count // GROUP_TOK
    places = jnp.arange(row_count, dtype=jnp.int32) % GROUP_TOK
    labels = jnp.arange(CONTS + 1, dtype=jnp.int32)
    one_hot = (cont_ids[:, None] == labels[None, :]).astype(jnp.int32)
    counts = jnp.sum(one_hot.reshape(group_count, GROUP_TOK, CONTS + 1), axis=1)
    starts = jnp.cumsum(counts, axis=1) - counts
    starts_tok = jnp.broadcast_to(starts[:, None, :], (group_count, GROUP_TOK, CONTS + 1)).reshape(
        row_count, CONTS + 1
    )
    start_of = jnp.sum(starts_tok * one_hot, axis=1)
    return (places, places - start_of + PROMPT * (cont_ids > 0).astype(jnp.int32))


def rms_parts(values):
    row_scale = lax.rsqrt(jnp.mean(values * values, axis=-1, keepdims=True) + norm_eps)
    return (values * row_scale, row_scale)


def rms_back(grad_out, normed, row_scale, gain_vec):
    through = grad_out * gain_vec
    grad_in = row_scale * (through - normed * jnp.mean(through * normed, axis=-1, keepdims=True))
    return grad_in


def dot_nt(left, right):
    return lax.dot_general(left, right, contract_last, preferred_element_type=f32)


def dot_tn(left, right):
    return lax.dot_general(left, right, contract_first, preferred_element_type=f32)


def dot_nn(left, right):
    return jnp.dot(left, right, preferred_element_type=f32)


def before_counts(flags):
    count = flags.shape[-1]
    steps = jnp.arange(count, dtype=jnp.int32)
    earlier = (steps[:, None] < steps[None, :]).astype(bf16)
    return jnp.dot(flags.astype(bf16), earlier, preferred_element_type=f32).astype(jnp.int32)


def project_kernel(rope_blocks, tile, x_ref, w_ref, cos_ref, sin_ref, out_ref):
    rows = x_ref.shape[0]
    turn = pl.program_id(0) < rope_blocks
    for start in range(0, rows, tile):
        span = pl.ds(start, tile)
        product = jnp.dot(x_ref[span, :], w_ref[...], preferred_element_type=f32)

        @pl.when(turn)
        def _():
            cosine, sine = cos_ref[span, :], sin_ref[span, :]
            for col in range(0, product.shape[1], HEAD):
                piece = product[:, col : col + HEAD]
                turned = piece * cosine + pltpu.roll(piece, HEAD // 2, 1) * sine
                out_ref[span, col : col + HEAD] = turned.astype(bf16)

        @pl.when(jnp.logical_not(turn))
        def _():
            out_ref[span, :] = product.astype(bf16)


def project(rows, weight, cosine, sine, rope_cols, tile):
    count, width = rows.shape
    cols = weight.shape[1]
    block = 512
    return pl.pallas_call(
        functools.partial(project_kernel, rope_cols // block, tile),
        grid=(cols // block,),
        in_specs=[
            pl.BlockSpec((count, width), lambda i: (0, 0)),
            pl.BlockSpec((width, block), lambda i: (0, i)),
            pl.BlockSpec((count, HEAD), lambda i: (0, 0)),
            pl.BlockSpec((count, HEAD), lambda i: (0, 0)),
        ],
        out_specs=pl.BlockSpec((count, block), lambda i: (0, i)),
        out_shape=jax.ShapeDtypeStruct((count, cols), bf16),
        cost_estimate=pl.CostEstimate(
            flops=2 * count * width * cols,
            bytes_accessed=2 * (count * width + width * cols + count * cols),
            transcendentals=0,
        ),
    )(rows, weight, cosine, sine)


def key_spans(blocks, tokens, keys):
    return [min(-(-(tokens * (s + 1)) // 128) * 128, keys) for s in range(blocks)]


def fill_bias(bias, place_ref, cont_ref, kcont_ref):
    blocks, slots, keys = bias.shape
    kplace = lax.broadcasted_iota(jnp.int32, (slots, keys), 1)
    kcont = kcont_ref[...]
    for s in range(blocks):
        allowed = (kplace <= place_ref[s]) & ((kcont == 0) | (kcont == cont_ref[s]))
        bias[s] = jnp.where(allowed, 0.0, neg_fill)


def attend_kernel(spans, q_ref, k_ref, v_ref, place_ref, cont_ref, kcont_ref, out_ref, lse_ref, bias):
    @pl.when(pl.program_id(0) == 0)
    def _():
        fill_bias(bias, place_ref, cont_ref, kcont_ref)

    scale2 = log2e / math.sqrt(HEAD)
    for s, span in enumerate(spans):
        scores = dot_nt(q_ref[s], k_ref[:span, :]) * scale2 + bias[s, :, :span]
        peak = jnp.max(scores, axis=1, keepdims=True)
        weights = jnp.exp2(scores - peak)
        total = jnp.sum(weights, axis=1, keepdims=True)
        mixed = dot_nn(weights.astype(bf16), v_ref[:span, :])
        out_ref[s] = (mixed / total).astype(bf16)
        lse_ref[s] = jnp.broadcast_to(peak + jnp.log2(total), lse_ref.shape[1:])


def attend(query, kv_low, place, cont, kcont, tokens):
    blocks, slots, features = query.shape
    keys = kv_low.shape[0]
    heads = features // HEAD
    spans = key_spans(blocks, tokens, keys)
    work = 2 * 2 * slots * sum(spans) * HEAD * heads
    qspec = pl.BlockSpec((blocks, slots, HEAD), lambda h: (0, 0, h))
    whole = pl.BlockSpec((blocks, slots, 1), lambda h: (0, 0, 0))
    return pl.pallas_call(
        functools.partial(attend_kernel, spans),
        grid=(heads,),
        in_specs=[
            qspec,
            pl.BlockSpec((keys, HEAD), lambda h: (0, h)),
            pl.BlockSpec((keys, HEAD), lambda h: (0, heads + h)),
            whole,
            whole,
            pl.BlockSpec((1, keys), lambda h: (0, 0)),
        ],
        out_specs=[qspec, qspec],
        out_shape=[
            jax.ShapeDtypeStruct(query.shape, bf16),
            jax.ShapeDtypeStruct(query.shape, f32),
        ],
        scratch_shapes=[pltpu.VMEM((blocks, slots, keys), f32)],
        cost_estimate=pl.CostEstimate(
            flops=work,
            bytes_accessed=4 * query.size + 2 * kv_low.size + 4 * query.size,
            transcendentals=slots * sum(spans) * heads,
        ),
        name="attend",
    )(query, kv_low, kv_low, place, cont, kcont)


def attend_back_kernel(
    spans,
    q_ref,
    k_ref,
    v_ref,
    g_ref,
    lse_ref,
    place_ref,
    cont_ref,
    kcont_ref,
    qcos_ref,
    qsin_ref,
    kcos_ref,
    ksin_ref,
    dq_ref,
    dk_ref,
    dv_ref,
    bias,
    dk_sum,
    dv_sum,
):
    @pl.when(pl.program_id(0) == 0)
    def _():
        fill_bias(bias, place_ref, cont_ref, kcont_ref)

    scale = 1.0 / math.sqrt(HEAD)
    scale2 = log2e * scale
    last = len(spans) - 1
    for s in range(last, -1, -1):
        span = spans[s]
        query, grad = q_ref[s], g_ref[s]
        keys = k_ref[:span, :]
        scores = dot_nt(query, keys) * scale2 + bias[s, :, :span]
        prob = jnp.exp2(scores - lse_ref[s][:, :1])
        grad_prob = dot_nt(grad, v_ref[:span, :])
        inner = jnp.sum(prob * grad_prob, axis=1, keepdims=True)
        grad_scores = (prob * (grad_prob - inner)).astype(bf16)
        dq = dot_nn(grad_scores, keys) * scale
        dq = dq * qcos_ref[s] - pltpu.roll(dq, HEAD // 2, 1) * qsin_ref[s]
        dq_ref[s] = dq.astype(bf16)
        dk = dot_tn(grad_scores, query)
        dv = dot_tn(prob.astype(bf16), grad)
        if s == last:
            dk_sum[...] = dk
            dv_sum[...] = dv
        else:
            dk_sum[:span, :] += dk
            dv_sum[:span, :] += dv
    dk = dk_sum[...] * scale
    dk_ref[...] = (dk * kcos_ref[...] - pltpu.roll(dk, HEAD // 2, 1) * ksin_ref[...]).astype(bf16)
    dv_ref[...] = dv_sum[...].astype(bf16)


def attend_back(query, kv_low, grad, lse, place, cont, kcont, qcos, qsin, kcos, ksin, tokens):
    blocks, slots, features = query.shape
    keys = kv_low.shape[0]
    heads = features // HEAD
    spans = key_spans(blocks, tokens, keys)
    work = 5 * 2 * slots * sum(spans) * HEAD * heads
    qspec = pl.BlockSpec((blocks, slots, HEAD), lambda h: (0, 0, h))
    kspec = pl.BlockSpec((keys, HEAD), lambda h: (0, h))
    whole = pl.BlockSpec((blocks, slots, 1), lambda h: (0, 0, 0))
    qtab = pl.BlockSpec((blocks, slots, HEAD), lambda h: (0, 0, 0))
    ktab = pl.BlockSpec((keys, HEAD), lambda h: (0, 0))
    return pl.pallas_call(
        functools.partial(attend_back_kernel, spans),
        grid=(heads,),
        in_specs=[
            qspec,
            kspec,
            pl.BlockSpec((keys, HEAD), lambda h: (0, heads + h)),
            qspec,
            qspec,
            whole,
            whole,
            pl.BlockSpec((1, keys), lambda h: (0, 0)),
            qtab,
            qtab,
            ktab,
            ktab,
        ],
        out_specs=[qspec, kspec, kspec],
        out_shape=[
            jax.ShapeDtypeStruct(query.shape, bf16),
            jax.ShapeDtypeStruct((keys, features), bf16),
            jax.ShapeDtypeStruct((keys, features), bf16),
        ],
        scratch_shapes=[
            pltpu.VMEM((blocks, slots, keys), f32),
            pltpu.VMEM((keys, HEAD), f32),
            pltpu.VMEM((keys, HEAD), f32),
        ],
        cost_estimate=pl.CostEstimate(
            flops=work,
            bytes_accessed=10 * query.size + 4 * kv_low.size,
            transcendentals=slots * sum(spans) * heads,
        ),
        name="attend_back",
    )(query, kv_low, kv_low, grad, lse, place, cont, kcont, qcos, qsin, kcos, ksin)


def unit_kernel(
    x_hbm,
    g_hbm,
    gate_ref,
    up_ref,
    down_ref,
    in_ref,
    out_hbm,
    gg_hbm,
    gu_hbm,
    hid_hbm,
    xbuf,
    gbuf,
    obuf,
    kbuf,
    psend,
    precv,
    ssend,
    frecv,
    load_sem,
    store_sem,
    psend_sem,
    precv_sem,
    ssend_sem,
    frecv_sem,
):
    rows = xbuf.shape[1]
    chips = ssend.shape[0]
    me = lax.axis_index("dp")
    chip = me // 2
    core = me % 2
    partner = me + 1 - 2 * core

    def peer(hop):
        return {"dp": (chip + hop) % chips * 2 + core}

    barrier = pltpu.get_barrier_semaphore()
    pl.semaphore_signal(barrier, inc=1, device_id={"dp": partner}, device_id_type=MESH)
    for hop in range(1, chips):
        pl.semaphore_signal(barrier, inc=1, device_id=peer(hop), device_id_type=MESH)
    pl.semaphore_wait(barrier, chips)

    def block_rows(j, own):
        dest = (chip + chips - 1 - j) % chips
        block = dest * 2 + (core if own else 1 - core)
        return pl.ds(pl.multiple_of(block * rows, 8), rows)

    def loads(j, own):
        span, slot = block_rows(j, own), int(own)
        return [
            pltpu.make_async_copy(x_hbm.at[span], xbuf.at[slot], load_sem.at[0, slot]),
            pltpu.make_async_copy(g_hbm.at[span], gbuf.at[slot], load_sem.at[1, slot]),
        ]

    def stores(j, own):
        span, slot = block_rows(j, own), int(own)
        return [pltpu.make_async_copy(obuf.at[slot], out_hbm.at[span], store_sem.at[0, slot])] + [
            pltpu.make_async_copy(kbuf.at[slot, i], dst.at[span], store_sem.at[1 + i, slot])
            for i, dst in enumerate((gg_hbm, gu_hbm, hid_hbm))
        ]

    def to_partner(j):
        return pltpu.make_async_remote_copy(
            src_ref=psend.at[j % 2],
            dst_ref=precv.at[j],
            send_sem=psend_sem.at[j % 2],
            recv_sem=precv_sem.at[j],
            device_id={"dp": partner},
            device_id_type=MESH,
        )

    def to_owner(j):
        return pltpu.make_async_remote_copy(
            src_ref=ssend.at[j],
            dst_ref=frecv.at[j],
            send_sem=ssend_sem.at[j],
            recv_sem=frecv_sem.at[j],
            device_id=peer(chips - 1 - j),
            device_id_type=MESH,
        )

    def compute(j, own):
        slot = int(own)
        for copy in loads(j, own):
            copy.wait()
        rows_in, rows_grad = xbuf[slot], gbuf[slot]
        gate_val = dot_nt(rows_in, gate_ref[...])
        up_val = dot_nt(rows_in, up_ref[...])
        grad_hidden = dot_nt(rows_grad, down_ref[...])
        sigma = jax.nn.sigmoid(gate_val)
        active = gate_val * sigma
        hidden = (active * up_val).astype(bf16)
        grad_gate = (grad_hidden * up_val * sigma * (1.0 + gate_val * (1.0 - sigma))).astype(bf16)
        grad_up = (grad_hidden * active).astype(bf16)

        @pl.when(j > 0)
        def _():
            for copy in stores(j - 1, own):
                copy.wait()

        kbuf[slot, 0] = grad_gate
        kbuf[slot, 1] = grad_up
        kbuf[slot, 2] = hidden
        obuf[slot] = dot_nn(hidden, down_ref[...]).astype(bf16)
        for copy in stores(j, own):
            copy.start()
        return dot_nn(grad_gate, gate_ref[...]) + dot_nn(grad_up, up_ref[...])

    for copy in loads(0, False):
        copy.start()

    def step(j, carry):
        for copy in loads(j, True):
            copy.start()
        term = compute(j, False)

        @pl.when(j > 1)
        def _():
            to_partner(j - 2).wait_send()

        psend[j % 2] = term.astype(bf16)
        to_partner(j).start()

        @pl.when(j < chips - 1)
        def _():
            for copy in loads(j + 1, False):
                copy.start()

        term = compute(j, True)
        to_partner(j).wait_recv()
        ssend[j] = (term + precv[j].astype(f32)).astype(bf16)

        @pl.when(j < chips - 1)
        def _():
            to_owner(j).start()

        return carry

    lax.fori_loop(0, chips, step, 0)
    total = ssend[chips - 1].astype(f32)
    for j in range(chips - 1):
        to_owner(j).wait_recv()
        total = total + frecv[j].astype(f32)
    in_ref[...] = total.astype(bf16)
    for j in range(chips - 1):
        to_owner(j).wait_send()
    for j in range(max(chips - 2, 0), chips):
        to_partner(j).wait_send()
    for own in (False, True):
        for copy in stores(chips - 1, own):
            copy.wait()


def unit_block(rows_in, rows_grad, gate_rows, up_rows, down_rows, owners, number):
    total, width = rows_in.shape
    units = gate_rows.shape[0]
    rows = total // owners
    chips = owners // 2
    hbm = pl.BlockSpec(memory_space=pl.ANY)
    vmem = pl.BlockSpec(memory_space=pltpu.VMEM)
    kept = jax.ShapeDtypeStruct((total, units), bf16)
    return pl.pallas_call(
        unit_kernel,
        in_specs=[hbm, hbm, vmem, vmem, vmem],
        out_specs=[vmem, hbm, hbm, hbm, hbm],
        out_shape=[
            jax.ShapeDtypeStruct((rows, width), bf16),
            jax.ShapeDtypeStruct((total, width), bf16),
            kept,
            kept,
            kept,
        ],
        scratch_shapes=[
            pltpu.VMEM((2, rows, width), bf16),
            pltpu.VMEM((2, rows, width), bf16),
            pltpu.VMEM((2, rows, width), bf16),
            pltpu.VMEM((2, 3, rows, units), bf16),
            pltpu.VMEM((2, rows, width), bf16),
            pltpu.VMEM((chips, rows, width), bf16),
            pltpu.VMEM((chips, rows, width), bf16),
            pltpu.VMEM((chips - 1, rows, width), bf16),
            pltpu.SemaphoreType.DMA((2, 2)),
            pltpu.SemaphoreType.DMA((4, 2)),
            pltpu.SemaphoreType.DMA((2,)),
            pltpu.SemaphoreType.DMA((chips,)),
            pltpu.SemaphoreType.DMA((chips,)),
            pltpu.SemaphoreType.DMA((chips,)),
        ],
        compiler_params=pltpu.CompilerParams(
            collective_id=number, has_side_effects=True, vmem_limit_bytes=67043328
        ),
        cost_estimate=pl.CostEstimate(
            flops=6 * 2 * total * units * width,
            bytes_accessed=2 * (3 * total * width + 3 * total * units + 3 * units * width),
            transcendentals=total * units,
        ),
        name="unit_block",
    )(rows_in, rows_grad, gate_rows, up_rows, down_rows)


def line_kernel(own_ref, *refs):
    all_ref, bounce, up_send, up_recv, down_send, down_recv, local_sem = refs[-7:]
    me = lax.axis_index("expert")
    count = all_ref.shape[0]
    below = jnp.maximum(me - 1, 0)
    above = jnp.minimum(me + 1, count - 1)
    barrier = pltpu.get_barrier_semaphore()

    @pl.when(me > 0)
    def _():
        pl.semaphore_signal(barrier, inc=1, device_id={"expert": below}, device_id_type=MESH)

    @pl.when(me < count - 1)
    def _():
        pl.semaphore_signal(barrier, inc=1, device_id={"expert": above}, device_id_type=MESH)

    inner = (me > 0) & (me < count - 1)

    @pl.when(inner)
    def _():
        pl.semaphore_wait(barrier, 2)

    @pl.when(jnp.logical_not(inner))
    def _():
        pl.semaphore_wait(barrier, 1)

    def upward(step, block):
        return pltpu.make_async_remote_copy(
            src_ref=own_ref if step == 0 else all_ref.at[block],
            dst_ref=all_ref.at[block],
            send_sem=up_send.at[step],
            recv_sem=up_recv.at[step],
            device_id={"expert": above},
            device_id_type=MESH,
        )

    def downward(step, block):
        return pltpu.make_async_remote_copy(
            src_ref=own_ref if step == 0 else all_ref.at[block],
            dst_ref=all_ref.at[block],
            send_sem=down_send.at[step],
            recv_sem=down_recv.at[step],
            device_id={"expert": below},
            device_id_type=MESH,
        )

    steps = range(count - 1)
    for step in steps:
        if step > 0:

            @pl.when(me - step >= 0)
            def _():
                upward(step - 1, jnp.maximum(me - step, 0)).wait_recv()

            @pl.when(me + step < count)
            def _():
                downward(step - 1, jnp.minimum(me + step, count - 1)).wait_recv()

        @pl.when((me - step >= 0) & (me < count - 1))
        def _():
            upward(step, jnp.maximum(me - step, 0)).start()

        @pl.when((me + step < count) & (me > 0))
        def _():
            downward(step, jnp.minimum(me + step, count - 1)).start()

        if step == 0:
            copy = pltpu.make_async_copy(own_ref, bounce, local_sem.at[0])
            copy.start()
            copy.wait()
            copy = pltpu.make_async_copy(bounce, all_ref.at[me], local_sem.at[1])
            copy.start()
            copy.wait()

    @pl.when(me == count - 1)
    def _():
        upward(count - 2, 0).wait_recv()

    @pl.when(me == 0)
    def _():
        downward(count - 2, count - 1).wait_recv()

    for step in steps:

        @pl.when((me - step >= 0) & (me < count - 1))
        def _():
            upward(step, jnp.maximum(me - step, 0)).wait_send()

        @pl.when((me + step < count) & (me > 0))
        def _():
            downward(step, jnp.minimum(me + step, count - 1)).wait_send()


def line_gather(own, experts, number, *waits):
    hbm = pl.BlockSpec(memory_space=pl.ANY)
    steps = (max(experts - 1, 1),)
    return pl.pallas_call(
        line_kernel,
        in_specs=[hbm] * (1 + len(waits)),
        out_specs=hbm,
        out_shape=jax.ShapeDtypeStruct((experts,) + own.shape, own.dtype),
        scratch_shapes=[pltpu.VMEM(own.shape, own.dtype)]
        + [pltpu.SemaphoreType.DMA(steps)] * 4
        + [pltpu.SemaphoreType.DMA((2,))],
        compiler_params=pltpu.CompilerParams(collective_id=number, has_side_effects=True),
        cost_estimate=pl.CostEstimate(
            flops=0, bytes_accessed=4 * experts * own.size, transcendentals=0
        ),
        name="line_gather",
    )(own, *waits)


def hold(value, *others):
    for other in others:
        last = other[(slice(-1, None),) * other.ndim].reshape(())
        value = value + jnp.minimum(jnp.abs(last), 0).astype(value.dtype)
    return value


def exchange(rows):
    return lax.all_to_all(rows, "expert", split_axis=0, concat_axis=0, tiled=True)


def hop_sum(parts, place, count):
    total = lax.dynamic_index_in_dim(parts, place, 0, keepdims=False).astype(f32)
    got = []
    for hop in range(1, count):
        ring = [(i, (i + hop) % count) for i in range(count)]
        piece = lax.dynamic_index_in_dim(parts, (place + hop) % count, 0, keepdims=False)
        got.append(lax.ppermute(piece, "expert", ring))
    for piece in got:
        total = total + piece.astype(f32)
    return total


def after(value, *others):
    return lax.optimization_barrier((value,) + others)[0]


def plane_sum(terms):
    return lax.psum_scatter(terms, "dp", scatter_dimension=0, tiled=True)


def hops(rows, sign):
    count = rows.shape[0]
    pieces = [rows[0]]
    for hop in range(1, count):
        ring = [(i, (i + sign * hop) % count) for i in range(count)]
        pieces.append(lax.ppermute(rows[hop], "expert", ring))
    return jnp.stack(pieces)


def spread(rows, axes, count):
    copies = jnp.broadcast_to(rows[None], (count,) + rows.shape)
    return lax.all_to_all(copies, axes, split_axis=0, concat_axis=0, tiled=True)


def layer(
    layer_input,
    cotangent,
    cont_ids,
    attn_routes,
    attn_gates,
    mlp_routes,
    mlp_gates,
    gain_attn,
    gain_mlp,
    kv_weight,
    query_weight,
    output_weight,
    mlp_weight,
):
    experts = lax.axis_size("expert")
    owners = lax.axis_size("dp")
    expert_id = lax.axis_index("expert")
    tok_dev, width = layer_input.shape
    per_token = attn_routes.shape[1]
    capacity = tok_dev * per_token * 9 // (8 * experts)
    slots = -(-capacity // 8) * 8
    slot_total = experts * slots
    group = cont_ids.shape[0]
    features = query_weight.shape[2]
    expert_ids = jnp.arange(experts, dtype=jnp.int32)
    slot_ids = jnp.arange(slots, dtype=jnp.int32)

    kv_part = line_gather(kv_weight, experts, 6).reshape(-1, kv_weight.shape[1])
    kv_full = lax.all_gather(kv_part, "dp", axis=0, tiled=True)
    x_all = line_gather(layer_input, experts, 7, kv_part).reshape(group, width)
    query_full = lax.all_gather(query_weight[:, 0, :], "dp", axis=0, tiled=True)
    output_full = lax.all_gather(output_weight[:, 0, :], "dp", axis=0, tiled=True)
    gains = jnp.concatenate([gain_attn, gain_mlp])[None]
    gains = spread(gains, ("dp", "expert"), owners * experts)
    part_size = gain_attn.shape[0]
    gains = gains.reshape(owners * experts, 2, part_size)
    gain_one = gains[:, 0].reshape(-1).astype(f32)
    gain_two = gains[:, 1].reshape(-1).astype(f32)

    hop_ids = (expert_id + expert_ids) % experts
    mlp_hot = mlp_routes.T[:, None, :] == hop_ids[None, :, None]
    mlp_mine = jnp.any(mlp_hot, axis=0)
    mlp_rank = before_counts(mlp_mine)
    mlp_pick = mlp_mine[:, None, :] & (mlp_rank[:, None, :] == slot_ids[None, :, None])
    mlp_gate_tok = jnp.sum(jnp.where(mlp_hot, mlp_gates.T[:, None, :], 0.0), axis=0)
    mlp_slot_gate = jnp.sum(jnp.where(mlp_pick, mlp_gate_tok[:, None, :], 0.0), axis=2)
    mlp_pick_low = mlp_pick.astype(bf16).reshape(slot_total, tok_dev)
    mlp_choice = [
        (mlp_pick & mlp_hot[k][:, None, :]).astype(bf16).reshape(slot_total, tok_dev)
        for k in range(per_token)
    ]
    mlp_back = jnp.concatenate(mlp_choice, axis=1)

    attn_all = attn_routes.reshape(experts, tok_dev, per_token)
    own_mine = jnp.any(attn_all == expert_id, axis=2)
    own_rank = before_counts(own_mine)
    own_pick = own_mine[:, None, :] & (own_rank[:, None, :] == slot_ids[None, :, None])
    own_low = own_pick.astype(bf16)
    places_row, positions_row = token_positions(cont_ids)

    def slot_value(row):
        return jnp.sum(
            jnp.where(own_pick, row.reshape(experts, 1, tok_dev), 0), axis=2, dtype=jnp.int32
        )

    slot_place = slot_value(places_row) + jnp.where(
        jnp.any(own_pick, axis=2), 0, expert_ids[:, None] * tok_dev
    )
    slot_cont = slot_value(cont_ids)
    slot_pos = slot_value(positions_row)
    attn_mine_routes = lax.dynamic_slice_in_dim(attn_routes, expert_id * tok_dev, tok_dev)
    attn_hot = attn_mine_routes.T[:, None, :] == expert_ids[None, :, None]
    attn_mine = jnp.any(attn_hot, axis=0)
    attn_rank = before_counts(attn_mine)
    attn_pick = attn_mine[:, None, :] & (attn_rank[:, None, :] == slot_ids[None, :, None])
    attn_gate_tok = jnp.sum(jnp.where(attn_hot, attn_gates.T[:, None, :], 0.0), axis=0)
    attn_slot_gate = jnp.sum(jnp.where(attn_pick, attn_gate_tok[:, None, :], 0.0), axis=2)
    attn_pick_low = attn_pick.astype(bf16).reshape(slot_total, tok_dev)
    attn_back = jnp.concatenate(
        [
            (attn_pick & attn_hot[k][:, None, :]).astype(bf16).reshape(slot_total, tok_dev)
            for k in range(per_token)
        ],
        axis=1,
    )
    kcos, ksin = rope_tables(positions_row)
    qcos, qsin = rope_tables(slot_pos.reshape(-1))

    cot_rows = dot_nn(mlp_pick_low, cotangent).reshape(experts, slots, width)
    send_grad = (mlp_slot_gate[:, :, None] * cot_rows).astype(bf16)
    steps = slots // 8
    cuts = [0, 8 * max(int(steps * MLP_FIRST), 1), slots]
    pieces = list(zip(cuts[:-1], cuts[1:]))

    def to_plane(rows):
        return lax.all_gather(rows.reshape(-1, width), "dp", axis=0, tiled=True)

    got_grad = hops(hold(send_grad, x_all), 1)

    input_f32 = x_all.astype(f32)
    normed_all, _ = rms_parts(input_f32)
    hidden_all = (normed_all * gain_one).astype(bf16)
    query_rows = lax.dot_general(
        own_low,
        hidden_all.reshape(experts, tok_dev, width),
        (((2,), (1,)), ((0,), (0,))),
        preferred_element_type=f32,
    ).astype(bf16).reshape(slot_total, width)
    query_low = project(
        query_rows, query_full, qcos, qsin, features, slot_total
    ).reshape(experts, slots, features)
    kv_low = project(hidden_all, kv_full, kcos, ksin, features, tok_dev)
    got_grad = hold(got_grad, kv_low)
    plane_grad = [to_plane(got_grad[:, low:high, :]) for low, high in pieces]
    slot_place3 = slot_place[:, :, None]
    slot_cont3 = slot_cont[:, :, None]
    key_cont = cont_ids[None, :]
    attn_low, lse = attend(query_low, kv_low, slot_place3, slot_cont3, key_cont, tok_dev)
    attn_flat = attn_low.reshape(slot_total, features)
    result_low = dot_nn(attn_flat, output_full).astype(bf16)
    result_back = exchange(result_low.reshape(experts, slots, width)).reshape(slot_total, width)
    result_tok = dot_tn(attn_back, result_back)
    own_f32 = layer_input.astype(f32)
    residual = own_f32
    for k in range(per_token):
        residual = residual + attn_gates[:, k : k + 1] * result_tok[k * tok_dev : (k + 1) * tok_dev]
    normed_two, scale_two = rms_parts(residual)
    second_low = (normed_two * gain_two).astype(bf16)

    send_in = dot_nn(mlp_pick_low, second_low).astype(bf16).reshape(experts, slots, width)
    gate_rows, up_rows, down_rows = (mlp_weight[:, 0, j, :] for j in range(3))
    plane_in = [to_plane(hops(send_in[:, low:high, :], 1)) for low, high in pieces]
    kept, out_parts, in_parts = [], [], []
    for number, (rows_in, rows_grad) in enumerate(zip(plane_in, plane_grad)):
        in_part, out_part, *keep = unit_block(
            rows_in, rows_grad, gate_rows, up_rows, down_rows, owners, number
        )
        in_parts.append(in_part)
        out_parts.append(out_part)
        kept.append(keep)

    def join(parts):
        back = []
        for part, (low, high) in zip(parts, pieces):
            back.append(hops(part.reshape(experts, high - low, width), -1))
        return jnp.concatenate(back, axis=1).reshape(slot_total, width)

    in_back = join(in_parts)
    grad_mlp = [dot_tn(k, r) for k, r in zip(kept[0], (plane_in[0], plane_in[0], plane_grad[0]))]
    grad_second = dot_tn(mlp_pick_low, after(in_back, *grad_mlp))
    cot_f32 = cotangent.astype(f32)
    grad_resid = cot_f32 + rms_back(grad_second, normed_two, scale_two, gain_two)

    cot_slots = dot_nn(attn_pick_low, grad_resid.astype(bf16)).reshape(experts, slots, width)
    send_cot = (attn_slot_gate[:, :, None] * cot_slots).astype(bf16)
    grad_mlp = [
        g + dot_tn(k, r)
        for g, k, r in zip(grad_mlp, kept[1], (plane_in[1], plane_in[1], plane_grad[1]))
    ]
    grad_mlp_weight = jnp.stack(grad_mlp, axis=1)[:, None, :, :]
    grad_result = after(exchange(send_cot), *grad_mlp).reshape(slot_total, width)
    output_term = dot_tn(attn_flat, grad_result).astype(bf16)
    grad_output_w = plane_sum(output_term)
    grad_attn = dot_nt(after(grad_result, output_term), output_full).astype(bf16)
    out_back = join([plane_sum(after(part, *in_parts)) for part in out_parts])
    attend_again = attend_back
    grad_query, grad_keys, grad_values = attend_again(
        query_low,
        kv_low,
        grad_attn.reshape(experts, slots, features),
        lse,
        slot_place3,
        slot_cont3,
        key_cont,
        qcos.reshape(experts, slots, HEAD),
        qsin.reshape(experts, slots, HEAD),
        kcos,
        ksin,
        tok_dev,
    )
    grad_query = grad_query.reshape(slot_total, features)
    mixed_tok = dot_tn(mlp_back, out_back)
    final = residual
    for k in range(per_token):
        final = final + mlp_gates[:, k : k + 1] * mixed_tok[k * tok_dev : (k + 1) * tok_dev]
    output = final.astype(bf16)

    grad_keys_w = dot_tn(hidden_all, grad_keys).astype(bf16)
    grad_values_w = dot_tn(hidden_all, grad_values).astype(bf16)
    grad_kv_w = jnp.concatenate([grad_keys_w, grad_values_w], axis=1)
    grad_query = hold(grad_query, grad_keys_w, grad_values_w)
    grad_kv_w = plane_sum(grad_kv_w)
    grad_rows = dot_nt(grad_query, query_full).astype(bf16)
    half = width // 2
    grad_h, grad_first = [], []
    for low in (0, half):
        span = slice(low, low + half)
        routed = lax.dot_general(
            own_low,
            grad_rows[:, span].reshape(experts, slots, half),
            (((1,), (1,)), ((0,), (0,))),
            preferred_element_type=f32,
        ).reshape(group, half)
        part = (
            dot_nt(grad_keys, kv_full[span, :features])
            + dot_nt(grad_values, kv_full[span, features:])
            + routed
        )
        grad_h.append(part)
        grad_first.append(
            hop_sum(part.astype(bf16).reshape(experts, tok_dev, half), expert_id, experts)
        )
    query_term = dot_tn(query_rows, hold(grad_query, grad_h[1])).astype(bf16)
    grad_query_w = plane_sum(query_term)
    grad_output_w, grad_query_w = hold(grad_output_w, grad_kv_w), hold(grad_query_w, grad_kv_w)
    grad_kv_w = hop_sum(grad_kv_w.reshape(experts, -1, 2 * features), expert_id, experts)
    grad_h = lax.optimization_barrier(tuple(grad_h))
    grad_gain_one = [
        jnp.sum(part * normed_all[:, low : low + half], axis=0)
        for part, low in zip(grad_h, (0, half))
    ]
    grad_gain_two = jnp.sum(grad_second * normed_two, axis=0)
    grad_first = jnp.concatenate(grad_first, axis=1)
    normed_one, scale_one = rms_parts(own_f32)
    grad_input = grad_resid + rms_back(grad_first, normed_one, scale_one, gain_one)

    gain_rows = jnp.concatenate(
        [
            jnp.concatenate(grad_gain_one).reshape(owners * experts, part_size),
            grad_gain_two.reshape(owners * experts, part_size),
        ],
        axis=1,
    )
    gain_rows = lax.all_to_all(
        gain_rows[:, None, :], ("dp", "expert"), split_axis=0, concat_axis=0, tiled=True
    )
    gain_rows = jnp.sum(gain_rows, axis=(0, 1))
    grad_gain_attn, grad_gain_mlp = gain_rows[:part_size], gain_rows[part_size:]
    return (
        output,
        grad_input,
        grad_gain_attn,
        grad_gain_mlp,
        grad_kv_w,
        grad_query_w.astype(f32)[:, None, :],
        grad_output_w.astype(f32)[:, None, :],
        grad_mlp_weight,
    )


def solution(mesh):
    placed = (
        P(("dp", "expert"), None),
        P(("dp", "expert"), None),
        P("dp"),
        P("dp", None),
        P(("dp", "expert"), None),
        P(("dp", "expert"), None),
        P(("dp", "expert"), None),
        P(("dp", "expert")),
        P(("dp", "expert")),
        P(("dp", "expert"), None),
        P("dp", "expert", None),
        P("dp", "expert", None),
        P("dp", "expert", None, None),
    )
    return jax.shard_map(
        layer,
        mesh=mesh,
        in_specs=placed,
        out_specs=(
            P(("dp", "expert"), None),
            P(("dp", "expert"), None),
            P(("dp", "expert")),
            P(("dp", "expert")),
            P(("dp", "expert"), None),
            P("dp", "expert", None),
            P("dp", "expert", None),
            P("dp", "expert", None, None),
        ),
        check_vma=False,
    )
```

time: 2720 us -> 1410 us (0.52)
  waiting for transfers between devices: 1180 us -> 417 us
  Pallas kernels: 0 us -> 500 us
  matrix products: 591 us -> 243 us
  blocking collectives: 318 us -> 0 us
  local copies, waits for them, and re-layouts: 333 us -> 75.8 us
  other arithmetic: 214 us -> 75.6 us
  starting transfers between devices: 41.5 us -> 71.9 us
    reduce_scatter x3 -> x5, waiting for transfers between devices: 561 us -> 1.5 us  [plane_sum(): return lax.psum_scatter(terms, 'dp', scatter_dimension=0, tiled=True)]
    pallas_call x0 -> x8, Pallas kernels: none -> 500 us  [the longest x2 231 us: unit_block(): pl.pallas_call(unit_kernel, in_specs=[hbm, hbm, vmem, vmem, vmem], out_sp...]
    all_to_all x9 -> x4, waiting for transfers between devices: 527 us -> 94.3 us  [the longest x2 93.8 us: exchange(): lax.all_to_all(rows, 'expert', split_axis=0, concat_axis=0, tiled=True)]
    dot_general x130 -> x29, matrix products: 591 us -> 243 us  [the longest x13 151 us: dot_tn(): lax.dot_general(left, right, contract_first, preferred_element_type=f32)]
    all_to_all x1 -> x0, blocking collectives: 232 us -> none  [local(): lax.all_to_all(grad_kv_term.astype(jnp.bfloat16), 'expert', split_axis=0,...]
    ppermute x0 -> x30, waiting for transfers between devices: none -> 202 us  [the longest x21 128 us: hops(): pieces.append(lax.ppermute(rows[hop], 'expert', ring))]
    gather x21 -> x0, local copies, waits for them, and re-layouts: 86.8 us -> none  [the longest x2 17.1 us: local(): rows_back.reshape(slot_total, width)[attn_back]]
    unnamed x2 -> x0, blocking collectives: 86.6 us -> none
  transfers between devices with their start and end apart: 16 -> 46, of which waited for: 10 -> 22; matrix products, arithmetic and copies ran while one was open for 26% -> 27% of each run, Pallas kernels for 0% -> 23%
where the time goes in v1:
time: 1410 us; the launch traced here: 1400 us
  Pallas kernels  500 us (35%)
  waiting for transfers between devices  417 us (30%)
  matrix products  243 us (17%)
  local copies, waits for them, and re-layouts  75.8 us (5%)
  other arithmetic  75.6 us (5%)
  starting transfers between devices  71.9 us (5%)
  between operations  19.6 us (1%)
    pallas_call x2, Pallas kernels, unit_block(): pl.pallas_call(unit_kernel, in_specs=[hbm, hbm, vmem, vmem, vmem], out_sp...  231 us
    dot_general x13, matrix products, dot_tn(): lax.dot_general(left, right, contract_first, preferred_element_type=f32)  151 us
    pallas_call x2, Pallas kernels, line_gather(): pl.pallas_call(line_kernel, in_specs=[hbm] * (1 + len(waits)), out_specs=...  132 us
    ppermute x21, waiting for transfers between devices, hops(): pieces.append(lax.ppermute(rows[hop], 'expert', ring))  128 us
    all_gather x4, waiting for transfers between devices, to_plane(): return lax.all_gather(rows.reshape(-1, width), 'dp', axis=0, tiled=True)  117 us
    all_to_all x2, waiting for transfers between devices, exchange(): lax.all_to_all(rows, 'expert', split_axis=0, concat_axis=0, tiled=True)  93.8 us
    ppermute x9, waiting for transfers between devices, hop_sum(): got.append(lax.ppermute(piece, 'expert', ring))  73.7 us
    dot_general x6, matrix products, dot_nt(): lax.dot_general(left, right, contract_last, preferred_element_type=f32)  64.3 us
  transfers between devices with their start and end apart: 46, of which 22 were waited for; matrix products, arithmetic and copies ran while one was open for 27% of the time, Pallas kernels for 23%

profile of v1, /device:TPU:0, one launch (start us, length us, event | category | flops | bytes accessed | tf_op | source)
XLA Modules:
  0.0 1403.6 jit_solution(3189978772869552448)
XLA Ops:
  7.2 41.0 %line_gather.2 = bf16[4,64,4096]{2,1,0:T(8,128)(2,1)} custom-call(bf16[64,4096]{1,0:T(8,128)(2,1)} %own_ref.2), custom_call_target="tpu_custom_call" | custom-call | bytes 4194304 | tf_op jit(solution)/shard_map/line_gather/pallas_call | solution.py:589
  55.3 91.4 %line_gather.3 = bf16[4,320,2048]{2,1,0:T(8,128)(2,1)} custom-call(bf16[320,2048]{1,0:T(8,128)(2,1)} %own_ref.3, bf16[256,4096]{1,0:T(8,128)(2,1)} %bitcast.242), custom_call_target="tpu_custom_call" | custom-call | bytes 10485760 | tf_op jit(solution)/shard_map/line_gather/pallas_call | solution.py:589
  173.6 36.2 %shard_map.189.k_ref.v_ref = bf16[1280,4096]{1,0:T(8,128)(2,1)} custom-call(bf16[1280,2048]{1,0:T(8,128)(2,1)} %get-tuple-element.109.x_ref, bf16[2048,4096]{1,0:T(8,128)(2,1)} %all-gather.10.cloned.1.call-done.w_ref, f32[1280,128]{1,0:T(8,128)} %get-tuple-element.183.cos_ref.kcos_ref, f32[1280,128]{1,0:T(8,128)} %get-tuple-element.184.sin_ref.ksin_ref), custom_call_target="tpu_custom_call" | custom-call | flops 21474836480 | bytes 32505856 | tf_op jit(solution)/shard_map/pallas_call | solution.py:110
  236.9 12.3 shard_map.188
  249.2 32.7 %attend.1 = (bf16[4,184,2048]{2,1,0:T(8,128)(2,1)}, f32[4,184,2048]{2,1,0:T(8,128)}) custom-call(bf16[4,184,2048]{2,1,0:T(8,128)(2,1)} %bitcast.263, bf16[1280,4096]{1,0:T(8,128)(2,1)} %shard_map.189.k_ref.v_ref, bf16[1280,4096]{1,0:T(8,128)(2,1)} %shard_map.189.k_ref.v_ref, s32[4,184,1]{2,1,0:T(8,128)} %select_add_fusion.place_ref, ...), custom_call_target="tpu_custom_call" | custom-call | flops 5016387584 | bytes 22544384 | tf_op jit(solution)/shard_map/attend/pallas_call | solution.py:166
  281.9 12.4 fusion.22
  302.0 65.5 %all-to-all-done.1 = bf16[4,184,2048]{2,1,0:T(8,128)(2,1)} async-done(((bf16[4,184,2048]{2,1,0:T(8,128)(2,1)}), bf16[4,184,2048]{2,1,0:T(8,128)(2,1)}, u32[]{:S(2)}, u32[]{:S(2)}) %all-to-all-start.1) | async-done | bytes 3014688 | tf_op jit(solution)/shard_map/all_to_all | solution.py:613
  387.4 15.5 %collective-permute-done.1 = bf16[72,2048]{1,0:T(8,128)(2,1)S(1)} collective-permute-done((bf16[72,2048]{1,0:T(8,128)(2,1)S(1)}, bf16[72,2048]{1,0:T(8,128)(2,1)S(1)}, u32[]{:S(2)}, u32[]{:S(2)}) %collective-permute-start.1) | collective-permute-done | bytes 294944 | tf_op jit(solution)/shard_map/ppermute | solution.py:641
  419.4 31.4 %collective-permute-done.7 = bf16[112,2048]{1,0:T(8,128)(2,1)S(1)} collective-permute-done((bf16[112,2048]{1,0:T(8,128)(2,1)S(1)}, bf16[112,2048]{1,0:T(8,128)(2,1)S(1)}, u32[]{:S(2)}, u32[]{:S(2)}) %collective-permute-start.7) | collective-permute-done | bytes 458784 | tf_op jit(solution)/shard_map/ppermute | solution.py:641
  463.9 98.7 %unit_block.2 = (bf16[288,2048]{1,0:T(8,128)(2,1)}, bf16[2304,2048]{1,0:T(8,128)(2,1)}, bf16[2304,704]{1,0:T(8,128)(2,1)}, bf16[2304,704]{1,0:T(8,128)(2,1)}, bf16[2304,704]{1,0:T(8,128)(2,1)}) custom-call(bf16[2304,2048]{1,0:T(8,128)(2,1)} %all-gather.12.cloned.1.call-done.x_hbm, bf16[2304,2048]{1,0:T(8,128)(2,1)} %all-gather.14.cloned.1.call-done.g_hbm, ...), custom_call_target="tpu_custom_call" | custom-call | flops 39862665216 | bytes 46694400 | tf_op jit(solution)/shard_map/unit_block/pallas_call | solution.py:454
  562.6 29.7 %all-gather.18.cloned.1.call-done.g_hbm = bf16[3584,2048]{1,0:T(8,128)(2,1)} async-done(((bf16[448,2048]{1,0:T(8,128)(2,1)}), bf16[3584,2048]{1,0:T(8,128)(2,1)}) %all-gather.18.cloned.1.call-update) | async-done | bytes 14680080 | tf_op jit(solution)/shard_map/all_gather | solution.py:746
  592.3 82.4 %all-gather.16.cloned.1.call-done.x_hbm = bf16[3584,2048]{1,0:T(8,128)(2,1)} async-done(((bf16[448,2048]{1,0:T(8,128)(2,1)}), bf16[3584,2048]{1,0:T(8,128)(2,1)}) %all-gather.16.cloned.1.call-update) | async-done | bytes 14680080 | tf_op jit(solution)/shard_map/all_gather | solution.py:746
  674.7 132.3 %unit_block.3 = (bf16[448,2048]{1,0:T(8,128)(2,1)}, bf16[3584,2048]{1,0:T(8,128)(2,1)}, bf16[3584,704]{1,0:T(8,128)(2,1)}, bf16[3584,704]{1,0:T(8,128)(2,1)}, bf16[3584,704]{1,0:T(8,128)(2,1)}) custom-call(bf16[3584,2048]{1,0:T(8,128)(2,1)} %all-gather.16.cloned.1.call-done.x_hbm, bf16[3584,2048]{1,0:T(8,128)(2,1)} %all-gather.18.cloned.1.call-done.g_hbm, ...), custom_call_target="tpu_custom_call" | custom-call | flops 62008590336 | bytes 67829760 | tf_op jit(solution)/shard_map/unit_block/pallas_call | solution.py:454
  816.1 12.3 fusion.109
  837.4 12.6 fusion.108
  854.1 18.3 %convolution_add_fusion = f32[704,2048]{1,0:T(8,128)} fusion(f32[704,2048]{1,0:T(8,128)} %fusion.109, bf16[3584,704]{1,0:T(8,128)(2,1)} %get-tuple-element.43, bf16[3584,2048]{1,0:T(8,128)(2,1)} %all-gather.18.cloned.1.call-done.g_hbm), kind=kOutput, calls=%fused_computation.37 | convolution fusion | flops 10336206848 | bytes 31260672 | tf_op jit(solution)/shard_map/dot_general | solution.py:72
  892.0 11.2 all-to-all-start.2
  903.2 20.1 %convolution_add_fusion.2 = f32[704,2048]{1,0:T(8,128)} fusion(f32[704,2048]{1,0:T(8,128)} %fusion.107, bf16[3584,704]{1,0:T(8,128)(2,1)} %get-tuple-element.41, bf16[3584,2048]{1,0:T(8,128)(2,1)} %all-gather.16.cloned.1.call-done.x_hbm), kind=kOutput, calls=%fused_computation.39 | convolution fusion | flops 10336206848 | bytes 31260672 | tf_op jit(solution)/shard_map/dot_general | solution.py:72
  923.3 18.3 %convolution_add_fusion.1 = f32[704,2048]{1,0:T(8,128)} fusion(f32[704,2048]{1,0:T(8,128)} %fusion.108, bf16[3584,704]{1,0:T(8,128)(2,1)} %get-tuple-element.42, bf16[3584,2048]{1,0:T(8,128)(2,1)} %all-gather.16.cloned.1.call-done.x_hbm), kind=kOutput, calls=%fused_computation.38 | convolution fusion | flops 10336206848 | bytes 31260672 | tf_op jit(solution)/shard_map/dot_general | solution.py:72
  941.7 28.3 %all-to-all-done.2 = bf16[4,184,2048]{2,1,0:T(8,128)(2,1)S(1)} async-done(((bf16[4,184,2048]{2,1,0:T(8,128)(2,1)}), bf16[4,184,2048]{2,1,0:T(8,128)(2,1)S(1)}, u32[]{:S(2)}, u32[]{:S(2)}) %all-to-all-start.2) | async-done | bytes 3014688 | tf_op jit(solution)/shard_map/all_to_all | solution.py:613
  970.0 11.3 bitcast_convert_fusion.1
  991.3 55.6 %attend_back.1 = (bf16[4,184,2048]{2,1,0:T(8,128)(2,1)}, bf16[1280,2048]{1,0:T(8,128)(2,1)}, bf16[1280,2048]{1,0:T(8,128)(2,1)}) custom-call(bf16[4,184,2048]{2,1,0:T(8,128)(2,1)} %bitcast.264, bf16[1280,4096]{1,0:T(8,128)(2,1)} %shard_map.189.k_ref.v_ref, bf16[1280,4096]{1,0:T(8,128)(2,1)} %shard_map.189.k_ref.v_ref, bf16[4,184,2048]{2,1,0:T(8,128)(2,1)} %bitcast.303, ...), custom_call_target="tpu_custom_call" | custom-call | flops 12540968960 | bytes 36044800 | tf_op jit(solution)/shard_map/attend_back/pallas_call | solution.py:256
  1046.9 15.3 %convolution_convert_fusion.1 = bf16[2048,2048]{1,0:T(8,128)(2,1)S(1)} fusion(bf16[1280,2048]{1,0:T(8,128)(2,1)} %get-tuple-element.109.x_ref, bf16[1280,2048]{1,0:T(8,128)(2,1)} %get-tuple-element.47), kind=kOutput, calls=%fused_computation.16 | convolution fusion | flops 10741612544 | bytes 18874368 | tf_op jit(solution)/shard_map/dot_general | solution.py:72
  1062.2 15.1 %convolution_convert_fusion = bf16[2048,2048]{1,0:T(8,128)(2,1)S(1)} fusion(bf16[1280,2048]{1,0:T(8,128)(2,1)S(1)} %bitcast.251, bf16[1280,2048]{1,0:T(8,128)(2,1)} %get-tuple-element.48), kind=kOutput, calls=%fused_computation.15 | convolution fusion | flops 10741612544 | bytes 18874368 | tf_op jit(solution)/shard_map/dot_general | solution.py:72
  1113.6 13.1 fusion.105
  1148.3 11.2 fusion.17
  1198.2 20.8 %copy.52 = f32[704,1,3,2048]{3,1,2,0:T(1,128)} copy(f32[704,1,3,2048]{3,0,2,1:T(8,128)S(1)} %maximum_bitcast_fusion) | data formatting | bytes 34603008
  1230.6 29.5 %collective-permute-done.22 = bf16[320,1024]{1,0:T(8,128)(2,1)} collective-permute-done((bf16[320,1024]{1,0:T(8,128)(2,1)}, bf16[320,1024]{1,0:T(8,128)(2,1)}, u32[]{:S(2)}, u32[]{:S(2)}) %collective-permute-start.22) | collective-permute-done | bytes 655392 | tf_op jit(solution)/shard_map/ppermute | solution.py:622
  1278.1 12.0 collective-permute-done.10
  1300.0 24.7 %collective-permute-done.13 = bf16[112,2048]{1,0:T(8,128)(2,1)S(1)} collective-permute-done((bf16[112,2048]{1,0:T(8,128)(2,1)S(1)}, bf16[112,2048]{1,0:T(8,128)(2,1)S(1)}, u32[]{:S(2)}, u32[]{:S(2)}) %collective-permute-start.13) | collective-permute-done | bytes 458784 | tf_op jit(solution)/shard_map/ppermute | solution.py:641
  1362.5 11.2 collective-permute-done.29
  1373.7 20.2 %collective-permute-done.28 = bf16[64,4096]{1,0:T(8,128)(2,1)} collective-permute-done((bf16[64,4096]{1,0:T(8,128)(2,1)S(1)}, bf16[64,4096]{1,0:T(8,128)(2,1)}, u32[]{:S(2)}, u32[]{:S(2)}) %collective-permute-start.28) | collective-permute-done | bytes 524320 | tf_op jit(solution)/shard_map/ppermute | solution.py:622
  (368 shorter events, 341.4 us)
Async XLA Ops:
  7.2 166.4 %all-gather.10.cloned.1.call-start = ((), (), s32[]{:S(2)}) async-start(), calls=%async_computation.9 | async-start | bytes 18874368 | tf_op jit(solution)/shard_map/all_gather | solution.py:679
  48.2 188.6 %all-gather.20.cloned.1.call-start = ((), (), s32[]{:S(2)}) async-start(), calls=%async_computation.19 | async-start | bytes 9437184 | tf_op jit(solution)/shard_map/all_gather | solution.py:681
  49.0 232.9 %all-gather.22.cloned.1.call-start = ((), (), s32[]{:S(2)}) async-start(), calls=%async_computation.20 | async-start | bytes 9437184 | tf_op jit(solution)/shard_map/all_gather | solution.py:682
  50.4 112.7 %all-to-all-start = ((bf16[32,1,128]{2,1,0:T(2,128)(2,1)}), bf16[32,1,128]{2,1,0:T(2,128)(2,1)S(1)}, u32[]{:S(2)}, u32[]{:S(2)}) async-start(bf16[32,1,128]{2,1,0:T(2,128)(2,1)} %broadcast_in_dim.151), calls=%async_computation | async-start | bytes 32768 | tf_op jit(solution)/shard_map/all_to_all | solution.py:647
  55.2 403.7 %all-gather.14.cloned.1.call-start = ((), (), s32[]{:S(2)}) async-start(), calls=%async_computation.11 | async-start | bytes 10616832 | tf_op jit(solution)/shard_map/all_gather | solution.py:746
  152.4 59.4 %collective-permute-start.5 = (bf16[184,2048]{1,0:T(8,128)(2,1)}, bf16[184,2048]{1,0:T(8,128)(2,1)S(1)}, u32[]{:S(2)}, u32[]{:S(2)}) collective-permute-start(bf16[184,2048]{1,0:T(8,128)(2,1)} %get-tuple-element.117), channel_id=1, source_target_pairs={{0,3},{1,0},{2,1},{3,2},{4,7},{5,4},{6,5},{7,6},{8,11},{9,8},{10,9... | collective-permute-start | bytes 2261000 | tf_op jit(solution)/shard_map/ppermute | solution.py:641
  154.6 62.4 %collective-permute-start.4 = (bf16[184,2048]{1,0:T(8,128)(2,1)}, bf16[184,2048]{1,0:T(8,128)(2,1)S(1)}, u32[]{:S(2)}, u32[]{:S(2)}) collective-permute-start(bf16[184,2048]{1,0:T(8,128)(2,1)} %get-tuple-element.118), channel_id=1, source_target_pairs={{0,2},{1,3},{2,0},{3,1},{4,6},{5,7},{6,4},{7,5},{8,10},{9,11},{10,... | collective-permute-start | bytes 2261000 | tf_op jit(solution)/shard_map/ppermute | solution.py:641
  154.6 62.4 %collective-permute-start.3 = (bf16[184,2048]{1,0:T(8,128)(2,1)S(1)}, bf16[184,2048]{1,0:T(8,128)(2,1)S(1)}, u32[]{:S(2)}, u32[]{:S(2)}) collective-permute-start(bf16[184,2048]{1,0:T(8,128)(2,1)S(1)} %get-tuple-element.119), channel_id=1, source_target_pairs={{0,1},{1,2},{2,3},{3,0},{4,5},{5,6},{6,7},{7,4},{8,9},{9,10},{10,1... | collective-permute-start | bytes 2261000 | tf_op jit(solution)/shard_map/ppermute | solution.py:641
  294.2 73.2 %all-to-all-start.1 = ((bf16[4,184,2048]{2,1,0:T(8,128)(2,1)}), bf16[4,184,2048]{2,1,0:T(8,128)(2,1)}, u32[]{:S(2)}, u32[]{:S(2)}) async-start(bf16[4,184,2048]{2,1,0:T(8,128)(2,1)} %bitcast.258), calls=%async_computation.1 | async-start | bytes 6029312 | tf_op jit(solution)/shard_map/all_to_all | solution.py:613
  299.0 164.9 %all-gather.12.cloned.1.call-start = ((), (), s32[]{:S(2)}) async-start(), calls=%async_computation.10 | async-start | bytes 10616832 | tf_op jit(solution)/shard_map/all_gather | solution.py:746
  404.1 188.2 %all-gather.18.cloned.1.call-start = ((), (), s32[]{:S(2)}) async-start(), calls=%async_computation.13 | async-start | bytes 16515072 | tf_op jit(solution)/shard_map/all_gather | solution.py:746
  405.5 269.2 %all-gather.16.cloned.1.call-start = ((), (), s32[]{:S(2)}) async-start(), calls=%async_computation.12 | async-start | bytes 16515072 | tf_op jit(solution)/shard_map/all_gather | solution.py:746
  407.2 43.6 %collective-permute-start.7 = (bf16[112,2048]{1,0:T(8,128)(2,1)S(1)}, bf16[112,2048]{1,0:T(8,128)(2,1)S(1)}, u32[]{:S(2)}, u32[]{:S(2)}) collective-permute-start(bf16[112,2048]{1,0:T(8,128)(2,1)S(1)} %get-tuple-element.122), channel_id=1, source_target_pairs={{0,2},{1,3},{2,0},{3,1},{4,6},{5,7},{6,4},{7,5},{8,10},{9,11},{10,... | collective-permute-start | bytes 1376264 | tf_op jit(solution)/shard_map/ppermute | solution.py:641
  410.7 40.1 %collective-permute-start.6 = (bf16[112,2048]{1,0:T(8,128)(2,1)S(1)}, bf16[112,2048]{1,0:T(8,128)(2,1)S(1)}, u32[]{:S(2)}, u32[]{:S(2)}) collective-permute-start(bf16[112,2048]{1,0:T(8,128)(2,1)S(1)} %get-tuple-element.123), channel_id=1, source_target_pairs={{0,1},{1,2},{2,3},{3,0},{4,5},{5,6},{6,7},{7,4},{8,9},{9,10},{10,1... | collective-permute-start | bytes 1376264 | tf_op jit(solution)/shard_map/ppermute | solution.py:641
  452.3 810.6 %reduce-scatter.6.cloned.1.call-start = ((), (), s32[]{:S(2)}) async-start(), calls=%async_computation.14 | async-start | bytes 10616832 | tf_op jit(solution)/shard_map/reduce_scatter | solution.py:633
  807.1 462.2 %reduce-scatter.8.cloned.1.call-start = ((), (), s32[]{:S(2)}) async-start(), calls=%async_computation.15 | async-start | bytes 16515072 | tf_op jit(solution)/shard_map/reduce_scatter | solution.py:633
  810.7 40.2 %collective-permute-start.17 = (bf16[72,2048]{1,0:T(8,128)(2,1)S(1)}, bf16[72,2048]{1,0:T(8,128)(2,1)S(1)}, u32[]{:S(2)}, u32[]{:S(2)}) collective-permute-start(bf16[72,2048]{1,0:T(8,128)(2,1)S(1)} %get-tuple-element.145), channel_id=1, source_target_pairs={{0,1},{1,2},{2,3},{3,0},{4,5},{5,6},{6,7},{7,4},{8,9},{9,10},{10,1... | collective-permute-start | bytes 884744 | tf_op jit(solution)/shard_map/ppermute | solution.py:641
  812.2 60.2 %collective-permute-start.16 = (bf16[72,2048]{1,0:T(8,128)(2,1)S(1)}, bf16[72,2048]{1,0:T(8,128)(2,1)S(1)}, u32[]{:S(2)}, u32[]{:S(2)}) collective-permute-start(bf16[72,2048]{1,0:T(8,128)(2,1)S(1)} %get-tuple-element.146), channel_id=1, source_target_pairs={{0,2},{1,3},{2,0},{3,1},{4,6},{5,7},{6,4},{7,5},{8,10},{9,11},{10,... | collective-permute-start | bytes 884744 | tf_op jit(solution)/shard_map/ppermute | solution.py:641
  814.6 57.8 %collective-permute-start.15 = (bf16[72,2048]{1,0:T(8,128)(2,1)S(1)}, bf16[72,2048]{1,0:T(8,128)(2,1)S(1)}, u32[]{:S(2)}, u32[]{:S(2)}) collective-permute-start(bf16[72,2048]{1,0:T(8,128)(2,1)S(1)} %get-tuple-element.147), channel_id=1, source_target_pairs={{0,3},{1,0},{2,1},{3,2},{4,7},{5,4},{6,5},{7,6},{8,11},{9,8},{10,9... | collective-permute-start | bytes 884744 | tf_op jit(solution)/shard_map/ppermute | solution.py:641
  892.0 78.0 %all-to-all-start.2 = ((bf16[4,184,2048]{2,1,0:T(8,128)(2,1)}), bf16[4,184,2048]{2,1,0:T(8,128)(2,1)S(1)}, u32[]{:S(2)}, u32[]{:S(2)}) async-start(bf16[4,184,2048]{2,1,0:T(8,128)(2,1)} %multiply_convert_fusion.1), calls=%async_computation.4 | async-start | bytes 6029312 | tf_op jit(solution)/shard_map/all_to_all | solution.py:613
  903.2 429.5 %reduce-scatter.10.cloned.1.call-start = ((), (), s32[]{:S(2)}) async-start(), calls=%async_computation.16 | async-start | bytes 18874368 | tf_op jit(solution)/shard_map/reduce_scatter | solution.py:633
  1087.6 247.0 %reduce-scatter.14.cloned.1.call-start = ((), (), s32[]{:S(2)}) async-start(), calls=%async_computation.18 | async-start | bytes 9437184 | tf_op jit(solution)/shard_map/reduce_scatter | solution.py:633
  1088.4 264.7 %reduce-scatter.12.cloned.1.call-start = ((), (), s32[]{:S(2)}) async-start(), calls=%async_computation.17 | async-start | bytes 9437184 | tf_op jit(solution)/shard_map/reduce_scatter | solution.py:633
  1143.5 44.7 %collective-permute-start.24 = (bf16[320,1024]{1,0:T(8,128)(2,1)}, bf16[320,1024]{1,0:T(8,128)(2,1)S(1)}, u32[]{:S(2)}, u32[]{:S(2)}) collective-permute-start(bf16[320,1024]{1,0:T(8,128)(2,1)} %get-tuple-element.129), channel_id=1, source_target_pairs={{0,1},{1,2},{2,3},{3,0},{4,5},{5,6},{6,7},{7,4},{8,9},{9,10},{10,1... | collective-permute-start | bytes 1966088 | tf_op jit(solution)/shard_map/ppermute | solution.py:622
  1144.1 76.0 %collective-permute-start.26 = (bf16[320,1024]{1,0:T(8,128)(2,1)}, bf16[320,1024]{1,0:T(8,128)(2,1)}, u32[]{:S(2)}, u32[]{:S(2)}) collective-permute-start(bf16[320,1024]{1,0:T(8,128)(2,1)} %get-tuple-element.130), channel_id=1, source_target_pairs={{0,3},{1,0},{2,1},{3,2},{4,7},{5,4},{6,5},{7,6},{8,11},{9,8},{10,9... | collective-permute-start | bytes 1966088 | tf_op jit(solution)/shard_map/ppermute | solution.py:622
  1147.3 72.8 %collective-permute-start.25 = (bf16[320,1024]{1,0:T(8,128)(2,1)}, bf16[320,1024]{1,0:T(8,128)(2,1)}, u32[]{:S(2)}, u32[]{:S(2)}) collective-permute-start(bf16[320,1024]{1,0:T(8,128)(2,1)} %get-tuple-element.131), channel_id=1, source_target_pairs={{0,2},{1,3},{2,0},{3,1},{4,6},{5,7},{6,4},{7,5},{8,10},{9,11},{10,... | collective-permute-start | bytes 1966088 | tf_op jit(solution)/shard_map/ppermute | solution.py:622
  1179.0 40.5 %all-to-all-start.3 = ((f32[32,1,128]{2,1,0:T(1,128)}), f32[32,1,128]{2,1,0:T(1,128)S(1)}, u32[]{:S(2)}, u32[]{:S(2)}) async-start(f32[32,1,128]{2,1,0:T(1,128)} %bitcast.98), calls=%async_computation.5 | async-start | bytes 32768 | tf_op jit(solution)/shard_map/all_to_all | solution.py:884
  1186.1 44.4 %collective-permute-start.23 = (bf16[320,1024]{1,0:T(8,128)(2,1)}, bf16[320,1024]{1,0:T(8,128)(2,1)S(1)}, u32[]{:S(2)}, u32[]{:S(2)}) collective-permute-start(bf16[320,1024]{1,0:T(8,128)(2,1)} %get-tuple-element.127), channel_id=1, source_target_pairs={{0,3},{1,0},{2,1},{3,2},{4,7},{5,4},{6,5},{7,6},{8,11},{9,8},{10,9... | collective-permute-start | bytes 1966088 | tf_op jit(solution)/shard_map/ppermute | solution.py:622
  1188.2 71.9 %collective-permute-start.22 = (bf16[320,1024]{1,0:T(8,128)(2,1)}, bf16[320,1024]{1,0:T(8,128)(2,1)}, u32[]{:S(2)}, u32[]{:S(2)}) collective-permute-start(bf16[320,1024]{1,0:T(8,128)(2,1)} %get-tuple-element.128), channel_id=1, source_target_pairs={{0,2},{1,3},{2,0},{3,1},{4,6},{5,7},{6,4},{7,5},{8,10},{9,11},{10,... | collective-permute-start | bytes 1966088 | tf_op jit(solution)/shard_map/ppermute | solution.py:622
  1271.6 53.1 %collective-permute-start.13 = (bf16[112,2048]{1,0:T(8,128)(2,1)S(1)}, bf16[112,2048]{1,0:T(8,128)(2,1)S(1)}, u32[]{:S(2)}, u32[]{:S(2)}) collective-permute-start(bf16[112,2048]{1,0:T(8,128)(2,1)S(1)} %get-tuple-element.141), channel_id=1, source_target_pairs={{0,2},{1,3},{2,0},{3,1},{4,6},{5,7},{6,4},{7,5},{8,10},{9,11},{10,... | collective-permute-start | bytes 1376264 | tf_op jit(solution)/shard_map/ppermute | solution.py:641
  1277.5 47.2 %collective-permute-start.12 = (bf16[112,2048]{1,0:T(8,128)(2,1)S(1)}, bf16[112,2048]{1,0:T(8,128)(2,1)S(1)}, u32[]{:S(2)}, u32[]{:S(2)}) collective-permute-start(bf16[112,2048]{1,0:T(8,128)(2,1)S(1)} %get-tuple-element.142), channel_id=1, source_target_pairs={{0,3},{1,0},{2,1},{3,2},{4,7},{5,4},{6,5},{7,6},{8,11},{9,8},{10,9... | collective-permute-start | bytes 1376264 | tf_op jit(solution)/shard_map/ppermute | solution.py:641
  1350.1 43.8 %collective-permute-start.28 = (bf16[64,4096]{1,0:T(8,128)(2,1)S(1)}, bf16[64,4096]{1,0:T(8,128)(2,1)}, u32[]{:S(2)}, u32[]{:S(2)}) collective-permute-start(bf16[64,4096]{1,0:T(8,128)(2,1)S(1)} %get-tuple-element.134), channel_id=1, source_target_pairs={{0,2},{1,3},{2,0},{3,1},{4,6},{5,7},{6,4},{7,5},{8,10},{9,11},{10,... | collective-permute-start | bytes 1572872 | tf_op jit(solution)/shard_map/ppermute | solution.py:622
  (90 other events, 1453.4 us)
Sparse Core Ops, SparseCore 0:
  48.4 89.8 all-gather.9
  140.1 54.2 all-gather.19
  196.4 54.2 all-gather.21
  252.4 58.6 all-gather.13
  404.2 59.6 all-gather.11
  466.2 126.0 all-gather.17
  594.8 79.9 all-gather.15
  807.2 75.8 reduce-scatter.5
  886.6 104.6 reduce-scatter.7
  1087.7 115.3 reduce-scatter.9
  1206.6 71.5 reduce-scatter.13
  1281.5 71.5 reduce-scatter.11

commit v2 on v1

--- a/solution.py
+++ b/solution.py
@@ -13,7 +13,7 @@
 PROMPT = 1024
 CONTS = 2
 GROUP_TOK = 1280
-MLP_FIRST = 0.4
+MLP_FIRST = 0.5
 
 norm_eps = 1e-06
 rope_base = 10000.0
@@ -139,14 +139,18 @@
         bias[s] = jnp.where(allowed, 0.0, neg_fill)
 
 
-def attend_kernel(spans, q_ref, k_ref, v_ref, place_ref, cont_ref, kcont_ref, out_ref, lse_ref, bias):
+def attend_kernel(
+    spans, low, q_ref, k_ref, v_ref, place_ref, cont_ref, kcont_ref, out_ref, lse_ref, bias
+):
+    high = low + out_ref.shape[1]
+
     @pl.when(pl.program_id(0) == 0)
     def _():
         fill_bias(bias, place_ref, cont_ref, kcont_ref)
 
     scale2 = log2e / math.sqrt(HEAD)
     for s, span in enumerate(spans):
-        scores = dot_nt(q_ref[s], k_ref[:span, :]) * scale2 + bias[s, :, :span]
+        scores = dot_nt(q_ref[s, low:high, :], k_ref[:span, :]) * scale2 + bias[s, :, :span]
         peak = jnp.max(scores, axis=1, keepdims=True)
         weights = jnp.exp2(scores - peak)
         total = jnp.sum(weights, axis=1, keepdims=True)
@@ -155,16 +159,18 @@
         lse_ref[s] = jnp.broadcast_to(peak + jnp.log2(total), lse_ref.shape[1:])
 
 
-def attend(query, kv_low, place, cont, kcont, tokens):
-    blocks, slots, features = query.shape
+def attend(query, kv_low, place, cont, kcont, tokens, low, high):
+    blocks, total, features = query.shape
+    slots = high - low
     keys = kv_low.shape[0]
     heads = features // HEAD
     spans = key_spans(blocks, tokens, keys)
     work = 2 * 2 * slots * sum(spans) * HEAD * heads
-    qspec = pl.BlockSpec((blocks, slots, HEAD), lambda h: (0, 0, h))
+    qspec = pl.BlockSpec((blocks, total, HEAD), lambda h: (0, 0, h))
+    ospec = pl.BlockSpec((blocks, slots, HEAD), lambda h: (0, 0, h))
     whole = pl.BlockSpec((blocks, slots, 1), lambda h: (0, 0, 0))
     return pl.pallas_call(
-        functools.partial(attend_kernel, spans),
+        functools.partial(attend_kernel, spans, low),
         grid=(heads,),
         in_specs=[
             qspec,
@@ -174,42 +180,32 @@
             whole,
             pl.BlockSpec((1, keys), lambda h: (0, 0)),
         ],
-        out_specs=[qspec, qspec],
+        out_specs=[ospec, ospec],
         out_shape=[
-            jax.ShapeDtypeStruct(query.shape, bf16),
-            jax.ShapeDtypeStruct(query.shape, f32),
+            jax.ShapeDtypeStruct((blocks, slots, features), bf16),
+            jax.ShapeDtypeStruct((blocks, slots, features), f32),
         ],
         scratch_shapes=[pltpu.VMEM((blocks, slots, keys), f32)],
         cost_estimate=pl.CostEstimate(
             flops=work,
-            bytes_accessed=4 * query.size + 2 * kv_low.size + 4 * query.size,
+            bytes_accessed=2 * query.size + 2 * kv_low.size + 6 * blocks * slots * features,
             transcendentals=slots * sum(spans) * heads,
         ),
         name="attend",
-    )(query, kv_low, kv_low, place, cont, kcont)
-
-
-def attend_back_kernel(
-    spans,
-    q_ref,
-    k_ref,
-    v_ref,
-    g_ref,
-    lse_ref,
-    place_ref,
-    cont_ref,
-    kcont_ref,
-    qcos_ref,
-    qsin_ref,
-    kcos_ref,
-    ksin_ref,
-    dq_ref,
-    dk_ref,
-    dv_ref,
-    bias,
-    dk_sum,
-    dv_sum,
-):
+    )(query, kv_low, kv_low, place[:, low:high], cont[:, low:high], kcont)
+
+
+def attend_back_kernel(spans, low, carried, *refs):
+    q_ref, k_ref, v_ref, g_ref, lse_ref, place_ref, cont_ref, kcont_ref = refs[:8]
+    qcos_ref, qsin_ref, kcos_ref, ksin_ref = refs[8:12]
+    refs = refs[12:]
+    if carried:
+        old_dq_ref, old_dk_ref, old_dv_ref = refs[:3]
+        refs = refs[3:]
+    dq_ref, dk_ref, dv_ref, bias, dk_sum, dv_sum = refs
+    slots = g_ref.shape[1]
+    high = low + slots
+
     @pl.when(pl.program_id(0) == 0)
     def _():
         fill_bias(bias, place_ref, cont_ref, kcont_ref)
@@ -219,7 +215,7 @@
     last = len(spans) - 1
     for s in range(last, -1, -1):
         span = spans[s]
-        query, grad = q_ref[s], g_ref[s]
+        query, grad = q_ref[s, low:high, :], g_ref[s]
         keys = k_ref[:span, :]
         scores = dot_nt(query, keys) * scale2 + bias[s, :, :span]
         prob = jnp.exp2(scores - lse_ref[s][:, :1])
@@ -228,40 +224,61 @@
         grad_scores = (prob * (grad_prob - inner)).astype(bf16)
         dq = dot_nn(grad_scores, keys) * scale
         dq = dq * qcos_ref[s] - pltpu.roll(dq, HEAD // 2, 1) * qsin_ref[s]
-        dq_ref[s] = dq.astype(bf16)
+        if carried:
+            dq_ref[s, :low, :] = old_dq_ref[s]
+            dq_ref[s, low:high, :] = dq.astype(bf16)
+        else:
+            dq_ref[s] = dq.astype(bf16)
         dk = dot_tn(grad_scores, query)
         dv = dot_tn(prob.astype(bf16), grad)
-        if s == last:
+        if s < last:
+            dk_sum[:span, :] += dk
+            dv_sum[:span, :] += dv
+        elif carried:
+            dk_sum[...] = old_dk_ref[...] + dk
+            dv_sum[...] = old_dv_ref[...] + dv
+        else:
             dk_sum[...] = dk
             dv_sum[...] = dv
-        else:
-            dk_sum[:span, :] += dk
-            dv_sum[:span, :] += dv
-    dk = dk_sum[...] * scale
-    dk_ref[...] = (dk * kcos_ref[...] - pltpu.roll(dk, HEAD // 2, 1) * ksin_ref[...]).astype(bf16)
-    dv_ref[...] = dv_sum[...].astype(bf16)
-
-
-def attend_back(query, kv_low, grad, lse, place, cont, kcont, qcos, qsin, kcos, ksin, tokens):
-    blocks, slots, features = query.shape
+    if carried:
+        dk = dk_sum[...] * scale
+        dk = dk * kcos_ref[...] - pltpu.roll(dk, HEAD // 2, 1) * ksin_ref[...]
+        dk_ref[...] = dk.astype(bf16)
+        dv_ref[...] = dv_sum[...].astype(bf16)
+    else:
+        dk_ref[...] = dk_sum[...]
+        dv_ref[...] = dv_sum[...]
+
+
+def attend_back(
+    query, kv_low, grad, lse, place, cont, kcont, qcos, qsin, kcos, ksin, tokens, low, old=()
+):
+    blocks, total, features = query.shape
+    slots = grad.shape[1]
+    high = low + slots
     keys = kv_low.shape[0]
     heads = features // HEAD
     spans = key_spans(blocks, tokens, keys)
     work = 5 * 2 * slots * sum(spans) * HEAD * heads
-    qspec = pl.BlockSpec((blocks, slots, HEAD), lambda h: (0, 0, h))
+    carried = bool(old)
+
+    def by_head(rows):
+        return pl.BlockSpec((blocks, rows, HEAD), lambda h: (0, 0, h))
+
     kspec = pl.BlockSpec((keys, HEAD), lambda h: (0, h))
     whole = pl.BlockSpec((blocks, slots, 1), lambda h: (0, 0, 0))
     qtab = pl.BlockSpec((blocks, slots, HEAD), lambda h: (0, 0, 0))
     ktab = pl.BlockSpec((keys, HEAD), lambda h: (0, 0))
+    kept_type = bf16 if carried else f32
     return pl.pallas_call(
-        functools.partial(attend_back_kernel, spans),
+        functools.partial(attend_back_kernel, spans, low, carried),
         grid=(heads,),
         in_specs=[
-            qspec,
+            by_head(total),
             kspec,
             pl.BlockSpec((keys, HEAD), lambda h: (0, heads + h)),
-            qspec,
-            qspec,
+            by_head(slots),
+            by_head(slots),
             whole,
             whole,
             pl.BlockSpec((1, keys), lambda h: (0, 0)),
@@ -269,12 +286,13 @@
             qtab,
             ktab,
             ktab,
-        ],
-        out_specs=[qspec, kspec, kspec],
+        ]
+        + ([by_head(low), kspec, kspec] if carried else []),
+        out_specs=[by_head(total if carried else slots), kspec, kspec],
         out_shape=[
-            jax.ShapeDtypeStruct(query.shape, bf16),
-            jax.ShapeDtypeStruct((keys, features), bf16),
-            jax.ShapeDtypeStruct((keys, features), bf16),
+            jax.ShapeDtypeStruct((blocks, total if carried else slots, features), bf16),
+            jax.ShapeDtypeStruct((keys, features), kept_type),
+            jax.ShapeDtypeStruct((keys, features), kept_type),
         ],
         scratch_shapes=[
             pltpu.VMEM((blocks, slots, keys), f32),
@@ -283,11 +301,25 @@
         ],
         cost_estimate=pl.CostEstimate(
             flops=work,
-            bytes_accessed=10 * query.size + 4 * kv_low.size,
+            bytes_accessed=10 * blocks * slots * features + 8 * kv_low.size,
             transcendentals=slots * sum(spans) * heads,
         ),
         name="attend_back",
-    )(query, kv_low, kv_low, grad, lse, place, cont, kcont, qcos, qsin, kcos, ksin)
+    )(
+        query,
+        kv_low,
+        kv_low,
+        grad,
+        lse,
+        place[:, low:high],
+        cont[:, low:high],
+        kcont,
+        qcos[:, low:high],
+        qsin[:, low:high],
+        kcos,
+        ksin,
+        *old,
+    )
 
 
 def unit_kernel(
@@ -609,10 +641,6 @@
     return value
 
 
-def exchange(rows):
-    return lax.all_to_all(rows, "expert", split_axis=0, concat_axis=0, tiled=True)
-
-
 def hop_sum(parts, place, count):
     total = lax.dynamic_index_in_dim(parts, place, 0, keepdims=False).astype(f32)
     got = []
@@ -633,6 +661,23 @@
     return lax.psum_scatter(terms, "dp", scatter_dimension=0, tiled=True)
 
 
+def chip_sum(terms, owners):
+    chips = owners // 2
+    place = lax.axis_index("dp")
+    chip, core = place // 2, place % 2
+    blocks = terms.reshape(chips, 2, -1, terms.shape[1])
+    mine = lax.dynamic_index_in_dim(blocks, core, 1, keepdims=False)
+    other = lax.dynamic_index_in_dim(blocks, 1 - core, 1, keepdims=False)
+    other = lax.ppermute(other, "dp", [(i, i + 1 - 2 * (i % 2)) for i in range(owners)])
+    mine = (mine.astype(f32) + other.astype(f32)).astype(bf16)
+    got = [lax.dynamic_index_in_dim(mine, chip, 0, keepdims=False)]
+    for hop in range(1, chips):
+        ring = [(i, (i // 2 + hop) % chips * 2 + i % 2) for i in range(owners)]
+        piece = lax.dynamic_index_in_dim(mine, (chip + hop) % chips, 0, keepdims=False)
+        got.append(lax.ppermute(piece, "dp", ring))
+    return sum(piece.astype(f32) for piece in got)
+
+
 def hops(rows, sign):
     count = rows.shape[0]
     pieces = [rows[0]]
@@ -640,6 +685,28 @@
         ring = [(i, (i + sign * hop) % count) for i in range(count)]
         pieces.append(lax.ppermute(rows[hop], "expert", ring))
     return jnp.stack(pieces)
+
+
+def scatter_hops(rows, place):
+    count = rows.shape[0]
+    pieces = [lax.dynamic_index_in_dim(rows, place, 0, keepdims=False)]
+    for hop in range(1, count):
+        ring = [(i, (i + hop) % count) for i in range(count)]
+        piece = lax.dynamic_index_in_dim(rows, (place + hop) % count, 0, keepdims=False)
+        pieces.append(lax.ppermute(piece, "expert", ring))
+    return jnp.stack(pieces)
+
+
+def ordered_hops(rows, place):
+    count = rows.shape[0]
+    got = jnp.zeros_like(rows)
+    for hop in range(count):
+        piece = lax.dynamic_index_in_dim(rows, (place + hop) % count, 0, keepdims=False)
+        if hop:
+            ring = [(i, (i + hop) % count) for i in range(count)]
+            piece = lax.ppermute(piece, "expert", ring)
+        got = lax.dynamic_update_index_in_dim(got, piece, (place - hop) % count, 0)
+    return got
 
 
 def spread(rows, axes, count):
@@ -726,12 +793,15 @@
     attn_gate_tok = jnp.sum(jnp.where(attn_hot, attn_gates.T[:, None, :], 0.0), axis=0)
     attn_slot_gate = jnp.sum(jnp.where(attn_pick, attn_gate_tok[:, None, :], 0.0), axis=2)
     attn_pick_low = attn_pick.astype(bf16).reshape(slot_total, tok_dev)
-    attn_back = jnp.concatenate(
-        [
-            (attn_pick & attn_hot[k][:, None, :]).astype(bf16).reshape(slot_total, tok_dev)
-            for k in range(per_token)
-        ],
-        axis=1,
+    from_ids = (expert_id - expert_ids) % experts
+    result_hot = attn_mine_routes.T[:, None, :] == from_ids[None, :, None]
+    result_pick = jnp.any(result_hot, axis=0)
+    result_rank = before_counts(result_pick)
+    result_pick = result_pick[:, None, :] & (
+        result_rank[:, None, :] == slot_ids[None, :, None]
+    )
+    result_hot = jnp.concatenate(
+        [(result_pick & result_hot[k][:, None, :]).astype(bf16) for k in range(per_token)], axis=2
     )
     kcos, ksin = rope_tables(positions_row)
     qcos, qsin = rope_tables(slot_pos.reshape(-1))
@@ -765,11 +835,21 @@
     slot_place3 = slot_place[:, :, None]
     slot_cont3 = slot_cont[:, :, None]
     key_cont = cont_ids[None, :]
-    attn_low, lse = attend(query_low, kv_low, slot_place3, slot_cont3, key_cont, tok_dev)
-    attn_flat = attn_low.reshape(slot_total, features)
-    result_low = dot_nn(attn_flat, output_full).astype(bf16)
-    result_back = exchange(result_low.reshape(experts, slots, width)).reshape(slot_total, width)
-    result_tok = dot_tn(attn_back, result_back)
+    mid = min(-(-slots // 32) * 16, slots - 8)
+    halves = ((0, mid), (mid, slots))
+    attn_low, lse, result_tok = [], [], 0.0
+    for low, high in halves:
+        attn_part, lse_part = attend(
+            query_low, kv_low, slot_place3, slot_cont3, key_cont, tok_dev, low, high
+        )
+        attn_part = attn_part.reshape(-1, features)
+        attn_low.append(attn_part)
+        lse.append(lse_part)
+        result_low = dot_nn(attn_part, output_full).astype(bf16)
+        result_back = scatter_hops(result_low.reshape(experts, high - low, width), expert_id)
+        result_tok = result_tok + dot_tn(
+            result_hot[:, low:high].reshape(-1, per_token * tok_dev), result_back.reshape(-1, width)
+        )
     own_f32 = layer_input.astype(f32)
     residual = own_f32
     for k in range(per_token):
@@ -803,22 +883,24 @@
 
     cot_slots = dot_nn(attn_pick_low, grad_resid.astype(bf16)).reshape(experts, slots, width)
     send_cot = (attn_slot_gate[:, :, None] * cot_slots).astype(bf16)
-    grad_mlp = [
-        g + dot_tn(k, r)
-        for g, k, r in zip(grad_mlp, kept[1], (plane_in[1], plane_in[1], plane_grad[1]))
+    for j, rows in enumerate((plane_in[1], plane_in[1], plane_grad[1])):
+        grad_mlp[j] = grad_mlp[j] + dot_tn(kept[1][j], rows)
+    grad_mlp_weight = jnp.stack(grad_mlp, axis=1)[:, None, :, :]
+    grad_result = [
+        ordered_hops(send_cot[:, low:high], expert_id).reshape(-1, width)
+        for low, high in halves
     ]
-    grad_mlp_weight = jnp.stack(grad_mlp, axis=1)[:, None, :, :]
-    grad_result = after(exchange(send_cot), *grad_mlp).reshape(slot_total, width)
-    output_term = dot_tn(attn_flat, grad_result).astype(bf16)
-    grad_output_w = plane_sum(output_term)
-    grad_attn = dot_nt(after(grad_result, output_term), output_full).astype(bf16)
-    out_back = join([plane_sum(after(part, *in_parts)) for part in out_parts])
-    attend_again = attend_back
-    grad_query, grad_keys, grad_values = attend_again(
-        query_low,
-        kv_low,
-        grad_attn.reshape(experts, slots, features),
-        lse,
+    grad_attn = []
+    for rows in grad_result:
+        grad_attn.append(
+            dot_nt(rows, output_full).astype(bf16).reshape(experts, -1, features)
+        )
+    output_term = (
+        dot_tn(attn_low[0], grad_result[0]) + dot_tn(attn_low[1], grad_result[1])
+    ).astype(bf16)
+    grad_output_w = chip_sum(output_term, owners)
+    out_back = join([plane_sum(part) for part in out_parts])
+    tables = (
         slot_place3,
         slot_cont3,
         key_cont,
@@ -828,6 +910,10 @@
         ksin,
         tok_dev,
     )
+    carried = attend_back(query_low, kv_low, grad_attn[0], lse[0], *tables, 0)
+    grad_query, grad_keys, grad_values = attend_back(
+        query_low, kv_low, grad_attn[1], lse[1], *tables, mid, tuple(carried)
+    )
     grad_query = grad_query.reshape(slot_total, features)
     mixed_tok = dot_tn(mlp_back, out_back)
     final = residual
@@ -837,9 +923,9 @@
 
     grad_keys_w = dot_tn(hidden_all, grad_keys).astype(bf16)
     grad_values_w = dot_tn(hidden_all, grad_values).astype(bf16)
-    grad_kv_w = jnp.concatenate([grad_keys_w, grad_values_w], axis=1)
     grad_query = hold(grad_query, grad_keys_w, grad_values_w)
-    grad_kv_w = plane_sum(grad_kv_w)
+    grad_kv_w = [plane_sum(grad_keys_w), plane_sum(grad_values_w)]
+
     grad_rows = dot_nt(grad_query, query_full).astype(bf16)
     half = width // 2
     grad_h, grad_first = [], []
@@ -861,15 +947,18 @@
             hop_sum(part.astype(bf16).reshape(experts, tok_dev, half), expert_id, experts)
         )
     query_term = dot_tn(query_rows, hold(grad_query, grad_h[1])).astype(bf16)
-    grad_query_w = plane_sum(query_term)
-    grad_output_w, grad_query_w = hold(grad_output_w, grad_kv_w), hold(grad_query_w, grad_kv_w)
-    grad_kv_w = hop_sum(grad_kv_w.reshape(experts, -1, 2 * features), expert_id, experts)
+    grad_query_w = chip_sum(query_term, owners)
+    grad_kv_w = jnp.concatenate(
+        [hop_sum(part.reshape(experts, -1, features), expert_id, experts) for part in grad_kv_w],
+        axis=1,
+    )
     grad_h = lax.optimization_barrier(tuple(grad_h))
     grad_gain_one = [
         jnp.sum(part * normed_all[:, low : low + half], axis=0)
         for part, low in zip(grad_h, (0, half))
     ]
     grad_gain_two = jnp.sum(grad_second * normed_two, axis=0)
+    first_sum = grad_first[0]
     grad_first = jnp.concatenate(grad_first, axis=1)
     normed_one, scale_one = rms_parts(own_f32)
     grad_input = grad_resid + rms_back(grad_first, normed_one, scale_one, gain_one)
@@ -882,7 +971,7 @@
         axis=1,
     )
     gain_rows = lax.all_to_all(
-        gain_rows[:, None, :], ("dp", "expert"), split_axis=0, concat_axis=0, tiled=True
+        hold(gain_rows, first_sum)[:, None, :], ("dp", "expert"), split_axis=0, concat_axis=0, tiled=True
     )
     gain_rows = jnp.sum(gain_rows, axis=(0, 1))
     grad_gain_attn, grad_gain_mlp = gain_rows[:part_size], gain_rows[part_size:]
@@ -892,8 +981,8 @@
         grad_gain_attn,
         grad_gain_mlp,
         grad_kv_w,
-        grad_query_w.astype(f32)[:, None, :],
-        grad_output_w.astype(f32)[:, None, :],
+        grad_query_w[:, None, :],
+        grad_output_w[:, None, :],
         grad_mlp_weight,
     )
 

time: 1410 us -> 1560 us (1.11)
  Pallas kernels: 500 us -> 549 us
  waiting for transfers between devices: 417 us -> 461 us
  starting transfers between devices: 71.9 us -> 95 us
  local copies, waits for them, and re-layouts: 75.8 us -> 92.6 us
    ppermute x0 -> x20, waiting for transfers between devices: none -> 169 us  [the longest x6 89.9 us: chip_sum(): got.append(lax.ppermute(piece, 'dp', ring))]
    all_to_all x3 -> x1, waiting for transfers between devices: 94.3 us -> 0.01 us  [layer(): lax.all_to_all(hold(gain_rows, first_sum)[:, None, :], ('dp', 'expert'),...]
    pallas_call x2 -> x4, Pallas kernels: 88.2 us -> 135 us  [the longest x2 80.9 us: attend_back(): pl.pallas_call(functools.partial(attend_back_kernel, spans, low, carried)...]
    ppermute x0 -> x20, starting transfers between devices: none -> 39.7 us  [the longest x6 17.4 us: scatter_hops(): pieces.append(lax.ppermute(piece, 'expert', ring))]
    all_gather x4, waiting for transfers between devices: 117 us -> 78.6 us  [to_plane(): return lax.all_gather(rows.reshape(-1, width), 'dp', axis=0, tiled=True)]
    all_to_all x3 -> x1, starting transfers between devices: 20 us -> 3.53 us  [layer(): lax.all_to_all(hold(gain_rows, first_sum)[:, None, :], ('dp', 'expert'),...]
    ppermute x9 -> x12, waiting for transfers between devices: 73.7 us -> 82.8 us  [hop_sum(): got.append(lax.ppermute(piece, 'expert', ring))]
    dot_general x13 -> x15, matrix products: 151 us -> 158 us  [dot_tn(): lax.dot_general(left, right, contract_first, preferred_element_type=f32)]
  transfers between devices with their start and end apart: 46 -> 66, of which waited for: 22 -> 28; matrix products, arithmetic and copies ran while one was open for 27% -> 25% of each run, Pallas kernels for 23% -> 27%
where the time goes in v2:
time: 1560 us; the launch traced here: 1550 us
  Pallas kernels  549 us (35%)
  waiting for transfers between devices  461 us (30%)
  matrix products  248 us (16%)
  starting transfers between devices  95 us (6%)
  local copies, waits for them, and re-layouts  92.6 us (6%)
  other arithmetic  89.7 us (6%)
  between operations  20.3 us (1%)
    pallas_call x2, Pallas kernels, unit_block(): pl.pallas_call(unit_kernel, in_specs=[hbm, hbm, vmem, vmem, vmem], out_sp...  233 us
    dot_general x15, matrix products, dot_tn(): lax.dot_general(left, right, contract_first, preferred_element_type=f32)  158 us
    pallas_call x2, Pallas kernels, line_gather(): pl.pallas_call(line_kernel, in_specs=[hbm] * (1 + len(waits)), out_specs=...  132 us
    ppermute x21, waiting for transfers between devices, hops(): pieces.append(lax.ppermute(rows[hop], 'expert', ring))  128 us
    ppermute x6, waiting for transfers between devices, chip_sum(): got.append(lax.ppermute(piece, 'dp', ring))  89.9 us
    ppermute x12, waiting for transfers between devices, hop_sum(): got.append(lax.ppermute(piece, 'expert', ring))  82.8 us
    pallas_call x2, Pallas kernels, attend_back(): pl.pallas_call(functools.partial(attend_back_kernel, spans, low, carried)...  80.9 us
    all_gather x4, waiting for transfers between devices, to_plane(): return lax.all_gather(rows.reshape(-1, width), 'dp', axis=0, tiled=True)  78.6 us
  transfers between devices with their start and end apart: 66, of which 28 were waited for; matrix products, arithmetic and copies ran while one was open for 25% of the time, Pallas kernels for 27%

profile of v2, /device:TPU:0, one launch (start us, length us, event | category | flops | bytes accessed | tf_op | source)
XLA Modules:
  0.0 1554.7 jit_solution(4746157148420011744)
XLA Ops:
  7.2 41.0 %line_gather.2 = bf16[4,64,4096]{2,1,0:T(8,128)(2,1)} custom-call(bf16[64,4096]{1,0:T(8,128)(2,1)} %own_ref.2), custom_call_target="tpu_custom_call" | custom-call | bytes 4194304 | tf_op jit(solution)/shard_map/line_gather/pallas_call | solution.py:621
  55.3 91.4 %line_gather.3 = bf16[4,320,2048]{2,1,0:T(8,128)(2,1)} custom-call(bf16[320,2048]{1,0:T(8,128)(2,1)} %own_ref.3, bf16[256,4096]{1,0:T(8,128)(2,1)} %bitcast.334), custom_call_target="tpu_custom_call" | custom-call | bytes 10485760 | tf_op jit(solution)/shard_map/line_gather/pallas_call | solution.py:621
  173.9 36.0 %shard_map.189.k_ref.v_ref.refs_1_.refs_2_ = bf16[1280,4096]{1,0:T(8,128)(2,1)} custom-call(bf16[1280,2048]{1,0:T(8,128)(2,1)} %get-tuple-element.111.x_ref, bf16[2048,4096]{1,0:T(8,128)(2,1)} %all-gather.10.cloned.1.call-done.w_ref, f32[1280,128]{1,0:T(8,128)} %get-tuple-element.209.cos_ref.refs_10_, f32[1280,128]{1,0:T(8,128)} %get-tuple-element.210.sin_ref.refs_11_), custom_call_target="tpu_custom_call" | custom-call | flops 21474836480 | bytes 32505856 | tf_op jit(solution)/shard_map/pallas_call | solution.py:110
  258.6 27.2 %attend.2 = (bf16[4,96,2048]{2,1,0:T(8,128)(2,1)}, f32[4,96,2048]{2,1,0:T(8,128)}) custom-call(bf16[4,184,2048]{2,1,0:T(8,128)(2,1)} %bitcast.328, bf16[1280,4096]{1,0:T(8,128)(2,1)} %shard_map.189.k_ref.v_ref.refs_1_.refs_2_, bf16[1280,4096]{1,0:T(8,128)(2,1)} %shard_map.189.k_ref.v_ref.refs_1_.refs_2_, s32[4,96,1]{2,1,0:T(8,128)} %slice.345.place_ref.refs_5_, ...), custom_call_target="tpu_custom_call" | custom-call | flops 2617245696 | bytes 18219008 | tf_op jit(solution)/shard_map/attend/pallas_call | solution.py:172
  309.1 26.9 %attend.3 = (bf16[4,88,2048]{2,1,0:T(8,128)(2,1)}, f32[4,88,2048]{2,1,0:T(8,128)}) custom-call(bf16[4,184,2048]{2,1,0:T(8,128)(2,1)} %bitcast.329, bf16[1280,4096]{1,0:T(8,128)(2,1)} %shard_map.189.k_ref.v_ref.refs_1_.refs_2_, bf16[1280,4096]{1,0:T(8,128)(2,1)} %shard_map.189.k_ref.v_ref.refs_1_.refs_2_, s32[4,88,1]{2,1,0:T(8,128)} %slice.347.place_ref.refs_5_, ...), custom_call_target="tpu_custom_call" | custom-call | flops 2399141888 | bytes 17825792 | tf_op jit(solution)/shard_map/attend/pallas_call | solution.py:172
  355.5 21.4 %collective-permute-done.4 = bf16[88,2048]{1,0:T(8,128)(2,1)} collective-permute-done((bf16[88,2048]{1,0:T(8,128)(2,1)}, bf16[88,2048]{1,0:T(8,128)(2,1)}, u32[]{:S(2)}, u32[]{:S(2)}) %collective-permute-start.4) | collective-permute-done | bytes 360480 | tf_op jit(solution)/shard_map/ppermute | solution.py:696
  394.7 23.6 %collective-permute-done.7 = bf16[88,2048]{1,0:T(8,128)(2,1)S(1)} collective-permute-done((bf16[88,2048]{1,0:T(8,128)(2,1)S(1)}, bf16[88,2048]{1,0:T(8,128)(2,1)S(1)}, u32[]{:S(2)}, u32[]{:S(2)}) %collective-permute-start.7) | collective-permute-done | bytes 360480 | tf_op jit(solution)/shard_map/ppermute | solution.py:686
  432.6 24.7 %collective-permute-done.16 = bf16[96,2048]{1,0:T(8,128)(2,1)S(1)} collective-permute-done((bf16[96,2048]{1,0:T(8,128)(2,1)S(1)}, bf16[96,2048]{1,0:T(8,128)(2,1)S(1)}, u32[]{:S(2)}, u32[]{:S(2)}) %collective-permute-start.16) | collective-permute-done | bytes 393248 | tf_op jit(solution)/shard_map/ppermute | solution.py:686
  469.4 16.1 %all-gather.12.cloned.1.call-done.x_hbm = bf16[2816,2048]{1,0:T(8,128)(2,1)} async-done(((bf16[352,2048]{1,0:T(8,128)(2,1)}), bf16[2816,2048]{1,0:T(8,128)(2,1)}) %all-gather.12.cloned.1.call-update) | async-done | bytes 11534352 | tf_op jit(solution)/shard_map/all_gather | solution.py:816
  485.5 118.3 %unit_block.2 = (bf16[352,2048]{1,0:T(8,128)(2,1)}, bf16[2816,2048]{1,0:T(8,128)(2,1)}, bf16[2816,704]{1,0:T(8,128)(2,1)}, bf16[2816,704]{1,0:T(8,128)(2,1)}, bf16[2816,704]{1,0:T(8,128)(2,1)}) custom-call(bf16[2816,2048]{1,0:T(8,128)(2,1)} %all-gather.12.cloned.1.call-done.x_hbm, bf16[2816,2048]{1,0:T(8,128)(2,1)} %all-gather.14.cloned.1.call-done.g_hbm, ...), custom_call_target="tpu_custom_call" | custom-call | flops 48721035264 | bytes 55148544 | tf_op jit(solution)/shard_map/unit_block/pallas_call | solution.py:486
  611.7 14.3 fusion.150
  636.6 62.5 %all-gather.16.cloned.1.call-done.x_hbm = bf16[3072,2048]{1,0:T(8,128)(2,1)} async-done(((bf16[384,2048]{1,0:T(8,128)(2,1)}), bf16[3072,2048]{1,0:T(8,128)(2,1)}) %all-gather.16.cloned.1.call-update) | async-done | bytes 12582928 | tf_op jit(solution)/shard_map/all_gather | solution.py:816
  699.0 114.7 %unit_block.3 = (bf16[384,2048]{1,0:T(8,128)(2,1)}, bf16[3072,2048]{1,0:T(8,128)(2,1)}, bf16[3072,704]{1,0:T(8,128)(2,1)}, bf16[3072,704]{1,0:T(8,128)(2,1)}, bf16[3072,704]{1,0:T(8,128)(2,1)}) custom-call(bf16[3072,2048]{1,0:T(8,128)(2,1)} %all-gather.16.cloned.1.call-done.x_hbm, bf16[3072,2048]{1,0:T(8,128)(2,1)} %all-gather.18.cloned.1.call-done.g_hbm, ...), custom_call_target="tpu_custom_call" | custom-call | flops 53150220288 | bytes 59375616 | tf_op jit(solution)/shard_map/unit_block/pallas_call | solution.py:486
  820.6 14.1 fusion.149
  871.7 21.5 %collective-permute-done.28 = bf16[88,2048]{1,0:T(8,128)(2,1)S(1)} collective-permute-done((bf16[88,2048]{1,0:T(8,128)(2,1)S(1)}, bf16[88,2048]{1,0:T(8,128)(2,1)S(1)}, u32[]{:S(2)}, u32[]{:S(2)}) %collective-permute-start.28) | collective-permute-done | bytes 360480 | tf_op jit(solution)/shard_map/ppermute | solution.py:707
  909.3 16.0 %collective-permute-done.31 = bf16[96,2048]{1,0:T(8,128)(2,1)S(1)} collective-permute-done((bf16[96,2048]{1,0:T(8,128)(2,1)S(1)}, bf16[96,2048]{1,0:T(8,128)(2,1)S(1)}, u32[]{:S(2)}, u32[]{:S(2)}) %collective-permute-start.31) | collective-permute-done | bytes 393248 | tf_op jit(solution)/shard_map/ppermute | solution.py:707
  930.0 39.3 %attend_back.2 = (bf16[4,96,2048]{2,1,0:T(8,128)(2,1)}, f32[1280,2048]{1,0:T(8,128)}, f32[1280,2048]{1,0:T(8,128)}) custom-call(bf16[4,184,2048]{2,1,0:T(8,128)(2,1)} %bitcast.330, bf16[1280,4096]{1,0:T(8,128)(2,1)} %shard_map.189.k_ref.v_ref.refs_1_.refs_2_, bf16[1280,4096]{1,0:T(8,128)(2,1)} %shard_map.189.k_ref.v_ref.refs_1_.refs_2_, ...), custom_call_target="tpu_custom_call" | custom-call | flops 6543114240 | bytes 49807360 | tf_op jit(solution)/shard_map/attend_back/pallas_call | solution.py:273
  969.3 41.6 %attend_back.3 = (bf16[4,184,2048]{2,1,0:T(8,128)(2,1)}, bf16[1280,2048]{1,0:T(8,128)(2,1)}, bf16[1280,2048]{1,0:T(8,128)(2,1)}) custom-call(bf16[4,184,2048]{2,1,0:T(8,128)(2,1)} %bitcast.331, bf16[1280,4096]{1,0:T(8,128)(2,1)} %shard_map.189.k_ref.v_ref.refs_1_.refs_2_, bf16[1280,4096]{1,0:T(8,128)(2,1)} %shard_map.189.k_ref.v_ref.refs_1_.refs_2_, ...), custom_call_target="tpu_custom_call" | custom-call | flops 5997854720 | bytes 49152000 | tf_op jit(solution)/shard_map/attend_back/pallas_call | solution.py:273
  1010.9 17.0 %convolution_convert_fusion.1 = bf16[2048,2048]{1,0:T(8,128)(2,1)} fusion(bf16[1280,2048]{1,0:T(8,128)(2,1)} %get-tuple-element.111.x_ref, bf16[1280,2048]{1,0:T(8,128)(2,1)} %get-tuple-element.46), kind=kOutput, calls=%fused_computation.24 | convolution fusion | flops 10741612544 | bytes 18874368 | tf_op jit(solution)/shard_map/dot_general | solution.py:72
  1027.9 16.8 %convolution_convert_fusion = bf16[2048,2048]{1,0:T(8,128)(2,1)} fusion(bf16[1280,2048]{1,0:T(8,128)(2,1)} %get-tuple-element.111.x_ref, bf16[1280,2048]{1,0:T(8,128)(2,1)} %get-tuple-element.47), kind=kOutput, calls=%fused_computation.23 | convolution fusion | flops 10741612544 | bytes 18874368 | tf_op jit(solution)/shard_map/dot_general | solution.py:72
  1046.7 17.0 %add_bitcast_fusion = f32[704,1,2048]{2,0,1:T(8,128)} fusion(f32[704,2048]{1,0:T(8,128)} %fusion.150, bf16[3072,704]{1,0:T(8,128)(2,1)} %get-tuple-element.53, bf16[3072,2048]{1,0:T(8,128)(2,1)} %all-gather.18.cloned.1.call-done.g_hbm), kind=kOutput, calls=%fused_computation.27 | convolution fusion | flops 8859811840 | bytes 28442624 | tf_op jit(solution)/shard_map/dot_general | solution.py:72
  1063.7 16.3 %add_bitcast_fusion.2 = f32[704,1,2048]{2,0,1:T(8,128)} fusion(f32[704,2048]{1,0:T(8,128)} %fusion.148, bf16[3072,704]{1,0:T(8,128)(2,1)} %get-tuple-element.51, bf16[3072,2048]{1,0:T(8,128)(2,1)} %all-gather.16.cloned.1.call-done.x_hbm), kind=kOutput, calls=%fused_computation.29 | convolution fusion | flops 8859811840 | bytes 28442624 | tf_op jit(solution)/shard_map/dot_general | solution.py:72
  1080.1 13.4 add_bitcast_fusion.1
  1202.1 20.8 %copy.44 = f32[704,1,3,2048]{3,1,2,0:T(1,128)} copy(f32[704,1,3,2048]{3,0,2,1:T(8,128)S(1)} %maximum_bitcast_fusion) | data formatting | bytes 34603008
  1228.1 41.0 %collective-permute-done.34 = bf16[320,1024]{1,0:T(8,128)(2,1)} collective-permute-done((bf16[320,1024]{1,0:T(8,128)(2,1)}, bf16[320,1024]{1,0:T(8,128)(2,1)}, u32[]{:S(2)}, u32[]{:S(2)}) %collective-permute-start.34) | collective-permute-done | bytes 655392 | tf_op jit(solution)/shard_map/ppermute | solution.py:650
  1288.7 21.0 %collective-permute-done.37 = bf16[320,1024]{1,0:T(8,128)(2,1)} collective-permute-done((bf16[320,1024]{1,0:T(8,128)(2,1)S(1)}, bf16[320,1024]{1,0:T(8,128)(2,1)}, u32[]{:S(2)}, u32[]{:S(2)}) %collective-permute-start.37) | collective-permute-done | bytes 655392 | tf_op jit(solution)/shard_map/ppermute | solution.py:650
  1336.1 19.0 %collective-permute-done.50 = bf16[256,2048]{1,0:T(8,128)(2,1)} collective-permute-done((bf16[256,2048]{1,0:T(8,128)(2,1)}, bf16[256,2048]{1,0:T(8,128)(2,1)}, u32[]{:S(2)}, u32[]{:S(2)}) %collective-permute-start.50) | collective-permute-done | bytes 1048608 | tf_op jit(solution)/shard_map/ppermute | solution.py:677
  1356.0 27.0 %collective-permute-done.52 = bf16[256,2048]{1,0:T(8,128)(2,1)S(1)} collective-permute-done((bf16[256,2048]{1,0:T(8,128)(2,1)}, bf16[256,2048]{1,0:T(8,128)(2,1)S(1)}, u32[]{:S(2)}, u32[]{:S(2)}) %collective-permute-start.52) | collective-permute-done | bytes 1048608 | tf_op jit(solution)/shard_map/ppermute | solution.py:677
  1391.9 24.9 %collective-permute-done.46 = bf16[256,2048]{1,0:T(8,128)(2,1)} collective-permute-done((bf16[256,2048]{1,0:T(8,128)(2,1)}, bf16[256,2048]{1,0:T(8,128)(2,1)}, u32[]{:S(2)}, u32[]{:S(2)}) %collective-permute-start.46) | collective-permute-done | bytes 1048608 | tf_op jit(solution)/shard_map/ppermute | solution.py:677
  1419.3 18.5 %collective-permute-done.48 = bf16[256,2048]{1,0:T(8,128)(2,1)} collective-permute-done((bf16[256,2048]{1,0:T(8,128)(2,1)}, bf16[256,2048]{1,0:T(8,128)(2,1)}, u32[]{:S(2)}, u32[]{:S(2)}) %collective-permute-start.48) | collective-permute-done | bytes 1048608 | tf_op jit(solution)/shard_map/ppermute | solution.py:677
  1494.3 13.0 collective-permute-done.13
  1515.6 23.6 %collective-permute-done.19 = bf16[96,2048]{1,0:T(8,128)(2,1)S(1)} collective-permute-done((bf16[96,2048]{1,0:T(8,128)(2,1)S(1)}, bf16[96,2048]{1,0:T(8,128)(2,1)S(1)}, u32[]{:S(2)}, u32[]{:S(2)}) %collective-permute-start.19) | collective-permute-done | bytes 393248 | tf_op jit(solution)/shard_map/ppermute | solution.py:686
  (489 shorter events, 494.5 us)
Async XLA Ops:
  7.2 166.7 %all-gather.10.cloned.1.call-start = ((), (), s32[]{:S(2)}) async-start(), calls=%async_computation.6 | async-start | bytes 18874368 | tf_op jit(solution)/shard_map/all_gather | solution.py:746
  48.2 198.1 %all-gather.20.cloned.1.call-start = ((), (), s32[]{:S(2)}) async-start(), calls=%async_computation.15 | async-start | bytes 9437184 | tf_op jit(solution)/shard_map/all_gather | solution.py:748
  49.0 236.8 %all-gather.22.cloned.1.call-start = ((), (), s32[]{:S(2)}) async-start(), calls=%async_computation.16 | async-start | bytes 9437184 | tf_op jit(solution)/shard_map/all_gather | solution.py:749
  50.4 113.5 %all-to-all-start = ((bf16[32,1,128]{2,1,0:T(2,128)(2,1)}), bf16[32,1,128]{2,1,0:T(2,128)(2,1)S(1)}, u32[]{:S(2)}, u32[]{:S(2)}) async-start(bf16[32,1,128]{2,1,0:T(2,128)(2,1)} %broadcast_in_dim.178), calls=%async_computation | async-start | bytes 32768 | tf_op jit(solution)/shard_map/all_to_all | solution.py:714
  55.2 414.2 %all-gather.14.cloned.1.call-start = ((), (), s32[]{:S(2)}) async-start(), calls=%async_computation.8 | async-start | bytes 12976128 | tf_op jit(solution)/shard_map/all_gather | solution.py:816
  152.9 58.9 %collective-permute-start.11 = (bf16[184,2048]{1,0:T(8,128)(2,1)}, bf16[184,2048]{1,0:T(8,128)(2,1)S(1)}, u32[]{:S(2)}, u32[]{:S(2)}) collective-permute-start(bf16[184,2048]{1,0:T(8,128)(2,1)} %get-tuple-element.125), channel_id=1, source_target_pairs={{0,3},{1,0},{2,1},{3,2},{4,7},{5,4},{6,5},{7,6},{8,11},{9,8},{10,9... | collective-permute-start | bytes 2261000 | tf_op jit(solution)/shard_map/ppermute | solution.py:686
  155.2 62.4 %collective-permute-start.10 = (bf16[184,2048]{1,0:T(8,128)(2,1)}, bf16[184,2048]{1,0:T(8,128)(2,1)S(1)}, u32[]{:S(2)}, u32[]{:S(2)}) collective-permute-start(bf16[184,2048]{1,0:T(8,128)(2,1)} %get-tuple-element.126), channel_id=1, source_target_pairs={{0,2},{1,3},{2,0},{3,1},{4,6},{5,7},{6,4},{7,5},{8,10},{9,11},{10,... | collective-permute-start | bytes 2261000 | tf_op jit(solution)/shard_map/ppermute | solution.py:686
  155.2 62.4 %collective-permute-start.9 = (bf16[184,2048]{1,0:T(8,128)(2,1)S(1)}, bf16[184,2048]{1,0:T(8,128)(2,1)S(1)}, u32[]{:S(2)}, u32[]{:S(2)}) collective-permute-start(bf16[184,2048]{1,0:T(8,128)(2,1)S(1)} %get-tuple-element.127), channel_id=1, source_target_pairs={{0,1},{1,2},{2,3},{3,0},{4,5},{5,6},{6,7},{7,4},{8,9},{9,10},{10,1... | collective-permute-start | bytes 2261000 | tf_op jit(solution)/shard_map/ppermute | solution.py:686
  221.9 263.6 %all-gather.12.cloned.1.call-start = ((), (), s32[]{:S(2)}) async-start(), calls=%async_computation.7 | async-start | bytes 12976128 | tf_op jit(solution)/shard_map/all_gather | solution.py:816
  419.6 216.9 %all-gather.18.cloned.1.call-start = ((), (), s32[]{:S(2)}) async-start(), calls=%async_computation.11 | async-start | bytes 14155776 | tf_op jit(solution)/shard_map/all_gather | solution.py:816
  420.9 278.1 %all-gather.16.cloned.1.call-start = ((), (), s32[]{:S(2)}) async-start(), calls=%async_computation.10 | async-start | bytes 14155776 | tf_op jit(solution)/shard_map/all_gather | solution.py:816
  458.8 928.1 %reduce-scatter.9.cloned.1.call-start = ((), (), s32[]{:S(2)}) async-start(), calls=%async_computation.13 | async-start | bytes 9437184 | tf_op jit(solution)/shard_map/reduce_scatter | solution.py:661
  606.4 212.7 %collective-permute-start.23 = (bf16[88,2048]{1,0:T(8,128)(2,1)}, bf16[88,2048]{1,0:T(8,128)(2,1)}, u32[]{:S(2)}, u32[]{:S(2)}) collective-permute-start(bf16[88,2048]{1,0:T(8,128)(2,1)} %get-tuple-element.161), channel_id=1, source_target_pairs={{0,1},{1,2},{2,3},{3,0},{4,5},{5,6},{6,7},{7,4},{8,9},{9,10},{10,1... | collective-permute-start | bytes 1081352 | tf_op jit(solution)/shard_map/ppermute | solution.py:686
  607.9 226.8 %collective-permute-start.22 = (bf16[88,2048]{1,0:T(8,128)(2,1)}, bf16[88,2048]{1,0:T(8,128)(2,1)}, u32[]{:S(2)}, u32[]{:S(2)}) collective-permute-start(bf16[88,2048]{1,0:T(8,128)(2,1)} %get-tuple-element.162), channel_id=1, source_target_pairs={{0,2},{1,3},{2,0},{3,1},{4,6},{5,7},{6,4},{7,5},{8,10},{9,11},{10,... | collective-permute-start | bytes 1081352 | tf_op jit(solution)/shard_map/ppermute | solution.py:686
  610.3 224.4 %collective-permute-start.21 = (bf16[88,2048]{1,0:T(8,128)(2,1)}, bf16[88,2048]{1,0:T(8,128)(2,1)}, u32[]{:S(2)}, u32[]{:S(2)}) collective-permute-start(bf16[88,2048]{1,0:T(8,128)(2,1)} %get-tuple-element.163), channel_id=1, source_target_pairs={{0,3},{1,0},{2,1},{3,2},{4,7},{5,4},{6,5},{7,6},{8,11},{9,8},{10,9... | collective-permute-start | bytes 1081352 | tf_op jit(solution)/shard_map/ppermute | solution.py:686
  864.0 61.4 %collective-permute-start.32 = (bf16[96,2048]{1,0:T(8,128)(2,1)S(1)}, bf16[96,2048]{1,0:T(8,128)(2,1)S(1)}, u32[]{:S(2)}, u32[]{:S(2)}) collective-permute-start(bf16[96,2048]{1,0:T(8,128)(2,1)S(1)} %get-tuple-element.140), channel_id=1, source_target_pairs={{0,3},{1,0},{2,1},{3,2},{4,7},{5,4},{6,5},{7,6},{8,11},{9,8},{10,9... | collective-permute-start | bytes 1179656 | tf_op jit(solution)/shard_map/ppermute | solution.py:707
  866.3 59.0 %collective-permute-start.31 = (bf16[96,2048]{1,0:T(8,128)(2,1)S(1)}, bf16[96,2048]{1,0:T(8,128)(2,1)S(1)}, u32[]{:S(2)}, u32[]{:S(2)}) collective-permute-start(bf16[96,2048]{1,0:T(8,128)(2,1)S(1)} %get-tuple-element.141), channel_id=1, source_target_pairs={{0,2},{1,3},{2,0},{3,1},{4,6},{5,7},{6,4},{7,5},{8,10},{9,11},{10,... | collective-permute-start | bytes 1179656 | tf_op jit(solution)/shard_map/ppermute | solution.py:707
  1027.9 418.4 %reduce-scatter.11.cloned.1.call-start = ((), (), s32[]{:S(2)}) async-start(), calls=%async_computation.14 | async-start | bytes 9437184 | tf_op jit(solution)/shard_map/reduce_scatter | solution.py:661
  1044.7 431.2 %reduce-scatter.5.cloned.1.call-start = ((), (), s32[]{:S(2)}) async-start(), calls=%async_computation.9 | async-start | bytes 12976128 | tf_op jit(solution)/shard_map/reduce_scatter | solution.py:661
  1045.3 436.8 %reduce-scatter.7.cloned.1.call-start = ((), (), s32[]{:S(2)}) async-start(), calls=%async_computation.12 | async-start | bytes 14155776 | tf_op jit(solution)/shard_map/reduce_scatter | solution.py:661
  1121.5 191.4 %collective-permute-start.49 = (bf16[4,256,2048]{2,1,0:T(8,128)(2,1)}, bf16[4,256,2048]{2,1,0:T(8,128)(2,1)}, u32[]{:S(2)}, u32[]{:S(2)}) collective-permute-start(bf16[4,256,2048]{2,1,0:T(8,128)(2,1)} %dynamic-slice_bitcast_fusion), channel_id=1, source_target_pairs={{0,4},{4,0},{8,12},{12,8},{16,20},{20,16},{24,28},{28,24},{1,5},{5... | collective-permute-start | bytes 12582920 | tf_op jit(solution)/shard_map/ppermute | solution.py:671
  1166.9 157.7 %collective-permute-start.45 = (bf16[4,256,2048]{2,1,0:T(8,128)(2,1)}, bf16[4,256,2048]{2,1,0:T(8,128)(2,1)}, u32[]{:S(2)}, u32[]{:S(2)}) collective-permute-start(bf16[4,256,2048]{2,1,0:T(8,128)(2,1)} %dynamic-slice_bitcast_fusion.1), channel_id=1, source_target_pairs={{0,4},{4,0},{8,12},{12,8},{16,20},{20,16},{24,28},{28,24},{1,5},{5... | collective-permute-start | bytes 12582920 | tf_op jit(solution)/shard_map/ppermute | solution.py:671
  1197.5 71.6 %collective-permute-start.34 = (bf16[320,1024]{1,0:T(8,128)(2,1)}, bf16[320,1024]{1,0:T(8,128)(2,1)}, u32[]{:S(2)}, u32[]{:S(2)}) collective-permute-start(bf16[320,1024]{1,0:T(8,128)(2,1)} %get-tuple-element.136), channel_id=1, source_target_pairs={{0,2},{1,3},{2,0},{3,1},{4,6},{5,7},{6,4},{7,5},{8,10},{9,11},{10,... | collective-permute-start | bytes 1966088 | tf_op jit(solution)/shard_map/ppermute | solution.py:650
  1224.3 64.4 %collective-permute-start.36 = (bf16[320,1024]{1,0:T(8,128)(2,1)}, bf16[320,1024]{1,0:T(8,128)(2,1)}, u32[]{:S(2)}, u32[]{:S(2)}) collective-permute-start(bf16[320,1024]{1,0:T(8,128)(2,1)} %get-tuple-element.137), channel_id=1, source_target_pairs={{0,1},{1,2},{2,3},{3,0},{4,5},{5,6},{6,7},{7,4},{8,9},{9,10},{10,1... | collective-permute-start | bytes 1966088 | tf_op jit(solution)/shard_map/ppermute | solution.py:650
  1224.8 63.9 %collective-permute-start.38 = (bf16[320,1024]{1,0:T(8,128)(2,1)}, bf16[320,1024]{1,0:T(8,128)(2,1)}, u32[]{:S(2)}, u32[]{:S(2)}) collective-permute-start(bf16[320,1024]{1,0:T(8,128)(2,1)} %get-tuple-element.138), channel_id=1, source_target_pairs={{0,3},{1,0},{2,1},{3,2},{4,7},{5,4},{6,5},{7,6},{8,11},{9,8},{10,9... | collective-permute-start | bytes 1966088 | tf_op jit(solution)/shard_map/ppermute | solution.py:650
  1321.4 61.6 %collective-permute-start.52 = (bf16[256,2048]{1,0:T(8,128)(2,1)}, bf16[256,2048]{1,0:T(8,128)(2,1)S(1)}, u32[]{:S(2)}, u32[]{:S(2)}) collective-permute-start(bf16[256,2048]{1,0:T(8,128)(2,1)} %get-tuple-element.113), channel_id=1, source_target_pairs={{0,24},{4,28},{8,0},{12,4},{16,8},{20,12},{24,16},{28,20},{1,25},{... | collective-permute-start | bytes 3145736 | tf_op jit(solution)/shard_map/ppermute | solution.py:677
  1324.6 58.7 %collective-permute-start.51 = (bf16[256,2048]{1,0:T(8,128)(2,1)}, bf16[256,2048]{1,0:T(8,128)(2,1)S(1)}, u32[]{:S(2)}, u32[]{:S(2)}) collective-permute-start(bf16[256,2048]{1,0:T(8,128)(2,1)} %get-tuple-element.114), channel_id=1, source_target_pairs={{0,16},{4,20},{8,24},{12,28},{16,0},{20,4},{24,8},{28,12},{1,17},{... | collective-permute-start | bytes 3145736 | tf_op jit(solution)/shard_map/ppermute | solution.py:677
  1333.2 83.7 %collective-permute-start.46 = (bf16[256,2048]{1,0:T(8,128)(2,1)}, bf16[256,2048]{1,0:T(8,128)(2,1)}, u32[]{:S(2)}, u32[]{:S(2)}) collective-permute-start(bf16[256,2048]{1,0:T(8,128)(2,1)} %get-tuple-element.115), channel_id=1, source_target_pairs={{0,8},{4,12},{8,16},{12,20},{16,24},{20,28},{24,0},{28,4},{1,9},{5... | collective-permute-start | bytes 3145736 | tf_op jit(solution)/shard_map/ppermute | solution.py:677
  1333.9 103.9 %collective-permute-start.48 = (bf16[256,2048]{1,0:T(8,128)(2,1)}, bf16[256,2048]{1,0:T(8,128)(2,1)}, u32[]{:S(2)}, u32[]{:S(2)}) collective-permute-start(bf16[256,2048]{1,0:T(8,128)(2,1)} %get-tuple-element.116), channel_id=1, source_target_pairs={{0,24},{4,28},{8,0},{12,4},{16,8},{20,12},{24,16},{28,20},{1,25},{... | collective-permute-start | bytes 3145736 | tf_op jit(solution)/shard_map/ppermute | solution.py:677
  1355.1 82.8 %collective-permute-start.47 = (bf16[256,2048]{1,0:T(8,128)(2,1)}, bf16[256,2048]{1,0:T(8,128)(2,1)}, u32[]{:S(2)}, u32[]{:S(2)}) collective-permute-start(bf16[256,2048]{1,0:T(8,128)(2,1)} %get-tuple-element.117), channel_id=1, source_target_pairs={{0,16},{4,20},{8,24},{12,28},{16,0},{20,4},{24,8},{28,12},{1,17},{... | collective-permute-start | bytes 3145736 | tf_op jit(solution)/shard_map/ppermute | solution.py:677
  1388.0 63.3 %collective-permute-start.39 = (bf16[64,2048]{1,0:T(8,128)(2,1)S(1)}, bf16[64,2048]{1,0:T(8,128)(2,1)}, u32[]{:S(2)}, u32[]{:S(2)}) collective-permute-start(bf16[64,2048]{1,0:T(8,128)(2,1)S(1)} %get-tuple-element.173), channel_id=1, source_target_pairs={{0,1},{1,2},{2,3},{3,0},{4,5},{5,6},{6,7},{7,4},{8,9},{9,10},{10,1... | collective-permute-start | bytes 786440 | tf_op jit(solution)/shard_map/ppermute | solution.py:650
  1389.5 62.4 %collective-permute-start.41 = (bf16[64,2048]{1,0:T(8,128)(2,1)S(1)}, bf16[64,2048]{1,0:T(8,128)(2,1)}, u32[]{:S(2)}, u32[]{:S(2)}) collective-permute-start(bf16[64,2048]{1,0:T(8,128)(2,1)S(1)} %get-tuple-element.174), channel_id=1, source_target_pairs={{0,3},{1,0},{2,1},{3,2},{4,7},{5,4},{6,5},{7,6},{8,11},{9,8},{10,9... | collective-permute-start | bytes 786440 | tf_op jit(solution)/shard_map/ppermute | solution.py:650
  (130 other events, 2688.5 us)
Sparse Core Ops, SparseCore 0:
  48.4 89.8 all-gather.9
  140.1 54.2 all-gather.19
  196.3 54.3 all-gather.21
  252.4 67.6 all-gather.13
  419.8 65.6 all-gather.11
  487.2 138.1 all-gather.17
  627.9 71.0 all-gather.15
  1028.0 69.3 reduce-scatter.8
  1100.9 71.5 reduce-scatter.10
  1175.8 87.1 reduce-scatter.4
  1266.4 161.1 reduce-scatter.6

commit v3 on v1

--- a/solution.py
+++ b/solution.py
@@ -13,7 +13,7 @@
 PROMPT = 1024
 CONTS = 2
 GROUP_TOK = 1280
-MLP_FIRST = 0.4
+MLP_FIRST = 0.5
 
 norm_eps = 1e-06
 rope_base = 10000.0
@@ -189,27 +189,11 @@
     )(query, kv_low, kv_low, place, cont, kcont)
 
 
-def attend_back_kernel(
-    spans,
-    q_ref,
-    k_ref,
-    v_ref,
-    g_ref,
-    lse_ref,
-    place_ref,
-    cont_ref,
-    kcont_ref,
-    qcos_ref,
-    qsin_ref,
-    kcos_ref,
-    ksin_ref,
-    dq_ref,
-    dk_ref,
-    dv_ref,
-    bias,
-    dk_sum,
-    dv_sum,
-):
+def attend_back_kernel(spans, *refs):
+    q_ref, k_ref, v_ref, g_ref, lse_ref, place_ref, cont_ref, kcont_ref = refs[:8]
+    qcos_ref, qsin_ref, kcos_ref, ksin_ref = refs[8:12]
+    dq_ref, dk_ref, dv_ref, bias, dk_sum, dv_sum = refs[12:]
+
     @pl.when(pl.program_id(0) == 0)
     def _():
         fill_bias(bias, place_ref, cont_ref, kcont_ref)
@@ -231,12 +215,12 @@
         dq_ref[s] = dq.astype(bf16)
         dk = dot_tn(grad_scores, query)
         dv = dot_tn(prob.astype(bf16), grad)
-        if s == last:
+        if s < last:
+            dk_sum[:span, :] += dk
+            dv_sum[:span, :] += dv
+        else:
             dk_sum[...] = dk
             dv_sum[...] = dv
-        else:
-            dk_sum[:span, :] += dk
-            dv_sum[:span, :] += dv
     dk = dk_sum[...] * scale
     dk_ref[...] = (dk * kcos_ref[...] - pltpu.roll(dk, HEAD // 2, 1) * ksin_ref[...]).astype(bf16)
     dv_ref[...] = dv_sum[...].astype(bf16)
@@ -633,6 +617,23 @@
     return lax.psum_scatter(terms, "dp", scatter_dimension=0, tiled=True)
 
 
+def chip_sum(terms, owners):
+    chips = owners // 2
+    place = lax.axis_index("dp")
+    chip, core = place // 2, place % 2
+    blocks = terms.reshape(chips, 2, -1, terms.shape[1])
+    mine = lax.dynamic_index_in_dim(blocks, core, 1, keepdims=False)
+    other = lax.dynamic_index_in_dim(blocks, 1 - core, 1, keepdims=False)
+    other = lax.ppermute(other, "dp", [(i, i + 1 - 2 * (i % 2)) for i in range(owners)])
+    mine = (mine.astype(f32) + other.astype(f32)).astype(bf16)
+    got = [lax.dynamic_index_in_dim(mine, chip, 0, keepdims=False)]
+    for hop in range(1, chips):
+        ring = [(i, (i // 2 + hop) % chips * 2 + i % 2) for i in range(owners)]
+        piece = lax.dynamic_index_in_dim(mine, (chip + hop) % chips, 0, keepdims=False)
+        got.append(lax.ppermute(piece, "dp", ring))
+    return sum(piece.astype(f32) for piece in got)
+
+
 def hops(rows, sign):
     count = rows.shape[0]
     pieces = [rows[0]]
@@ -803,18 +804,15 @@
 
     cot_slots = dot_nn(attn_pick_low, grad_resid.astype(bf16)).reshape(experts, slots, width)
     send_cot = (attn_slot_gate[:, :, None] * cot_slots).astype(bf16)
-    grad_mlp = [
-        g + dot_tn(k, r)
-        for g, k, r in zip(grad_mlp, kept[1], (plane_in[1], plane_in[1], plane_grad[1]))
-    ]
+    for j, rows in enumerate((plane_in[1], plane_in[1], plane_grad[1])):
+        grad_mlp[j] = grad_mlp[j] + dot_tn(kept[1][j], rows)
     grad_mlp_weight = jnp.stack(grad_mlp, axis=1)[:, None, :, :]
-    grad_result = after(exchange(send_cot), *grad_mlp).reshape(slot_total, width)
+    grad_result = after(exchange(send_cot), grad_mlp_weight).reshape(slot_total, width)
+    grad_attn = dot_nt(grad_result, output_full).astype(bf16)
     output_term = dot_tn(attn_flat, grad_result).astype(bf16)
-    grad_output_w = plane_sum(output_term)
-    grad_attn = dot_nt(after(grad_result, output_term), output_full).astype(bf16)
+    grad_output_w = chip_sum(output_term, owners)
     out_back = join([plane_sum(after(part, *in_parts)) for part in out_parts])
-    attend_again = attend_back
-    grad_query, grad_keys, grad_values = attend_again(
+    grad_query, grad_keys, grad_values = attend_back(
         query_low,
         kv_low,
         grad_attn.reshape(experts, slots, features),
@@ -837,9 +835,9 @@
 
     grad_keys_w = dot_tn(hidden_all, grad_keys).astype(bf16)
     grad_values_w = dot_tn(hidden_all, grad_values).astype(bf16)
-    grad_kv_w = jnp.concatenate([grad_keys_w, grad_values_w], axis=1)
     grad_query = hold(grad_query, grad_keys_w, grad_values_w)
-    grad_kv_w = plane_sum(grad_kv_w)
+    grad_kv_w = [plane_sum(grad_keys_w), plane_sum(grad_values_w)]
+
     grad_rows = dot_nt(grad_query, query_full).astype(bf16)
     half = width // 2
     grad_h, grad_first = [], []
@@ -861,15 +859,18 @@
             hop_sum(part.astype(bf16).reshape(experts, tok_dev, half), expert_id, experts)
         )
     query_term = dot_tn(query_rows, hold(grad_query, grad_h[1])).astype(bf16)
-    grad_query_w = plane_sum(query_term)
-    grad_output_w, grad_query_w = hold(grad_output_w, grad_kv_w), hold(grad_query_w, grad_kv_w)
-    grad_kv_w = hop_sum(grad_kv_w.reshape(experts, -1, 2 * features), expert_id, experts)
+    grad_query_w = chip_sum(query_term, owners)
+    grad_kv_w = jnp.concatenate(
+        [hop_sum(part.reshape(experts, -1, features), expert_id, experts) for part in grad_kv_w],
+        axis=1,
+    )
     grad_h = lax.optimization_barrier(tuple(grad_h))
     grad_gain_one = [
         jnp.sum(part * normed_all[:, low : low + half], axis=0)
         for part, low in zip(grad_h, (0, half))
     ]
     grad_gain_two = jnp.sum(grad_second * normed_two, axis=0)
+    first_sum = grad_first[0]
     grad_first = jnp.concatenate(grad_first, axis=1)
     normed_one, scale_one = rms_parts(own_f32)
     grad_input = grad_resid + rms_back(grad_first, normed_one, scale_one, gain_one)
@@ -882,7 +883,7 @@
         axis=1,
     )
     gain_rows = lax.all_to_all(
-        gain_rows[:, None, :], ("dp", "expert"), split_axis=0, concat_axis=0, tiled=True
+        hold(gain_rows, first_sum)[:, None, :], ("dp", "expert"), split_axis=0, concat_axis=0, tiled=True
     )
     gain_rows = jnp.sum(gain_rows, axis=(0, 1))
     grad_gain_attn, grad_gain_mlp = gain_rows[:part_size], gain_rows[part_size:]
@@ -892,8 +893,8 @@
         grad_gain_attn,
         grad_gain_mlp,
         grad_kv_w,
-        grad_query_w.astype(f32)[:, None, :],
-        grad_output_w.astype(f32)[:, None, :],
+        grad_query_w[:, None, :],
+        grad_output_w[:, None, :],
         grad_mlp_weight,
     )
 

time: 1410 us -> 1520 us (1.078); the launches traced: 1400 us -> 1500 us
  waiting for transfers between devices: 417 us -> 490 us
  matrix products: 243 us -> 227 us
    ppermute x0 -> x8, waiting for transfers between devices: none -> 89.2 us  [the longest x6 89.2 us: chip_sum(): got.append(lax.ppermute(piece, 'dp', ring))]
    ppermute x9 -> x12, waiting for transfers between devices: 73.7 us -> 134 us  [hop_sum(): got.append(lax.ppermute(piece, 'expert', ring))]
    all_gather x4, waiting for transfers between devices: 117 us -> 69.6 us  [to_plane(): return lax.all_gather(rows.reshape(-1, width), 'dp', axis=0, tiled=True)]
    ppermute x21, waiting for transfers between devices: 128 us -> 98.6 us  [hops(): pieces.append(lax.ppermute(rows[hop], 'expert', ring))]
    unnamed x155 -> x157, local copies, waits for them, and re-layouts: 41.1 us -> 36.8 us
  transfers between devices with their start and end apart: 46 -> 56, of which waited for: 22 -> 23; matrix products, arithmetic and copies ran while one was open for 27% -> 23% of each run, Pallas kernels for 23% -> 27%
where the time goes in v3:
time: 1520 us; the launch traced here: 1500 us
  Pallas kernels  502 us (33%)
  waiting for transfers between devices  490 us (32%)
  matrix products  227 us (15%)
  local copies, waits for them, and re-layouts  88.2 us (6%)
  starting transfers between devices  87.1 us (6%)
  other arithmetic  83.7 us (6%)
  between operations  19.7 us (1%)
    pallas_call x2, Pallas kernels, unit_block(): pl.pallas_call(unit_kernel, in_specs=[hbm, hbm, vmem, vmem, vmem], out_sp...  232 us
    dot_general x13, matrix products, dot_tn(): lax.dot_general(left, right, contract_first, preferred_element_type=f32)  137 us
    ppermute x12, waiting for transfers between devices, hop_sum(): got.append(lax.ppermute(piece, 'expert', ring))  134 us
    pallas_call x2, Pallas kernels, line_gather(): pl.pallas_call(line_kernel, in_specs=[hbm] * (1 + len(waits)), out_specs=...  132 us
    ppermute x21, waiting for transfers between devices, hops(): pieces.append(lax.ppermute(rows[hop], 'expert', ring))  98.6 us
    all_to_all x2, waiting for transfers between devices, exchange(): lax.all_to_all(rows, 'expert', split_axis=0, concat_axis=0, tiled=True)  96.1 us
    ppermute x6, waiting for transfers between devices, chip_sum(): got.append(lax.ppermute(piece, 'dp', ring))  89.2 us
    all_gather x4, waiting for transfers between devices, to_plane(): return lax.all_gather(rows.reshape(-1, width), 'dp', axis=0, tiled=True)  69.6 us
  transfers between devices with their start and end apart: 56, of which 23 were waited for; matrix products, arithmetic and copies ran while one was open for 23% of the time, Pallas kernels for 27%

profile of v3, /device:TPU:0, one launch (start us, length us, event | category | flops | bytes accessed | tf_op | source)
XLA Modules:
  0.0 1496.7 jit_solution(16397843877727616219)
XLA Ops:
  7.2 41.0 %line_gather.2 = bf16[4,64,4096]{2,1,0:T(8,128)(2,1)} custom-call(bf16[64,4096]{1,0:T(8,128)(2,1)} %own_ref.2), custom_call_target="tpu_custom_call" | custom-call | bytes 4194304 | tf_op jit(solution)/shard_map/line_gather/pallas_call | solution.py:573
  55.3 91.4 %line_gather.3 = bf16[4,320,2048]{2,1,0:T(8,128)(2,1)} custom-call(bf16[320,2048]{1,0:T(8,128)(2,1)} %own_ref.3, bf16[256,4096]{1,0:T(8,128)(2,1)} %bitcast.283), custom_call_target="tpu_custom_call" | custom-call | bytes 10485760 | tf_op jit(solution)/shard_map/line_gather/pallas_call | solution.py:573
  173.6 36.3 %shard_map.189.k_ref.v_ref.refs_1_.refs_2_ = bf16[1280,4096]{1,0:T(8,128)(2,1)} custom-call(bf16[1280,2048]{1,0:T(8,128)(2,1)} %get-tuple-element.107.x_ref, bf16[2048,4096]{1,0:T(8,128)(2,1)} %all-gather.10.cloned.1.call-done.w_ref, f32[1280,128]{1,0:T(8,128)} %get-tuple-element.190.cos_ref.refs_10_, f32[1280,128]{1,0:T(8,128)} %get-tuple-element.191.sin_ref.refs_11_), custom_call_target="tpu_custom_call" | custom-call | flops 21474836480 | bytes 32505856 | tf_op jit(solution)/shard_map/pallas_call | solution.py:110
  235.1 12.2 shard_map.188
  247.4 32.7 %attend.1 = (bf16[4,184,2048]{2,1,0:T(8,128)(2,1)}, f32[4,184,2048]{2,1,0:T(8,128)}) custom-call(bf16[4,184,2048]{2,1,0:T(8,128)(2,1)} %bitcast.303, bf16[1280,4096]{1,0:T(8,128)(2,1)} %shard_map.189.k_ref.v_ref.refs_1_.refs_2_, bf16[1280,4096]{1,0:T(8,128)(2,1)} %shard_map.189.k_ref.v_ref.refs_1_.refs_2_, s32[4,184,1]{2,1,0:T(8,128)} %select_add_fusion.place_ref.refs_5_, ...), custom_call_target="tpu_custom_call" | custom-call | flops 5016387584 | bytes 22544384 | tf_op jit(solution)/shard_map/attend/pallas_call | solution.py:166
  280.0 12.1 fusion.24
  299.9 64.9 %all-to-all-done.1 = bf16[4,184,2048]{2,1,0:T(8,128)(2,1)} async-done(((bf16[4,184,2048]{2,1,0:T(8,128)(2,1)}), bf16[4,184,2048]{2,1,0:T(8,128)(2,1)}, u32[]{:S(2)}, u32[]{:S(2)}) %all-to-all-start.1) | async-done | bytes 3014688 | tf_op jit(solution)/shard_map/all_to_all | solution.py:597
  386.1 19.7 %collective-permute-done.1 = bf16[88,2048]{1,0:T(8,128)(2,1)S(1)} collective-permute-done((bf16[88,2048]{1,0:T(8,128)(2,1)S(1)}, bf16[88,2048]{1,0:T(8,128)(2,1)S(1)}, u32[]{:S(2)}, u32[]{:S(2)}) %collective-permute-start.1) | collective-permute-done | bytes 360480 | tf_op jit(solution)/shard_map/ppermute | solution.py:642
  420.8 27.2 %collective-permute-done.7 = bf16[96,2048]{1,0:T(8,128)(2,1)S(1)} collective-permute-done((bf16[96,2048]{1,0:T(8,128)(2,1)S(1)}, bf16[96,2048]{1,0:T(8,128)(2,1)S(1)}, u32[]{:S(2)}, u32[]{:S(2)}) %collective-permute-start.7) | collective-permute-done | bytes 393248 | tf_op jit(solution)/shard_map/ppermute | solution.py:642
  459.0 17.0 %all-gather.12.cloned.1.call-done.x_hbm = bf16[2816,2048]{1,0:T(8,128)(2,1)} async-done(((bf16[352,2048]{1,0:T(8,128)(2,1)}), bf16[2816,2048]{1,0:T(8,128)(2,1)}) %all-gather.12.cloned.1.call-update) | async-done | bytes 11534352 | tf_op jit(solution)/shard_map/all_gather | solution.py:747
  475.9 117.6 %unit_block.2 = (bf16[352,2048]{1,0:T(8,128)(2,1)}, bf16[2816,2048]{1,0:T(8,128)(2,1)}, bf16[2816,704]{1,0:T(8,128)(2,1)}, bf16[2816,704]{1,0:T(8,128)(2,1)}, bf16[2816,704]{1,0:T(8,128)(2,1)}) custom-call(bf16[2816,2048]{1,0:T(8,128)(2,1)} %all-gather.12.cloned.1.call-done.x_hbm, bf16[2816,2048]{1,0:T(8,128)(2,1)} %all-gather.14.cloned.1.call-done.g_hbm, ...), custom_call_target="tpu_custom_call" | custom-call | flops 48721035264 | bytes 55148544 | tf_op jit(solution)/shard_map/unit_block/pallas_call | solution.py:438
  601.6 14.2 fusion.117
  636.9 52.6 %all-gather.16.cloned.1.call-done.x_hbm = bf16[3072,2048]{1,0:T(8,128)(2,1)} async-done(((bf16[384,2048]{1,0:T(8,128)(2,1)}), bf16[3072,2048]{1,0:T(8,128)(2,1)}) %all-gather.16.cloned.1.call-update) | async-done | bytes 12582928 | tf_op jit(solution)/shard_map/all_gather | solution.py:747
  689.5 114.7 %unit_block.3 = (bf16[384,2048]{1,0:T(8,128)(2,1)}, bf16[3072,2048]{1,0:T(8,128)(2,1)}, bf16[3072,704]{1,0:T(8,128)(2,1)}, bf16[3072,704]{1,0:T(8,128)(2,1)}, bf16[3072,704]{1,0:T(8,128)(2,1)}) custom-call(bf16[3072,2048]{1,0:T(8,128)(2,1)} %all-gather.16.cloned.1.call-done.x_hbm, bf16[3072,2048]{1,0:T(8,128)(2,1)} %all-gather.18.cloned.1.call-done.g_hbm, ...), custom_call_target="tpu_custom_call" | custom-call | flops 53150220288 | bytes 59375616 | tf_op jit(solution)/shard_map/unit_block/pallas_call | solution.py:438
  811.1 15.9 %add_bitcast_fusion = f32[704,1,2048]{2,0,1:T(8,128)} fusion(f32[704,2048]{1,0:T(8,128)} %fusion.117, bf16[3072,704]{1,0:T(8,128)(2,1)} %get-tuple-element.42, bf16[3072,2048]{1,0:T(8,128)(2,1)} %all-gather.18.cloned.1.call-done.g_hbm), kind=kOutput, calls=%fused_computation.22 | convolution fusion | flops 8859811840 | bytes 28442624 | tf_op jit(solution)/shard_map/dot_general | solution.py:72
  855.1 15.0 %add_bitcast_fusion.2 = f32[704,1,2048]{2,0,1:T(8,128)S(1)} fusion(f32[704,2048]{1,0:T(8,128)} %fusion.115, bf16[3072,704]{1,0:T(8,128)(2,1)} %get-tuple-element.40, bf16[3072,2048]{1,0:T(8,128)(2,1)} %all-gather.16.cloned.1.call-done.x_hbm), kind=kOutput, calls=%fused_computation.24 | convolution fusion | flops 8859811840 | bytes 28442624 | tf_op jit(solution)/shard_map/dot_general | solution.py:72
  870.1 14.5 add_bitcast_fusion.1
  891.0 31.3 %all-to-all-done.2 = bf16[4,184,2048]{2,1,0:T(8,128)(2,1)S(1)} async-done(((bf16[4,184,2048]{2,1,0:T(8,128)(2,1)}), bf16[4,184,2048]{2,1,0:T(8,128)(2,1)S(1)}, u32[]{:S(2)}, u32[]{:S(2)}) %all-to-all-start.2) | async-done | bytes 3014688 | tf_op jit(solution)/shard_map/all_to_all | solution.py:597
  932.2 55.7 %attend_back.1 = (bf16[4,184,2048]{2,1,0:T(8,128)(2,1)}, bf16[1280,2048]{1,0:T(8,128)(2,1)}, bf16[1280,2048]{1,0:T(8,128)(2,1)}) custom-call(bf16[4,184,2048]{2,1,0:T(8,128)(2,1)} %bitcast.304, bf16[1280,4096]{1,0:T(8,128)(2,1)} %shard_map.189.k_ref.v_ref.refs_1_.refs_2_, bf16[1280,4096]{1,0:T(8,128)(2,1)} %shard_map.189.k_ref.v_ref.refs_1_.refs_2_, ...), custom_call_target="tpu_custom_call" | custom-call | flops 12540968960 | bytes 36044800 | tf_op jit(solution)/shard_map/attend_back/pallas_call | solution.py:240
  987.9 16.7 %convolution_convert_fusion.1 = bf16[2048,2048]{1,0:T(8,128)(2,1)} fusion(bf16[1280,2048]{1,0:T(8,128)(2,1)} %get-tuple-element.107.x_ref, bf16[1280,2048]{1,0:T(8,128)(2,1)} %get-tuple-element.45), kind=kOutput, calls=%fused_computation.19 | convolution fusion | flops 10741612544 | bytes 18874368 | tf_op jit(solution)/shard_map/dot_general | solution.py:72
  1005.5 17.1 %convolution_convert_fusion = bf16[2048,2048]{1,0:T(8,128)(2,1)} fusion(bf16[1280,2048]{1,0:T(8,128)(2,1)} %get-tuple-element.107.x_ref, bf16[1280,2048]{1,0:T(8,128)(2,1)} %get-tuple-element.46), kind=kOutput, calls=%fused_computation.18 | convolution fusion | flops 10741612544 | bytes 18874368 | tf_op jit(solution)/shard_map/dot_general | solution.py:72
  1023.8 20.9 %copy.44 = f32[704,1,3,2048]{3,1,2,0:T(1,128)} copy(f32[704,1,3,2048]{3,0,2,1:T(8,128)} %maximum_bitcast_fusion) | data formatting | bytes 34603008
  1070.0 12.9 fusion.114
  1120.8 12.1 fusion.113
  1169.5 40.9 %collective-permute-done.22 = bf16[320,1024]{1,0:T(8,128)(2,1)} collective-permute-done((bf16[320,1024]{1,0:T(8,128)(2,1)}, bf16[320,1024]{1,0:T(8,128)(2,1)}, u32[]{:S(2)}, u32[]{:S(2)}) %collective-permute-start.22) | collective-permute-done | bytes 655392 | tf_op jit(solution)/shard_map/ppermute | solution.py:606
  1227.7 23.1 %collective-permute-done.25 = bf16[320,1024]{1,0:T(8,128)(2,1)} collective-permute-done((bf16[320,1024]{1,0:T(8,128)(2,1)S(1)}, bf16[320,1024]{1,0:T(8,128)(2,1)}, u32[]{:S(2)}, u32[]{:S(2)}) %collective-permute-start.25) | collective-permute-done | bytes 655392 | tf_op jit(solution)/shard_map/ppermute | solution.py:606
  1268.4 16.3 %collective-permute-done.36 = bf16[256,2048]{1,0:T(8,128)(2,1)} collective-permute-done((bf16[256,2048]{1,0:T(8,128)(2,1)}, bf16[256,2048]{1,0:T(8,128)(2,1)}, u32[]{:S(2)}, u32[]{:S(2)}) %collective-permute-start.36) | collective-permute-done | bytes 1048608 | tf_op jit(solution)/shard_map/ppermute | solution.py:633
  1291.3 38.1 %collective-permute-done.38 = bf16[256,2048]{1,0:T(8,128)(2,1)} collective-permute-done((bf16[256,2048]{1,0:T(8,128)(2,1)}, bf16[256,2048]{1,0:T(8,128)(2,1)}, u32[]{:S(2)}, u32[]{:S(2)}) %collective-permute-start.38) | collective-permute-done | bytes 1048608 | tf_op jit(solution)/shard_map/ppermute | solution.py:633
  1329.4 33.7 %collective-permute-done.40 = bf16[256,2048]{1,0:T(8,128)(2,1)} collective-permute-done((bf16[256,2048]{1,0:T(8,128)(2,1)}, bf16[256,2048]{1,0:T(8,128)(2,1)}, u32[]{:S(2)}, u32[]{:S(2)}) %collective-permute-start.40) | collective-permute-done | bytes 1048608 | tf_op jit(solution)/shard_map/ppermute | solution.py:633
  1391.3 28.7 %collective-permute-done.28 = bf16[64,2048]{1,0:T(8,128)(2,1)} collective-permute-done((bf16[64,2048]{1,0:T(8,128)(2,1)S(1)}, bf16[64,2048]{1,0:T(8,128)(2,1)}, u32[]{:S(2)}, u32[]{:S(2)}) %collective-permute-start.28) | collective-permute-done | bytes 262176 | tf_op jit(solution)/shard_map/ppermute | solution.py:606
  1421.4 21.8 %collective-permute-done.31 = bf16[64,2048]{1,0:T(8,128)(2,1)S(1)} collective-permute-done((bf16[64,2048]{1,0:T(8,128)(2,1)S(1)}, bf16[64,2048]{1,0:T(8,128)(2,1)S(1)}, u32[]{:S(2)}, u32[]{:S(2)}) %collective-permute-start.31) | collective-permute-done | bytes 262176 | tf_op jit(solution)/shard_map/ppermute | solution.py:606
  1466.1 15.2 %collective-permute-done.13 = bf16[96,2048]{1,0:T(8,128)(2,1)S(1)} collective-permute-done((bf16[96,2048]{1,0:T(8,128)(2,1)S(1)}, bf16[96,2048]{1,0:T(8,128)(2,1)S(1)}, u32[]{:S(2)}, u32[]{:S(2)}) %collective-permute-start.13) | collective-permute-done | bytes 393248 | tf_op jit(solution)/shard_map/ppermute | solution.py:642
  (401 shorter events, 393.4 us)
Async XLA Ops:
  7.2 166.4 %all-gather.10.cloned.1.call-start = ((), (), s32[]{:S(2)}) async-start(), calls=%async_computation.8 | async-start | bytes 18874368 | tf_op jit(solution)/shard_map/all_gather | solution.py:680
  48.2 186.9 %all-gather.20.cloned.1.call-start = ((), (), s32[]{:S(2)}) async-start(), calls=%async_computation.17 | async-start | bytes 9437184 | tf_op jit(solution)/shard_map/all_gather | solution.py:682
  49.0 231.0 %all-gather.22.cloned.1.call-start = ((), (), s32[]{:S(2)}) async-start(), calls=%async_computation.18 | async-start | bytes 9437184 | tf_op jit(solution)/shard_map/all_gather | solution.py:683
  50.4 112.8 %all-to-all-start = ((bf16[32,1,128]{2,1,0:T(2,128)(2,1)}), bf16[32,1,128]{2,1,0:T(2,128)(2,1)S(1)}, u32[]{:S(2)}, u32[]{:S(2)}) async-start(bf16[32,1,128]{2,1,0:T(2,128)(2,1)} %broadcast_in_dim.143), calls=%async_computation | async-start | bytes 32768 | tf_op jit(solution)/shard_map/all_to_all | solution.py:648
  55.2 403.8 %all-gather.14.cloned.1.call-start = ((), (), s32[]{:S(2)}) async-start(), calls=%async_computation.10 | async-start | bytes 12976128 | tf_op jit(solution)/shard_map/all_gather | solution.py:747
  152.4 59.4 %collective-permute-start.5 = (bf16[184,2048]{1,0:T(8,128)(2,1)}, bf16[184,2048]{1,0:T(8,128)(2,1)S(1)}, u32[]{:S(2)}, u32[]{:S(2)}) collective-permute-start(bf16[184,2048]{1,0:T(8,128)(2,1)} %get-tuple-element.121), channel_id=1, source_target_pairs={{0,3},{1,0},{2,1},{3,2},{4,7},{5,4},{6,5},{7,6},{8,11},{9,8},{10,9... | collective-permute-start | bytes 2261000 | tf_op jit(solution)/shard_map/ppermute | solution.py:642
  154.7 62.4 %collective-permute-start.4 = (bf16[184,2048]{1,0:T(8,128)(2,1)}, bf16[184,2048]{1,0:T(8,128)(2,1)S(1)}, u32[]{:S(2)}, u32[]{:S(2)}) collective-permute-start(bf16[184,2048]{1,0:T(8,128)(2,1)} %get-tuple-element.122), channel_id=1, source_target_pairs={{0,2},{1,3},{2,0},{3,1},{4,6},{5,7},{6,4},{7,5},{8,10},{9,11},{10,... | collective-permute-start | bytes 2261000 | tf_op jit(solution)/shard_map/ppermute | solution.py:642
  154.7 62.4 %collective-permute-start.3 = (bf16[184,2048]{1,0:T(8,128)(2,1)S(1)}, bf16[184,2048]{1,0:T(8,128)(2,1)S(1)}, u32[]{:S(2)}, u32[]{:S(2)}) collective-permute-start(bf16[184,2048]{1,0:T(8,128)(2,1)S(1)} %get-tuple-element.123), channel_id=1, source_target_pairs={{0,1},{1,2},{2,3},{3,0},{4,5},{5,6},{6,7},{7,4},{8,9},{9,10},{10,1... | collective-permute-start | bytes 2261000 | tf_op jit(solution)/shard_map/ppermute | solution.py:642
  292.1 72.7 %all-to-all-start.1 = ((bf16[4,184,2048]{2,1,0:T(8,128)(2,1)}), bf16[4,184,2048]{2,1,0:T(8,128)(2,1)}, u32[]{:S(2)}, u32[]{:S(2)}) async-start(bf16[4,184,2048]{2,1,0:T(8,128)(2,1)} %bitcast.299), calls=%async_computation.1 | async-start | bytes 6029312 | tf_op jit(solution)/shard_map/all_to_all | solution.py:597
  296.9 179.1 %all-gather.12.cloned.1.call-start = ((), (), s32[]{:S(2)}) async-start(), calls=%async_computation.9 | async-start | bytes 12976128 | tf_op jit(solution)/shard_map/all_gather | solution.py:747
  407.1 229.8 %all-gather.18.cloned.1.call-start = ((), (), s32[]{:S(2)}) async-start(), calls=%async_computation.12 | async-start | bytes 14155776 | tf_op jit(solution)/shard_map/all_gather | solution.py:747
  408.4 281.1 %all-gather.16.cloned.1.call-start = ((), (), s32[]{:S(2)}) async-start(), calls=%async_computation.11 | async-start | bytes 14155776 | tf_op jit(solution)/shard_map/all_gather | solution.py:747
  596.3 213.3 %collective-permute-start.17 = (bf16[88,2048]{1,0:T(8,128)(2,1)}, bf16[88,2048]{1,0:T(8,128)(2,1)}, u32[]{:S(2)}, u32[]{:S(2)}) collective-permute-start(bf16[88,2048]{1,0:T(8,128)(2,1)} %get-tuple-element.145), channel_id=1, source_target_pairs={{0,1},{1,2},{2,3},{3,0},{4,5},{5,6},{6,7},{7,4},{8,9},{9,10},{10,1... | collective-permute-start | bytes 1081352 | tf_op jit(solution)/shard_map/ppermute | solution.py:642
  597.8 229.2 %collective-permute-start.16 = (bf16[88,2048]{1,0:T(8,128)(2,1)}, bf16[88,2048]{1,0:T(8,128)(2,1)}, u32[]{:S(2)}, u32[]{:S(2)}) collective-permute-start(bf16[88,2048]{1,0:T(8,128)(2,1)} %get-tuple-element.146), channel_id=1, source_target_pairs={{0,2},{1,3},{2,0},{3,1},{4,6},{5,7},{6,4},{7,5},{8,10},{9,11},{10,... | collective-permute-start | bytes 1081352 | tf_op jit(solution)/shard_map/ppermute | solution.py:642
  600.2 226.8 %collective-permute-start.15 = (bf16[88,2048]{1,0:T(8,128)(2,1)}, bf16[88,2048]{1,0:T(8,128)(2,1)}, u32[]{:S(2)}, u32[]{:S(2)}) collective-permute-start(bf16[88,2048]{1,0:T(8,128)(2,1)} %get-tuple-element.147), channel_id=1, source_target_pairs={{0,3},{1,0},{2,1},{3,2},{4,7},{5,4},{6,5},{7,6},{8,11},{9,8},{10,9... | collective-permute-start | bytes 1081352 | tf_op jit(solution)/shard_map/ppermute | solution.py:642
  844.0 78.2 %all-to-all-start.2 = ((bf16[4,184,2048]{2,1,0:T(8,128)(2,1)}), bf16[4,184,2048]{2,1,0:T(8,128)(2,1)S(1)}, u32[]{:S(2)}, u32[]{:S(2)}) async-start(bf16[4,184,2048]{2,1,0:T(8,128)(2,1)} %multiply_convert_fusion.1), calls=%async_computation.4 | async-start | bytes 6029312 | tf_op jit(solution)/shard_map/all_to_all | solution.py:597
  855.1 513.7 %reduce-scatter.9.cloned.1.call-start = ((), (), s32[]{:S(2)}) async-start(), calls=%async_computation.15 | async-start | bytes 9437184 | tf_op jit(solution)/shard_map/reduce_scatter | solution.py:617
  1004.7 370.4 %reduce-scatter.5.cloned.1.call-start = ((), (), s32[]{:S(2)}) async-start(), calls=%async_computation.13 | async-start | bytes 12976128 | tf_op jit(solution)/shard_map/reduce_scatter | solution.py:617
  1005.4 374.3 %reduce-scatter.11.cloned.1.call-start = ((), (), s32[]{:S(2)}) async-start(), calls=%async_computation.16 | async-start | bytes 9437184 | tf_op jit(solution)/shard_map/reduce_scatter | solution.py:617
  1022.6 422.6 %reduce-scatter.7.cloned.1.call-start = ((), (), s32[]{:S(2)}) async-start(), calls=%async_computation.14 | async-start | bytes 14155776 | tf_op jit(solution)/shard_map/reduce_scatter | solution.py:617
  1098.2 119.5 %collective-permute-start.33 = (bf16[4,256,2048]{2,1,0:T(8,128)(2,1)}, bf16[4,256,2048]{2,1,0:T(8,128)(2,1)}, u32[]{:S(2)}, u32[]{:S(2)}) collective-permute-start(bf16[4,256,2048]{2,1,0:T(8,128)(2,1)} %dynamic-slice_bitcast_fusion.1), channel_id=1, source_target_pairs={{0,4},{4,0},{8,12},{12,8},{16,20},{20,16},{24,28},{28,24},{1,5},{5... | collective-permute-start | bytes 12582920 | tf_op jit(solution)/shard_map/ppermute | solution.py:627
  1110.2 142.9 %collective-permute-start.37 = (bf16[4,256,2048]{2,1,0:T(8,128)(2,1)}, bf16[4,256,2048]{2,1,0:T(8,128)(2,1)}, u32[]{:S(2)}, u32[]{:S(2)}) collective-permute-start(bf16[4,256,2048]{2,1,0:T(8,128)(2,1)} %dynamic-slice_bitcast_fusion), channel_id=1, source_target_pairs={{0,4},{4,0},{8,12},{12,8},{16,20},{20,16},{24,28},{28,24},{1,5},{5... | collective-permute-start | bytes 12582920 | tf_op jit(solution)/shard_map/ppermute | solution.py:627
  1138.2 72.2 %collective-permute-start.22 = (bf16[320,1024]{1,0:T(8,128)(2,1)}, bf16[320,1024]{1,0:T(8,128)(2,1)}, u32[]{:S(2)}, u32[]{:S(2)}) collective-permute-start(bf16[320,1024]{1,0:T(8,128)(2,1)} %get-tuple-element.132), channel_id=1, source_target_pairs={{0,2},{1,3},{2,0},{3,1},{4,6},{5,7},{6,4},{7,5},{8,10},{9,11},{10,... | collective-permute-start | bytes 1966088 | tf_op jit(solution)/shard_map/ppermute | solution.py:606
  1154.1 73.6 %collective-permute-start.24 = (bf16[320,1024]{1,0:T(8,128)(2,1)}, bf16[320,1024]{1,0:T(8,128)(2,1)S(1)}, u32[]{:S(2)}, u32[]{:S(2)}) collective-permute-start(bf16[320,1024]{1,0:T(8,128)(2,1)} %get-tuple-element.133), channel_id=1, source_target_pairs={{0,1},{1,2},{2,3},{3,0},{4,5},{5,6},{6,7},{7,4},{8,9},{9,10},{10,1... | collective-permute-start | bytes 1966088 | tf_op jit(solution)/shard_map/ppermute | solution.py:606
  1165.2 62.5 %collective-permute-start.26 = (bf16[320,1024]{1,0:T(8,128)(2,1)}, bf16[320,1024]{1,0:T(8,128)(2,1)S(1)}, u32[]{:S(2)}, u32[]{:S(2)}) collective-permute-start(bf16[320,1024]{1,0:T(8,128)(2,1)} %get-tuple-element.134), channel_id=1, source_target_pairs={{0,3},{1,0},{2,1},{3,2},{4,7},{5,4},{6,5},{7,6},{8,11},{9,8},{10,9... | collective-permute-start | bytes 1966088 | tf_op jit(solution)/shard_map/ppermute | solution.py:606
  1214.4 53.3 %all-to-all-start.3 = ((f32[32,1,128]{2,1,0:T(1,128)}), f32[32,1,128]{2,1,0:T(1,128)S(1)}, u32[]{:S(2)}, u32[]{:S(2)}) async-start(f32[32,1,128]{2,1,0:T(1,128)} %maximum_add_fusion.1), calls=%async_computation.5 | async-start | bytes 32768 | tf_op jit(solution)/shard_map/all_to_all | solution.py:885
  1262.3 67.2 %collective-permute-start.38 = (bf16[256,2048]{1,0:T(8,128)(2,1)}, bf16[256,2048]{1,0:T(8,128)(2,1)}, u32[]{:S(2)}, u32[]{:S(2)}) collective-permute-start(bf16[256,2048]{1,0:T(8,128)(2,1)} %get-tuple-element.108), channel_id=1, source_target_pairs={{0,8},{4,12},{8,16},{12,20},{16,24},{20,28},{24,0},{28,4},{1,9},{5... | collective-permute-start | bytes 3145736 | tf_op jit(solution)/shard_map/ppermute | solution.py:633
  1264.2 99.0 %collective-permute-start.40 = (bf16[256,2048]{1,0:T(8,128)(2,1)}, bf16[256,2048]{1,0:T(8,128)(2,1)}, u32[]{:S(2)}, u32[]{:S(2)}) collective-permute-start(bf16[256,2048]{1,0:T(8,128)(2,1)} %get-tuple-element.109), channel_id=1, source_target_pairs={{0,24},{4,28},{8,0},{12,4},{16,8},{20,12},{24,16},{28,20},{1,25},{... | collective-permute-start | bytes 3145736 | tf_op jit(solution)/shard_map/ppermute | solution.py:633
  1265.4 97.8 %collective-permute-start.39 = (bf16[256,2048]{1,0:T(8,128)(2,1)}, bf16[256,2048]{1,0:T(8,128)(2,1)}, u32[]{:S(2)}, u32[]{:S(2)}) collective-permute-start(bf16[256,2048]{1,0:T(8,128)(2,1)} %get-tuple-element.110), channel_id=1, source_target_pairs={{0,16},{4,20},{8,24},{12,28},{16,0},{20,4},{24,8},{28,12},{1,17},{... | collective-permute-start | bytes 3145736 | tf_op jit(solution)/shard_map/ppermute | solution.py:633
  1374.5 45.5 %collective-permute-start.28 = (bf16[64,2048]{1,0:T(8,128)(2,1)S(1)}, bf16[64,2048]{1,0:T(8,128)(2,1)}, u32[]{:S(2)}, u32[]{:S(2)}) collective-permute-start(bf16[64,2048]{1,0:T(8,128)(2,1)S(1)} %get-tuple-element.155), channel_id=1, source_target_pairs={{0,2},{1,3},{2,0},{3,1},{4,6},{5,7},{6,4},{7,5},{8,10},{9,11},{10,... | collective-permute-start | bytes 786440 | tf_op jit(solution)/shard_map/ppermute | solution.py:606
  1377.4 79.2 %collective-permute-start.11 = (bf16[88,2048]{1,0:T(8,128)(2,1)}, bf16[88,2048]{1,0:T(8,128)(2,1)}, u32[]{:S(2)}, u32[]{:S(2)}) collective-permute-start(bf16[88,2048]{1,0:T(8,128)(2,1)} %get-tuple-element.149), channel_id=1, source_target_pairs={{0,1},{1,2},{2,3},{3,0},{4,5},{5,6},{6,7},{7,4},{8,9},{9,10},{10,1... | collective-permute-start | bytes 1081352 | tf_op jit(solution)/shard_map/ppermute | solution.py:642
  1378.9 78.7 %collective-permute-start.10 = (bf16[88,2048]{1,0:T(8,128)(2,1)}, bf16[88,2048]{1,0:T(8,128)(2,1)}, u32[]{:S(2)}, u32[]{:S(2)}) collective-permute-start(bf16[88,2048]{1,0:T(8,128)(2,1)} %get-tuple-element.150), channel_id=1, source_target_pairs={{0,2},{1,3},{2,0},{3,1},{4,6},{5,7},{6,4},{7,5},{8,10},{9,11},{10,... | collective-permute-start | bytes 1081352 | tf_op jit(solution)/shard_map/ppermute | solution.py:642
  (102 other events, 2052.2 us)
Sparse Core Ops, SparseCore 0:
  48.4 89.8 all-gather.9
  140.1 54.2 all-gather.19
  196.4 54.2 all-gather.21
  252.4 67.5 all-gather.13
  407.2 68.7 all-gather.11
  478.3 137.5 all-gather.17
  618.3 71.0 all-gather.15
  1004.8 69.6 reduce-scatter.8
  1078.0 88.0 reduce-scatter.4
  1169.4 81.1 reduce-scatter.10
  1254.1 147.7 reduce-scatter.6

commit v4 on v3

--- a/solution.py
+++ b/solution.py
@@ -293,12 +293,14 @@
     precv,
     ssend,
     frecv,
+    relay,
     load_sem,
     store_sem,
     psend_sem,
     precv_sem,
     ssend_sem,
     frecv_sem,
+    relay_sem,
 ):
     rows = xbuf.shape[1]
     chips = ssend.shape[0]
@@ -307,18 +309,28 @@
     core = me % 2
     partner = me + 1 - 2 * core
 
-    def peer(hop):
-        return {"dp": (chip + hop) % chips * 2 + core}
-
+    square = chips == 4
+    fold = rows // 32 * 16
+    parts = (pl.ds(0, fold), pl.ds(fold, rows - fold))
+    incoming = 2 if square else chips - 1
+
+    def target(j):
+        if not square:
+            return (chip + chips - 1 - j) % chips
+        return (chip // 2 + 1 - j % 2) % 2 * 2 + (chip % 2 + 1 - j // 2) % 2
+
+    def peer(j):
+        return {"dp": target(j) * 2 + core}
+
+    meets = (1, 2) if square else range(chips - 1)
     barrier = pltpu.get_barrier_semaphore()
     pl.semaphore_signal(barrier, inc=1, device_id={"dp": partner}, device_id_type=MESH)
-    for hop in range(1, chips):
-        pl.semaphore_signal(barrier, inc=1, device_id=peer(hop), device_id_type=MESH)
-    pl.semaphore_wait(barrier, chips)
+    for j in meets:
+        pl.semaphore_signal(barrier, inc=1, device_id=peer(j), device_id_type=MESH)
+    pl.semaphore_wait(barrier, 1 + incoming)
 
     def block_rows(j, own):
-        dest = (chip + chips - 1 - j) % chips
-        block = dest * 2 + (core if own else 1 - core)
+        block = target(j) * 2 + (core if own else 1 - core)
         return pl.ds(pl.multiple_of(block * rows, 8), rows)
 
     def loads(j, own):
@@ -348,10 +360,20 @@
     def to_owner(j):
         return pltpu.make_async_remote_copy(
             src_ref=ssend.at[j],
-            dst_ref=frecv.at[j],
+            dst_ref=frecv.at[j - 1 if square else j],
             send_sem=ssend_sem.at[j],
             recv_sem=frecv_sem.at[j],
-            device_id=peer(chips - 1 - j),
+            device_id=peer(j),
+            device_id_type=MESH,
+        )
+
+    def to_relay(part):
+        return pltpu.make_async_remote_copy(
+            src_ref=ssend.at[0, parts[part]],
+            dst_ref=relay.at[parts[part]],
+            send_sem=relay_sem.at[0, part],
+            recv_sem=relay_sem.at[1, part],
+            device_id=peer(1 + part),
             device_id_type=MESH,
         )
 
@@ -405,8 +427,24 @@
         term = compute(j, True)
         to_partner(j).wait_recv()
         ssend[j] = (term + precv[j].astype(f32)).astype(bf16)
-
-        @pl.when(j < chips - 1)
+        if square:
+
+            @pl.when(j == 0)
+            def _():
+                for part in (0, 1):
+                    to_relay(part).start()
+
+            for part in (0, 1):
+
+                @pl.when(j == 2 - part)
+                def _():
+                    to_relay(part).wait_recv()
+                    span = parts[part]
+                    ssend[j, span] = (
+                        ssend[j, span].astype(f32) + relay[span].astype(f32)
+                    ).astype(bf16)
+
+        @pl.when((j < chips - 1) & (j > 0) if square else j < chips - 1)
         def _():
             to_owner(j).start()
 
@@ -414,12 +452,15 @@
 
     lax.fori_loop(0, chips, step, 0)
     total = ssend[chips - 1].astype(f32)
-    for j in range(chips - 1):
+    for slot, j in enumerate(meets):
         to_owner(j).wait_recv()
-        total = total + frecv[j].astype(f32)
+        total = total + frecv[slot].astype(f32)
     in_ref[...] = total.astype(bf16)
-    for j in range(chips - 1):
+    for j in meets:
         to_owner(j).wait_send()
+    if square:
+        for part in (0, 1):
+            to_relay(part).wait_send()
     for j in range(max(chips - 2, 0), chips):
         to_partner(j).wait_send()
     for own in (False, True):
@@ -454,13 +495,15 @@
             pltpu.VMEM((2, rows, width), bf16),
             pltpu.VMEM((chips, rows, width), bf16),
             pltpu.VMEM((chips, rows, width), bf16),
-            pltpu.VMEM((chips - 1, rows, width), bf16),
+            pltpu.VMEM((2 if chips == 4 else chips - 1, rows, width), bf16),
+            pltpu.VMEM((rows if chips == 4 else 16, width), bf16),
             pltpu.SemaphoreType.DMA((2, 2)),
             pltpu.SemaphoreType.DMA((4, 2)),
             pltpu.SemaphoreType.DMA((2,)),
             pltpu.SemaphoreType.DMA((chips,)),
             pltpu.SemaphoreType.DMA((chips,)),
             pltpu.SemaphoreType.DMA((chips,)),
+            pltpu.SemaphoreType.DMA((2, 2)),
         ],
         compiler_params=pltpu.CompilerParams(
             collective_id=number, has_side_effects=True, vmem_limit_bytes=67043328

time: 1520 us -> 1480 us (0.974)
  waiting for transfers between devices: 490 us -> 463 us
  Pallas kernels: 502 us -> 480 us
    all_gather x4, waiting for transfers between devices: 69.6 us -> 45.6 us  [to_plane(): return lax.all_gather(rows.reshape(-1, width), 'dp', axis=0, tiled=True)]
    pallas_call x2, Pallas kernels: 232 us -> 211 us  [unit_block(): pl.pallas_call(unit_kernel, in_specs=[hbm, hbm, vmem, vmem, vmem], out_sp...]
  transfers between devices with their start and end apart: 56 -> 56, of which waited for: 23 -> 23; matrix products, arithmetic and copies ran while one was open for 23% -> 24% of each run, Pallas kernels for 27% -> 26%
where the time goes in v4:
time: 1480 us; the launch traced here: 1450 us
  Pallas kernels  480 us (32%)
  waiting for transfers between devices  463 us (31%)
  matrix products  227 us (15%)
  local copies, waits for them, and re-layouts  89.3 us (6%)
  starting transfers between devices  88.5 us (6%)
  other arithmetic  83.8 us (6%)
  between operations  19.7 us (1%)
    pallas_call x2, Pallas kernels, unit_block(): pl.pallas_call(unit_kernel, in_specs=[hbm, hbm, vmem, vmem, vmem], out_sp...  211 us
    dot_general x13, matrix products, dot_tn(): lax.dot_general(left, right, contract_first, preferred_element_type=f32)  138 us
    ppermute x12, waiting for transfers between devices, hop_sum(): got.append(lax.ppermute(piece, 'expert', ring))  133 us
    pallas_call x2, Pallas kernels, line_gather(): pl.pallas_call(line_kernel, in_specs=[hbm] * (1 + len(waits)), out_specs=...  132 us
    ppermute x21, waiting for transfers between devices, hops(): pieces.append(lax.ppermute(rows[hop], 'expert', ring))  98.1 us
    all_to_all x2, waiting for transfers between devices, exchange(): lax.all_to_all(rows, 'expert', split_axis=0, concat_axis=0, tiled=True)  96.1 us
    ppermute x6, waiting for transfers between devices, chip_sum(): got.append(lax.ppermute(piece, 'dp', ring))  87.6 us
    dot_general x6, matrix products, dot_nt(): lax.dot_general(left, right, contract_last, preferred_element_type=f32)  61.5 us
  transfers between devices with their start and end apart: 56, of which 23 were waited for; matrix products, arithmetic and copies ran while one was open for 24% of the time, Pallas kernels for 26%

profile of v4, /device:TPU:0, one launch (start us, length us, event | category | flops | bytes accessed | tf_op | source)
XLA Modules:
  0.0 1451.7 jit_solution(8812117726460150986)
XLA Ops:
  7.2 41.0 %line_gather.2 = bf16[4,64,4096]{2,1,0:T(8,128)(2,1)} custom-call(bf16[64,4096]{1,0:T(8,128)(2,1)} %own_ref.2), custom_call_target="tpu_custom_call" | custom-call | bytes 4194304 | tf_op jit(solution)/shard_map/line_gather/pallas_call | solution.py:616
  55.3 91.4 %line_gather.3 = bf16[4,320,2048]{2,1,0:T(8,128)(2,1)} custom-call(bf16[320,2048]{1,0:T(8,128)(2,1)} %own_ref.3, bf16[256,4096]{1,0:T(8,128)(2,1)} %bitcast.283), custom_call_target="tpu_custom_call" | custom-call | bytes 10485760 | tf_op jit(solution)/shard_map/line_gather/pallas_call | solution.py:616
  173.6 36.3 %shard_map.189.k_ref.v_ref.refs_1_.refs_2_ = bf16[1280,4096]{1,0:T(8,128)(2,1)} custom-call(bf16[1280,2048]{1,0:T(8,128)(2,1)} %get-tuple-element.107.x_ref, bf16[2048,4096]{1,0:T(8,128)(2,1)} %all-gather.10.cloned.1.call-done.w_ref, f32[1280,128]{1,0:T(8,128)} %get-tuple-element.190.cos_ref.refs_10_, f32[1280,128]{1,0:T(8,128)} %get-tuple-element.191.sin_ref.refs_11_), custom_call_target="tpu_custom_call" | custom-call | flops 21474836480 | bytes 32505856 | tf_op jit(solution)/shard_map/pallas_call | solution.py:110
  235.1 12.2 shard_map.188
  247.4 32.7 %attend.1 = (bf16[4,184,2048]{2,1,0:T(8,128)(2,1)}, f32[4,184,2048]{2,1,0:T(8,128)}) custom-call(bf16[4,184,2048]{2,1,0:T(8,128)(2,1)} %bitcast.303, bf16[1280,4096]{1,0:T(8,128)(2,1)} %shard_map.189.k_ref.v_ref.refs_1_.refs_2_, bf16[1280,4096]{1,0:T(8,128)(2,1)} %shard_map.189.k_ref.v_ref.refs_1_.refs_2_, s32[4,184,1]{2,1,0:T(8,128)} %select_add_fusion.place_ref.refs_5_, ...), custom_call_target="tpu_custom_call" | custom-call | flops 5016387584 | bytes 22544384 | tf_op jit(solution)/shard_map/attend/pallas_call | solution.py:166
  280.0 12.1 fusion.24
  299.9 64.9 %all-to-all-done.1 = bf16[4,184,2048]{2,1,0:T(8,128)(2,1)} async-done(((bf16[4,184,2048]{2,1,0:T(8,128)(2,1)}), bf16[4,184,2048]{2,1,0:T(8,128)(2,1)}, u32[]{:S(2)}, u32[]{:S(2)}) %all-to-all-start.1) | async-done | bytes 3014688 | tf_op jit(solution)/shard_map/all_to_all | solution.py:640
  386.1 19.7 %collective-permute-done.1 = bf16[88,2048]{1,0:T(8,128)(2,1)S(1)} collective-permute-done((bf16[88,2048]{1,0:T(8,128)(2,1)S(1)}, bf16[88,2048]{1,0:T(8,128)(2,1)S(1)}, u32[]{:S(2)}, u32[]{:S(2)}) %collective-permute-start.1) | collective-permute-done | bytes 360480 | tf_op jit(solution)/shard_map/ppermute | solution.py:685
  420.8 27.2 %collective-permute-done.7 = bf16[96,2048]{1,0:T(8,128)(2,1)S(1)} collective-permute-done((bf16[96,2048]{1,0:T(8,128)(2,1)S(1)}, bf16[96,2048]{1,0:T(8,128)(2,1)S(1)}, u32[]{:S(2)}, u32[]{:S(2)}) %collective-permute-start.7) | collective-permute-done | bytes 393248 | tf_op jit(solution)/shard_map/ppermute | solution.py:685
  459.0 17.0 %all-gather.12.cloned.1.call-done.x_hbm = bf16[2816,2048]{1,0:T(8,128)(2,1)} async-done(((bf16[352,2048]{1,0:T(8,128)(2,1)}), bf16[2816,2048]{1,0:T(8,128)(2,1)}) %all-gather.12.cloned.1.call-update) | async-done | bytes 11534352 | tf_op jit(solution)/shard_map/all_gather | solution.py:790
  475.9 112.5 %unit_block.2 = (bf16[352,2048]{1,0:T(8,128)(2,1)}, bf16[2816,2048]{1,0:T(8,128)(2,1)}, bf16[2816,704]{1,0:T(8,128)(2,1)}, bf16[2816,704]{1,0:T(8,128)(2,1)}, bf16[2816,704]{1,0:T(8,128)(2,1)}) custom-call(bf16[2816,2048]{1,0:T(8,128)(2,1)} %all-gather.12.cloned.1.call-done.x_hbm, bf16[2816,2048]{1,0:T(8,128)(2,1)} %all-gather.14.cloned.1.call-done.g_hbm, ...), custom_call_target="tpu_custom_call" | custom-call | flops 48721035264 | bytes 55148544 | tf_op jit(solution)/shard_map/unit_block/pallas_call | solution.py:479
  596.5 15.2 %fusion.117 = f32[704,2048]{1,0:T(8,128)} fusion(bf16[2816,704]{1,0:T(8,128)(2,1)} %get-tuple-element.38, bf16[2816,2048]{1,0:T(8,128)(2,1)} %all-gather.14.cloned.1.call-done.g_hbm), kind=kOutput, calls=%fused_computation.255 | convolution fusion | flops 8120172544 | bytes 21266432 | tf_op jit(solution)/shard_map/dot_general | solution.py:72
  632.7 28.6 %all-gather.16.cloned.1.call-done.x_hbm = bf16[3072,2048]{1,0:T(8,128)(2,1)} async-done(((bf16[384,2048]{1,0:T(8,128)(2,1)}), bf16[3072,2048]{1,0:T(8,128)(2,1)}) %all-gather.16.cloned.1.call-update) | async-done | bytes 12582928 | tf_op jit(solution)/shard_map/all_gather | solution.py:790
  661.3 98.6 %unit_block.3 = (bf16[384,2048]{1,0:T(8,128)(2,1)}, bf16[3072,2048]{1,0:T(8,128)(2,1)}, bf16[3072,704]{1,0:T(8,128)(2,1)}, bf16[3072,704]{1,0:T(8,128)(2,1)}, bf16[3072,704]{1,0:T(8,128)(2,1)}) custom-call(bf16[3072,2048]{1,0:T(8,128)(2,1)} %all-gather.16.cloned.1.call-done.x_hbm, bf16[3072,2048]{1,0:T(8,128)(2,1)} %all-gather.18.cloned.1.call-done.g_hbm, ...), custom_call_target="tpu_custom_call" | custom-call | flops 53150220288 | bytes 59375616 | tf_op jit(solution)/shard_map/unit_block/pallas_call | solution.py:479
  766.7 15.9 %add_bitcast_fusion = f32[704,1,2048]{2,0,1:T(8,128)} fusion(f32[704,2048]{1,0:T(8,128)} %fusion.117, bf16[3072,704]{1,0:T(8,128)(2,1)} %get-tuple-element.42, bf16[3072,2048]{1,0:T(8,128)(2,1)} %all-gather.18.cloned.1.call-done.g_hbm), kind=kOutput, calls=%fused_computation.22 | convolution fusion | flops 8859811840 | bytes 28442624 | tf_op jit(solution)/shard_map/dot_general | solution.py:72
  810.2 15.0 %add_bitcast_fusion.2 = f32[704,1,2048]{2,0,1:T(8,128)S(1)} fusion(f32[704,2048]{1,0:T(8,128)} %fusion.115, bf16[3072,704]{1,0:T(8,128)(2,1)} %get-tuple-element.40, bf16[3072,2048]{1,0:T(8,128)(2,1)} %all-gather.16.cloned.1.call-done.x_hbm), kind=kOutput, calls=%fused_computation.24 | convolution fusion | flops 8859811840 | bytes 28442624 | tf_op jit(solution)/shard_map/dot_general | solution.py:72
  825.2 14.5 add_bitcast_fusion.1
  846.1 31.3 %all-to-all-done.2 = bf16[4,184,2048]{2,1,0:T(8,128)(2,1)S(1)} async-done(((bf16[4,184,2048]{2,1,0:T(8,128)(2,1)}), bf16[4,184,2048]{2,1,0:T(8,128)(2,1)S(1)}, u32[]{:S(2)}, u32[]{:S(2)}) %all-to-all-start.2) | async-done | bytes 3014688 | tf_op jit(solution)/shard_map/all_to_all | solution.py:640
  887.3 55.7 %attend_back.1 = (bf16[4,184,2048]{2,1,0:T(8,128)(2,1)}, bf16[1280,2048]{1,0:T(8,128)(2,1)}, bf16[1280,2048]{1,0:T(8,128)(2,1)}) custom-call(bf16[4,184,2048]{2,1,0:T(8,128)(2,1)} %bitcast.304, bf16[1280,4096]{1,0:T(8,128)(2,1)} %shard_map.189.k_ref.v_ref.refs_1_.refs_2_, bf16[1280,4096]{1,0:T(8,128)(2,1)} %shard_map.189.k_ref.v_ref.refs_1_.refs_2_, ...), custom_call_target="tpu_custom_call" | custom-call | flops 12540968960 | bytes 36044800 | tf_op jit(solution)/shard_map/attend_back/pallas_call | solution.py:240
  943.0 16.7 %convolution_convert_fusion.1 = bf16[2048,2048]{1,0:T(8,128)(2,1)} fusion(bf16[1280,2048]{1,0:T(8,128)(2,1)} %get-tuple-element.107.x_ref, bf16[1280,2048]{1,0:T(8,128)(2,1)} %get-tuple-element.45), kind=kOutput, calls=%fused_computation.19 | convolution fusion | flops 10741612544 | bytes 18874368 | tf_op jit(solution)/shard_map/dot_general | solution.py:72
  960.6 16.7 %convolution_convert_fusion = bf16[2048,2048]{1,0:T(8,128)(2,1)} fusion(bf16[1280,2048]{1,0:T(8,128)(2,1)} %get-tuple-element.107.x_ref, bf16[1280,2048]{1,0:T(8,128)(2,1)} %get-tuple-element.46), kind=kOutput, calls=%fused_computation.18 | convolution fusion | flops 10741612544 | bytes 18874368 | tf_op jit(solution)/shard_map/dot_general | solution.py:72
  978.6 20.9 %copy.44 = f32[704,1,3,2048]{3,1,2,0:T(1,128)} copy(f32[704,1,3,2048]{3,0,2,1:T(8,128)} %maximum_bitcast_fusion) | data formatting | bytes 34603008
  1024.8 12.9 fusion.114
  1075.8 12.1 fusion.113
  1124.2 41.1 %collective-permute-done.22 = bf16[320,1024]{1,0:T(8,128)(2,1)} collective-permute-done((bf16[320,1024]{1,0:T(8,128)(2,1)}, bf16[320,1024]{1,0:T(8,128)(2,1)}, u32[]{:S(2)}, u32[]{:S(2)}) %collective-permute-start.22) | collective-permute-done | bytes 655392 | tf_op jit(solution)/shard_map/ppermute | solution.py:649
  1183.7 22.1 %collective-permute-done.25 = bf16[320,1024]{1,0:T(8,128)(2,1)} collective-permute-done((bf16[320,1024]{1,0:T(8,128)(2,1)S(1)}, bf16[320,1024]{1,0:T(8,128)(2,1)}, u32[]{:S(2)}, u32[]{:S(2)}) %collective-permute-start.25) | collective-permute-done | bytes 655392 | tf_op jit(solution)/shard_map/ppermute | solution.py:649
  1225.0 14.8 %collective-permute-done.36 = bf16[256,2048]{1,0:T(8,128)(2,1)} collective-permute-done((bf16[256,2048]{1,0:T(8,128)(2,1)}, bf16[256,2048]{1,0:T(8,128)(2,1)}, u32[]{:S(2)}, u32[]{:S(2)}) %collective-permute-start.36) | collective-permute-done | bytes 1048608 | tf_op jit(solution)/shard_map/ppermute | solution.py:676
  1247.4 38.0 %collective-permute-done.38 = bf16[256,2048]{1,0:T(8,128)(2,1)} collective-permute-done((bf16[256,2048]{1,0:T(8,128)(2,1)}, bf16[256,2048]{1,0:T(8,128)(2,1)}, u32[]{:S(2)}, u32[]{:S(2)}) %collective-permute-start.38) | collective-permute-done | bytes 1048608 | tf_op jit(solution)/shard_map/ppermute | solution.py:676
  1285.4 32.8 %collective-permute-done.40 = bf16[256,2048]{1,0:T(8,128)(2,1)} collective-permute-done((bf16[256,2048]{1,0:T(8,128)(2,1)}, bf16[256,2048]{1,0:T(8,128)(2,1)}, u32[]{:S(2)}, u32[]{:S(2)}) %collective-permute-start.40) | collective-permute-done | bytes 1048608 | tf_op jit(solution)/shard_map/ppermute | solution.py:676
  1346.4 28.7 %collective-permute-done.28 = bf16[64,2048]{1,0:T(8,128)(2,1)} collective-permute-done((bf16[64,2048]{1,0:T(8,128)(2,1)S(1)}, bf16[64,2048]{1,0:T(8,128)(2,1)}, u32[]{:S(2)}, u32[]{:S(2)}) %collective-permute-start.28) | collective-permute-done | bytes 262176 | tf_op jit(solution)/shard_map/ppermute | solution.py:649
  1376.4 21.9 %collective-permute-done.31 = bf16[64,2048]{1,0:T(8,128)(2,1)S(1)} collective-permute-done((bf16[64,2048]{1,0:T(8,128)(2,1)S(1)}, bf16[64,2048]{1,0:T(8,128)(2,1)S(1)}, u32[]{:S(2)}, u32[]{:S(2)}) %collective-permute-start.31) | collective-permute-done | bytes 262176 | tf_op jit(solution)/shard_map/ppermute | solution.py:649
  1421.1 15.2 %collective-permute-done.13 = bf16[96,2048]{1,0:T(8,128)(2,1)S(1)} collective-permute-done((bf16[96,2048]{1,0:T(8,128)(2,1)S(1)}, bf16[96,2048]{1,0:T(8,128)(2,1)S(1)}, u32[]{:S(2)}, u32[]{:S(2)}) %collective-permute-start.13) | collective-permute-done | bytes 393248 | tf_op jit(solution)/shard_map/ppermute | solution.py:685
  (401 shorter events, 396.5 us)
Async XLA Ops:
  7.2 166.4 %all-gather.10.cloned.1.call-start = ((), (), s32[]{:S(2)}) async-start(), calls=%async_computation.8 | async-start | bytes 18874368 | tf_op jit(solution)/shard_map/all_gather | solution.py:723
  48.2 186.9 %all-gather.20.cloned.1.call-start = ((), (), s32[]{:S(2)}) async-start(), calls=%async_computation.17 | async-start | bytes 9437184 | tf_op jit(solution)/shard_map/all_gather | solution.py:725
  49.0 231.0 %all-gather.22.cloned.1.call-start = ((), (), s32[]{:S(2)}) async-start(), calls=%async_computation.18 | async-start | bytes 9437184 | tf_op jit(solution)/shard_map/all_gather | solution.py:726
  50.4 112.8 %all-to-all-start = ((bf16[32,1,128]{2,1,0:T(2,128)(2,1)}), bf16[32,1,128]{2,1,0:T(2,128)(2,1)S(1)}, u32[]{:S(2)}, u32[]{:S(2)}) async-start(bf16[32,1,128]{2,1,0:T(2,128)(2,1)} %broadcast_in_dim.143), calls=%async_computation | async-start | bytes 32768 | tf_op jit(solution)/shard_map/all_to_all | solution.py:691
  55.2 403.8 %all-gather.14.cloned.1.call-start = ((), (), s32[]{:S(2)}) async-start(), calls=%async_computation.10 | async-start | bytes 12976128 | tf_op jit(solution)/shard_map/all_gather | solution.py:790
  152.4 59.4 %collective-permute-start.5 = (bf16[184,2048]{1,0:T(8,128)(2,1)}, bf16[184,2048]{1,0:T(8,128)(2,1)S(1)}, u32[]{:S(2)}, u32[]{:S(2)}) collective-permute-start(bf16[184,2048]{1,0:T(8,128)(2,1)} %get-tuple-element.121), channel_id=1, source_target_pairs={{0,3},{1,0},{2,1},{3,2},{4,7},{5,4},{6,5},{7,6},{8,11},{9,8},{10,9... | collective-permute-start | bytes 2261000 | tf_op jit(solution)/shard_map/ppermute | solution.py:685
  154.7 62.4 %collective-permute-start.4 = (bf16[184,2048]{1,0:T(8,128)(2,1)}, bf16[184,2048]{1,0:T(8,128)(2,1)S(1)}, u32[]{:S(2)}, u32[]{:S(2)}) collective-permute-start(bf16[184,2048]{1,0:T(8,128)(2,1)} %get-tuple-element.122), channel_id=1, source_target_pairs={{0,2},{1,3},{2,0},{3,1},{4,6},{5,7},{6,4},{7,5},{8,10},{9,11},{10,... | collective-permute-start | bytes 2261000 | tf_op jit(solution)/shard_map/ppermute | solution.py:685
  154.7 62.4 %collective-permute-start.3 = (bf16[184,2048]{1,0:T(8,128)(2,1)S(1)}, bf16[184,2048]{1,0:T(8,128)(2,1)S(1)}, u32[]{:S(2)}, u32[]{:S(2)}) collective-permute-start(bf16[184,2048]{1,0:T(8,128)(2,1)S(1)} %get-tuple-element.123), channel_id=1, source_target_pairs={{0,1},{1,2},{2,3},{3,0},{4,5},{5,6},{6,7},{7,4},{8,9},{9,10},{10,1... | collective-permute-start | bytes 2261000 | tf_op jit(solution)/shard_map/ppermute | solution.py:685
  292.1 72.7 %all-to-all-start.1 = ((bf16[4,184,2048]{2,1,0:T(8,128)(2,1)}), bf16[4,184,2048]{2,1,0:T(8,128)(2,1)}, u32[]{:S(2)}, u32[]{:S(2)}) async-start(bf16[4,184,2048]{2,1,0:T(8,128)(2,1)} %bitcast.299), calls=%async_computation.1 | async-start | bytes 6029312 | tf_op jit(solution)/shard_map/all_to_all | solution.py:640
  296.9 179.1 %all-gather.12.cloned.1.call-start = ((), (), s32[]{:S(2)}) async-start(), calls=%async_computation.9 | async-start | bytes 12976128 | tf_op jit(solution)/shard_map/all_gather | solution.py:790
  407.1 225.6 %all-gather.18.cloned.1.call-start = ((), (), s32[]{:S(2)}) async-start(), calls=%async_computation.12 | async-start | bytes 14155776 | tf_op jit(solution)/shard_map/all_gather | solution.py:790
  408.4 252.9 %all-gather.16.cloned.1.call-start = ((), (), s32[]{:S(2)}) async-start(), calls=%async_computation.11 | async-start | bytes 14155776 | tf_op jit(solution)/shard_map/all_gather | solution.py:790
  591.1 174.2 %collective-permute-start.17 = (bf16[88,2048]{1,0:T(8,128)(2,1)}, bf16[88,2048]{1,0:T(8,128)(2,1)}, u32[]{:S(2)}, u32[]{:S(2)}) collective-permute-start(bf16[88,2048]{1,0:T(8,128)(2,1)} %get-tuple-element.145), channel_id=1, source_target_pairs={{0,1},{1,2},{2,3},{3,0},{4,5},{5,6},{6,7},{7,4},{8,9},{9,10},{10,1... | collective-permute-start | bytes 1081352 | tf_op jit(solution)/shard_map/ppermute | solution.py:685
  592.6 190.1 %collective-permute-start.16 = (bf16[88,2048]{1,0:T(8,128)(2,1)}, bf16[88,2048]{1,0:T(8,128)(2,1)}, u32[]{:S(2)}, u32[]{:S(2)}) collective-permute-start(bf16[88,2048]{1,0:T(8,128)(2,1)} %get-tuple-element.146), channel_id=1, source_target_pairs={{0,2},{1,3},{2,0},{3,1},{4,6},{5,7},{6,4},{7,5},{8,10},{9,11},{10,... | collective-permute-start | bytes 1081352 | tf_op jit(solution)/shard_map/ppermute | solution.py:685
  595.0 187.7 %collective-permute-start.15 = (bf16[88,2048]{1,0:T(8,128)(2,1)}, bf16[88,2048]{1,0:T(8,128)(2,1)}, u32[]{:S(2)}, u32[]{:S(2)}) collective-permute-start(bf16[88,2048]{1,0:T(8,128)(2,1)} %get-tuple-element.147), channel_id=1, source_target_pairs={{0,3},{1,0},{2,1},{3,2},{4,7},{5,4},{6,5},{7,6},{8,11},{9,8},{10,9... | collective-permute-start | bytes 1081352 | tf_op jit(solution)/shard_map/ppermute | solution.py:685
  799.1 78.2 %all-to-all-start.2 = ((bf16[4,184,2048]{2,1,0:T(8,128)(2,1)}), bf16[4,184,2048]{2,1,0:T(8,128)(2,1)S(1)}, u32[]{:S(2)}, u32[]{:S(2)}) async-start(bf16[4,184,2048]{2,1,0:T(8,128)(2,1)} %multiply_convert_fusion.1), calls=%async_computation.4 | async-start | bytes 6029312 | tf_op jit(solution)/shard_map/all_to_all | solution.py:640
  810.2 513.6 %reduce-scatter.9.cloned.1.call-start = ((), (), s32[]{:S(2)}) async-start(), calls=%async_computation.15 | async-start | bytes 9437184 | tf_op jit(solution)/shard_map/reduce_scatter | solution.py:660
  959.8 370.3 %reduce-scatter.5.cloned.1.call-start = ((), (), s32[]{:S(2)}) async-start(), calls=%async_computation.13 | async-start | bytes 12976128 | tf_op jit(solution)/shard_map/reduce_scatter | solution.py:660
  960.5 374.2 %reduce-scatter.11.cloned.1.call-start = ((), (), s32[]{:S(2)}) async-start(), calls=%async_computation.16 | async-start | bytes 9437184 | tf_op jit(solution)/shard_map/reduce_scatter | solution.py:660
  977.3 422.9 %reduce-scatter.7.cloned.1.call-start = ((), (), s32[]{:S(2)}) async-start(), calls=%async_computation.14 | async-start | bytes 14155776 | tf_op jit(solution)/shard_map/reduce_scatter | solution.py:660
  1053.2 120.5 %collective-permute-start.33 = (bf16[4,256,2048]{2,1,0:T(8,128)(2,1)}, bf16[4,256,2048]{2,1,0:T(8,128)(2,1)}, u32[]{:S(2)}, u32[]{:S(2)}) collective-permute-start(bf16[4,256,2048]{2,1,0:T(8,128)(2,1)} %dynamic-slice_bitcast_fusion.1), channel_id=1, source_target_pairs={{0,4},{4,0},{8,12},{12,8},{16,20},{20,16},{24,28},{28,24},{1,5},{5... | collective-permute-start | bytes 12582920 | tf_op jit(solution)/shard_map/ppermute | solution.py:670
  1065.2 145.3 %collective-permute-start.37 = (bf16[4,256,2048]{2,1,0:T(8,128)(2,1)}, bf16[4,256,2048]{2,1,0:T(8,128)(2,1)}, u32[]{:S(2)}, u32[]{:S(2)}) collective-permute-start(bf16[4,256,2048]{2,1,0:T(8,128)(2,1)} %dynamic-slice_bitcast_fusion), channel_id=1, source_target_pairs={{0,4},{4,0},{8,12},{12,8},{16,20},{20,16},{24,28},{28,24},{1,5},{5... | collective-permute-start | bytes 12582920 | tf_op jit(solution)/shard_map/ppermute | solution.py:670
  1093.1 72.2 %collective-permute-start.22 = (bf16[320,1024]{1,0:T(8,128)(2,1)}, bf16[320,1024]{1,0:T(8,128)(2,1)}, u32[]{:S(2)}, u32[]{:S(2)}) collective-permute-start(bf16[320,1024]{1,0:T(8,128)(2,1)} %get-tuple-element.132), channel_id=1, source_target_pairs={{0,2},{1,3},{2,0},{3,1},{4,6},{5,7},{6,4},{7,5},{8,10},{9,11},{10,... | collective-permute-start | bytes 1966088 | tf_op jit(solution)/shard_map/ppermute | solution.py:649
  1109.0 74.7 %collective-permute-start.24 = (bf16[320,1024]{1,0:T(8,128)(2,1)}, bf16[320,1024]{1,0:T(8,128)(2,1)S(1)}, u32[]{:S(2)}, u32[]{:S(2)}) collective-permute-start(bf16[320,1024]{1,0:T(8,128)(2,1)} %get-tuple-element.133), channel_id=1, source_target_pairs={{0,1},{1,2},{2,3},{3,0},{4,5},{5,6},{6,7},{7,4},{8,9},{9,10},{10,1... | collective-permute-start | bytes 1966088 | tf_op jit(solution)/shard_map/ppermute | solution.py:649
  1120.2 63.5 %collective-permute-start.26 = (bf16[320,1024]{1,0:T(8,128)(2,1)}, bf16[320,1024]{1,0:T(8,128)(2,1)S(1)}, u32[]{:S(2)}, u32[]{:S(2)}) collective-permute-start(bf16[320,1024]{1,0:T(8,128)(2,1)} %get-tuple-element.134), channel_id=1, source_target_pairs={{0,3},{1,0},{2,1},{3,2},{4,7},{5,4},{6,5},{7,6},{8,11},{9,8},{10,9... | collective-permute-start | bytes 1966088 | tf_op jit(solution)/shard_map/ppermute | solution.py:649
  1169.4 55.0 %all-to-all-start.3 = ((f32[32,1,128]{2,1,0:T(1,128)}), f32[32,1,128]{2,1,0:T(1,128)S(1)}, u32[]{:S(2)}, u32[]{:S(2)}) async-start(f32[32,1,128]{2,1,0:T(1,128)} %maximum_add_fusion.1), calls=%async_computation.5 | async-start | bytes 32768 | tf_op jit(solution)/shard_map/all_to_all | solution.py:928
  1220.2 65.2 %collective-permute-start.38 = (bf16[256,2048]{1,0:T(8,128)(2,1)}, bf16[256,2048]{1,0:T(8,128)(2,1)}, u32[]{:S(2)}, u32[]{:S(2)}) collective-permute-start(bf16[256,2048]{1,0:T(8,128)(2,1)} %get-tuple-element.108), channel_id=1, source_target_pairs={{0,8},{4,12},{8,16},{12,20},{16,24},{20,28},{24,0},{28,4},{1,9},{5... | collective-permute-start | bytes 3145736 | tf_op jit(solution)/shard_map/ppermute | solution.py:676
  1220.2 98.0 %collective-permute-start.40 = (bf16[256,2048]{1,0:T(8,128)(2,1)}, bf16[256,2048]{1,0:T(8,128)(2,1)}, u32[]{:S(2)}, u32[]{:S(2)}) collective-permute-start(bf16[256,2048]{1,0:T(8,128)(2,1)} %get-tuple-element.109), channel_id=1, source_target_pairs={{0,24},{4,28},{8,0},{12,4},{16,8},{20,12},{24,16},{28,20},{1,25},{... | collective-permute-start | bytes 3145736 | tf_op jit(solution)/shard_map/ppermute | solution.py:676
  1223.4 94.8 %collective-permute-start.39 = (bf16[256,2048]{1,0:T(8,128)(2,1)}, bf16[256,2048]{1,0:T(8,128)(2,1)}, u32[]{:S(2)}, u32[]{:S(2)}) collective-permute-start(bf16[256,2048]{1,0:T(8,128)(2,1)} %get-tuple-element.110), channel_id=1, source_target_pairs={{0,16},{4,20},{8,24},{12,28},{16,0},{20,4},{24,8},{28,12},{1,17},{... | collective-permute-start | bytes 3145736 | tf_op jit(solution)/shard_map/ppermute | solution.py:676
  1329.5 45.5 %collective-permute-start.28 = (bf16[64,2048]{1,0:T(8,128)(2,1)S(1)}, bf16[64,2048]{1,0:T(8,128)(2,1)}, u32[]{:S(2)}, u32[]{:S(2)}) collective-permute-start(bf16[64,2048]{1,0:T(8,128)(2,1)S(1)} %get-tuple-element.155), channel_id=1, source_target_pairs={{0,2},{1,3},{2,0},{3,1},{4,6},{5,7},{6,4},{7,5},{8,10},{9,11},{10,... | collective-permute-start | bytes 786440 | tf_op jit(solution)/shard_map/ppermute | solution.py:649
  1332.4 79.2 %collective-permute-start.11 = (bf16[88,2048]{1,0:T(8,128)(2,1)}, bf16[88,2048]{1,0:T(8,128)(2,1)}, u32[]{:S(2)}, u32[]{:S(2)}) collective-permute-start(bf16[88,2048]{1,0:T(8,128)(2,1)} %get-tuple-element.149), channel_id=1, source_target_pairs={{0,1},{1,2},{2,3},{3,0},{4,5},{5,6},{6,7},{7,4},{8,9},{9,10},{10,1... | collective-permute-start | bytes 1081352 | tf_op jit(solution)/shard_map/ppermute | solution.py:685
  1333.9 78.8 %collective-permute-start.10 = (bf16[88,2048]{1,0:T(8,128)(2,1)}, bf16[88,2048]{1,0:T(8,128)(2,1)}, u32[]{:S(2)}, u32[]{:S(2)}) collective-permute-start(bf16[88,2048]{1,0:T(8,128)(2,1)} %get-tuple-element.150), channel_id=1, source_target_pairs={{0,2},{1,3},{2,0},{3,1},{4,6},{5,7},{6,4},{7,5},{8,10},{9,11},{10,... | collective-permute-start | bytes 1081352 | tf_op jit(solution)/shard_map/ppermute | solution.py:685
  (102 other events, 2057.1 us)
Sparse Core Ops, SparseCore 0:
  48.4 89.8 all-gather.9
  140.1 54.2 all-gather.19
  196.4 54.2 all-gather.21
  252.4 67.5 all-gather.13
  407.2 68.7 all-gather.11
  478.3 107.5 all-gather.17
  588.3 72.9 all-gather.15
  959.9 70.5 reduce-scatter.8
  1034.0 87.0 reduce-scatter.4
  1124.4 80.0 reduce-scatter.10
  1208.0 148.8 reduce-scatter.6

commit v5 on v4

--- a/solution.py
+++ b/solution.py
@@ -13,7 +13,7 @@
 PROMPT = 1024
 CONTS = 2
 GROUP_TOK = 1280
-MLP_FIRST = 0.5
+MLP_CUTS = (0.27, 0.61)
 
 norm_eps = 1e-06
 rope_base = 10000.0
@@ -783,7 +783,7 @@
     cot_rows = dot_nn(mlp_pick_low, cotangent).reshape(experts, slots, width)
     send_grad = (mlp_slot_gate[:, :, None] * cot_rows).astype(bf16)
     steps = slots // 8
-    cuts = [0, 8 * max(int(steps * MLP_FIRST), 1), slots]
+    cuts = [0] + [8 * int(steps * cut) for cut in MLP_CUTS] + [slots]
     pieces = list(zip(cuts[:-1], cuts[1:]))
 
     def to_plane(rows):
@@ -823,7 +823,10 @@
 
     send_in = dot_nn(mlp_pick_low, second_low).astype(bf16).reshape(experts, slots, width)
     gate_rows, up_rows, down_rows = (mlp_weight[:, 0, j, :] for j in range(3))
-    plane_in = [to_plane(hops(send_in[:, low:high, :], 1)) for low, high in pieces]
+    plane_in = []
+    for low, high in pieces:
+        got_in = hops(send_in[:, low:high, :], 1)
+        plane_in.append(to_plane(got_in))
     kept, out_parts, in_parts = [], [], []
     for number, (rows_in, rows_grad) in enumerate(zip(plane_in, plane_grad)):
         in_part, out_part, *keep = unit_block(
@@ -840,15 +843,18 @@
         return jnp.concatenate(back, axis=1).reshape(slot_total, width)
 
     in_back = join(in_parts)
-    grad_mlp = [dot_tn(k, r) for k, r in zip(kept[0], (plane_in[0], plane_in[0], plane_grad[0]))]
-    grad_second = dot_tn(mlp_pick_low, after(in_back, *grad_mlp))
+    grad_mlp = []
+    for j, rows in enumerate((plane_in[0], plane_in[0], plane_grad[0])):
+        grad_mlp.append(dot_tn(kept[0][j], rows))
+    grad_second = dot_tn(mlp_pick_low, in_back)
     cot_f32 = cotangent.astype(f32)
     grad_resid = cot_f32 + rms_back(grad_second, normed_two, scale_two, gain_two)
 
     cot_slots = dot_nn(attn_pick_low, grad_resid.astype(bf16)).reshape(experts, slots, width)
     send_cot = (attn_slot_gate[:, :, None] * cot_slots).astype(bf16)
-    for j, rows in enumerate((plane_in[1], plane_in[1], plane_grad[1])):
-        grad_mlp[j] = grad_mlp[j] + dot_tn(kept[1][j], rows)
+    for number in range(1, len(pieces)):
+        for j, rows in enumerate((plane_in, plane_in, plane_grad)):
+            grad_mlp[j] = grad_mlp[j] + dot_tn(kept[number][j], rows[number])
     grad_mlp_weight = jnp.stack(grad_mlp, axis=1)[:, None, :, :]
     grad_result = after(exchange(send_cot), grad_mlp_weight).reshape(slot_total, width)
     grad_attn = dot_nt(grad_result, output_full).astype(bf16)
@@ -879,7 +885,7 @@
     grad_keys_w = dot_tn(hidden_all, grad_keys).astype(bf16)
     grad_values_w = dot_tn(hidden_all, grad_values).astype(bf16)
     grad_query = hold(grad_query, grad_keys_w, grad_values_w)
-    grad_kv_w = [plane_sum(grad_keys_w), plane_sum(grad_values_w)]
+    kv_sums = [plane_sum(grad_keys_w), plane_sum(grad_values_w)]
 
     grad_rows = dot_nt(grad_query, query_full).astype(bf16)
     half = width // 2
@@ -904,7 +910,7 @@
     query_term = dot_tn(query_rows, hold(grad_query, grad_h[1])).astype(bf16)
     grad_query_w = chip_sum(query_term, owners)
     grad_kv_w = jnp.concatenate(
-        [hop_sum(part.reshape(experts, -1, features), expert_id, experts) for part in grad_kv_w],
+        [hop_sum(part.reshape(experts, -1, features), expert_id, experts) for part in kv_sums],
         axis=1,
     )
     grad_h = lax.optimization_barrier(tuple(grad_h))
@@ -913,7 +919,6 @@
         for part, low in zip(grad_h, (0, half))
     ]
     grad_gain_two = jnp.sum(grad_second * normed_two, axis=0)
-    first_sum = grad_first[0]
     grad_first = jnp.concatenate(grad_first, axis=1)
     normed_one, scale_one = rms_parts(own_f32)
     grad_input = grad_resid + rms_back(grad_first, normed_one, scale_one, gain_one)
@@ -926,7 +931,7 @@
         axis=1,
     )
     gain_rows = lax.all_to_all(
-        hold(gain_rows, first_sum)[:, None, :], ("dp", "expert"), split_axis=0, concat_axis=0, tiled=True
+        hold(gain_rows, kv_sums[1])[:, None, :], ("dp", "expert"), split_axis=0, concat_axis=0, tiled=True
     )
     gain_rows = jnp.sum(gain_rows, axis=(0, 1))
     grad_gain_attn, grad_gain_mlp = gain_rows[:part_size], gain_rows[part_size:]

time: 1480 us -> 1460 us (0.986); the launches traced: 1450 us -> 1450 us
  waiting for transfers between devices: 463 us -> 413 us
  matrix products: 227 us -> 250 us
  Pallas kernels: 480 us -> 501 us
    ppermute x12, waiting for transfers between devices: 133 us -> 63.4 us  [hop_sum(): got.append(lax.ppermute(piece, 'expert', ring))]
    all_gather x4 -> x6, waiting for transfers between devices: 45.6 us -> 107 us  [to_plane(): return lax.all_gather(rows.reshape(-1, width), 'dp', axis=0, tiled=True)]
    ppermute x6, waiting for transfers between devices: 87.6 us -> 51.3 us  [chip_sum(): got.append(lax.ppermute(piece, 'dp', ring))]
    pallas_call x2 -> x3, Pallas kernels: 211 us -> 231 us  [unit_block(): pl.pallas_call(unit_kernel, in_specs=[hbm, hbm, vmem, vmem, vmem], out_sp...]
    dot_general x13 -> x16, matrix products: 138 us -> 155 us  [dot_tn(): lax.dot_general(left, right, contract_first, preferred_element_type=f32)]
    ppermute x21 -> x30, waiting for transfers between devices: 98.1 us -> 84.4 us  [hops(): pieces.append(lax.ppermute(rows[hop], 'expert', ring))]
    ppermute x21 -> x30, starting transfers between devices: 33.3 us -> 43.2 us  [hops(): pieces.append(lax.ppermute(rows[hop], 'expert', ring))]
    unnamed x157 -> x211, local copies, waits for them, and re-layouts: 38 us -> 36.6 us
  transfers between devices with their start and end apart: 56 -> 68, of which waited for: 23 -> 23; matrix products, arithmetic and copies ran while one was open for 24% -> 28% of each run, Pallas kernels for 26% -> 26%
where the time goes in v5:
time: 1460 us; the launch traced here: 1450 us
  Pallas kernels  501 us (34%)
  waiting for transfers between devices  413 us (28%)
  matrix products  250 us (17%)
  starting transfers between devices  99.1 us (7%)
  local copies, waits for them, and re-layouts  87.3 us (6%)
  other arithmetic  81.7 us (6%)
  between operations  21.3 us (1%)
    pallas_call x3, Pallas kernels, unit_block(): pl.pallas_call(unit_kernel, in_specs=[hbm, hbm, vmem, vmem, vmem], out_sp...  231 us
    dot_general x16, matrix products, dot_tn(): lax.dot_general(left, right, contract_first, preferred_element_type=f32)  155 us
    pallas_call x2, Pallas kernels, line_gather(): pl.pallas_call(line_kernel, in_specs=[hbm] * (1 + len(waits)), out_specs=...  132 us
    all_gather x6, waiting for transfers between devices, to_plane(): return lax.all_gather(rows.reshape(-1, width), 'dp', axis=0, tiled=True)  107 us
    all_to_all x2, waiting for transfers between devices, exchange(): lax.all_to_all(rows, 'expert', split_axis=0, concat_axis=0, tiled=True)  91 us
    ppermute x30, waiting for transfers between devices, hops(): pieces.append(lax.ppermute(rows[hop], 'expert', ring))  84.4 us
    dot_general x6, matrix products, dot_nt(): lax.dot_general(left, right, contract_last, preferred_element_type=f32)  66.6 us
    ppermute x12, waiting for transfers between devices, hop_sum(): got.append(lax.ppermute(piece, 'expert', ring))  63.4 us
  transfers between devices with their start and end apart: 68, of which 23 were waited for; matrix products, arithmetic and copies ran while one was open for 28% of the time, Pallas kernels for 26%

profile of v5, /device:TPU:0, one launch (start us, length us, event | category | flops | bytes accessed | tf_op | source)
XLA Modules:
  0.0 1454.4 jit_solution(9084896939721496752)
XLA Ops:
  7.2 41.0 %line_gather.2 = bf16[4,64,4096]{2,1,0:T(8,128)(2,1)} custom-call(bf16[64,4096]{1,0:T(8,128)(2,1)} %own_ref.2), custom_call_target="tpu_custom_call" | custom-call | bytes 4194304 | tf_op jit(solution)/shard_map/line_gather/pallas_call | solution.py:616
  55.3 91.4 %line_gather.3 = bf16[4,320,2048]{2,1,0:T(8,128)(2,1)} custom-call(bf16[320,2048]{1,0:T(8,128)(2,1)} %own_ref.3, bf16[256,4096]{1,0:T(8,128)(2,1)} %bitcast.314), custom_call_target="tpu_custom_call" | custom-call | bytes 10485760 | tf_op jit(solution)/shard_map/line_gather/pallas_call | solution.py:616
  178.2 36.2 %shard_map.189.k_ref.v_ref.refs_1_.refs_2_ = bf16[1280,4096]{1,0:T(8,128)(2,1)} custom-call(bf16[1280,2048]{1,0:T(8,128)(2,1)} %get-tuple-element.117.x_ref, bf16[2048,4096]{1,0:T(8,128)(2,1)} %all-gather.12.cloned.1.call-done.w_ref, f32[1280,128]{1,0:T(8,128)} %get-tuple-element.212.cos_ref.refs_10_, f32[1280,128]{1,0:T(8,128)} %get-tuple-element.213.sin_ref.refs_11_), custom_call_target="tpu_custom_call" | custom-call | flops 21474836480 | bytes 32505856 | tf_op jit(solution)/shard_map/pallas_call | solution.py:110
  231.1 12.3 shard_map.188
  243.4 32.7 %attend.1 = (bf16[4,184,2048]{2,1,0:T(8,128)(2,1)}, f32[4,184,2048]{2,1,0:T(8,128)}) custom-call(bf16[4,184,2048]{2,1,0:T(8,128)(2,1)} %bitcast.341, bf16[1280,4096]{1,0:T(8,128)(2,1)} %shard_map.189.k_ref.v_ref.refs_1_.refs_2_, bf16[1280,4096]{1,0:T(8,128)(2,1)} %shard_map.189.k_ref.v_ref.refs_1_.refs_2_, s32[4,184,1]{2,1,0:T(8,128)} %select_add_fusion.place_ref.refs_5_, ...), custom_call_target="tpu_custom_call" | custom-call | flops 5016387584 | bytes 22544384 | tf_op jit(solution)/shard_map/attend/pallas_call | solution.py:166
  276.1 12.8 fusion.24
  297.6 64.7 %all-to-all-done.1 = bf16[4,184,2048]{2,1,0:T(8,128)(2,1)} async-done(((bf16[4,184,2048]{2,1,0:T(8,128)(2,1)}), bf16[4,184,2048]{2,1,0:T(8,128)(2,1)}, u32[]{:S(2)}, u32[]{:S(2)}) %all-to-all-start.1) | async-done | bytes 3014688 | tf_op jit(solution)/shard_map/all_to_all | solution.py:640
  400.7 18.8 %collective-permute-done.7 = bf16[64,2048]{1,0:T(8,128)(2,1)S(1)} collective-permute-done((bf16[64,2048]{1,0:T(8,128)(2,1)S(1)}, bf16[64,2048]{1,0:T(8,128)(2,1)S(1)}, u32[]{:S(2)}, u32[]{:S(2)}) %collective-permute-start.7) | collective-permute-done | bytes 262176 | tf_op jit(solution)/shard_map/ppermute | solution.py:685
  432.8 15.9 %collective-permute-done.10 = bf16[72,2048]{1,0:T(8,128)(2,1)S(1)} collective-permute-done((bf16[72,2048]{1,0:T(8,128)(2,1)S(1)}, bf16[72,2048]{1,0:T(8,128)(2,1)S(1)}, u32[]{:S(2)}, u32[]{:S(2)}) %collective-permute-start.10) | collective-permute-done | bytes 294944 | tf_op jit(solution)/shard_map/ppermute | solution.py:685
  456.1 65.5 %unit_block.3 = (bf16[192,2048]{1,0:T(8,128)(2,1)}, bf16[1536,2048]{1,0:T(8,128)(2,1)}, bf16[1536,704]{1,0:T(8,128)(2,1)}, bf16[1536,704]{1,0:T(8,128)(2,1)}, bf16[1536,704]{1,0:T(8,128)(2,1)}) custom-call(bf16[1536,2048]{1,0:T(8,128)(2,1)} %all-gather.14.cloned.1.call-done.x_hbm, bf16[1536,2048]{1,0:T(8,128)(2,1)} %all-gather.16.cloned.1.call-done.g_hbm, ...), custom_call_target="tpu_custom_call" | custom-call | flops 26575110144 | bytes 34013184 | tf_op jit(solution)/shard_map/unit_block/pallas_call | solution.py:479
  521.7 46.5 %all-gather.18.cloned.1.call-done.x_hbm = bf16[2048,2048]{1,0:T(8,128)(2,1)} async-done(((bf16[256,2048]{1,0:T(8,128)(2,1)}), bf16[2048,2048]{1,0:T(8,128)(2,1)}) %all-gather.18.cloned.1.call-update) | async-done | bytes 8388624 | tf_op jit(solution)/shard_map/all_gather | solution.py:790
  568.2 89.3 %unit_block.4 = (bf16[256,2048]{1,0:T(8,128)(2,1)}, bf16[2048,2048]{1,0:T(8,128)(2,1)}, bf16[2048,704]{1,0:T(8,128)(2,1)}, bf16[2048,704]{1,0:T(8,128)(2,1)}, bf16[2048,704]{1,0:T(8,128)(2,1)}) custom-call(bf16[2048,2048]{1,0:T(8,128)(2,1)} %all-gather.18.cloned.1.call-done.x_hbm, bf16[2048,2048]{1,0:T(8,128)(2,1)} %all-gather.20.cloned.1.call-done.g_hbm, ...), custom_call_target="tpu_custom_call" | custom-call | flops 35433480192 | bytes 42467328 | tf_op jit(solution)/shard_map/unit_block/pallas_call | solution.py:479
  657.5 60.2 %all-gather.22.cloned.1.call-done.x_hbm = bf16[2304,2048]{1,0:T(8,128)(2,1)} async-done(((bf16[288,2048]{1,0:T(8,128)(2,1)}), bf16[2304,2048]{1,0:T(8,128)(2,1)}) %all-gather.22.cloned.1.call-update) | async-done | bytes 9437200 | tf_op jit(solution)/shard_map/all_gather | solution.py:790
  717.7 76.6 %unit_block.5 = (bf16[288,2048]{1,0:T(8,128)(2,1)}, bf16[2304,2048]{1,0:T(8,128)(2,1)}, bf16[2304,704]{1,0:T(8,128)(2,1)}, bf16[2304,704]{1,0:T(8,128)(2,1)}, bf16[2304,704]{1,0:T(8,128)(2,1)}) custom-call(bf16[2304,2048]{1,0:T(8,128)(2,1)} %all-gather.22.cloned.1.call-done.x_hbm, bf16[2304,2048]{1,0:T(8,128)(2,1)} %all-gather.24.cloned.1.call-done.g_hbm, ...), custom_call_target="tpu_custom_call" | custom-call | flops 39862665216 | bytes 46694400 | tf_op jit(solution)/shard_map/unit_block/pallas_call | solution.py:479
  803.7 12.1 fusion.151
  860.1 11.3 fusion.148
  898.1 12.6 fusion.150
  938.2 26.3 %all-to-all-done.2 = bf16[4,184,2048]{2,1,0:T(8,128)(2,1)} async-done(((bf16[4,184,2048]{2,1,0:T(8,128)(2,1)}), bf16[4,184,2048]{2,1,0:T(8,128)(2,1)}, u32[]{:S(2)}, u32[]{:S(2)}) %all-to-all-start.2) | async-done | bytes 3014688 | tf_op jit(solution)/shard_map/all_to_all | solution.py:640
  964.5 11.7 fusion.27
  976.2 56.0 %attend_back.1 = (bf16[4,184,2048]{2,1,0:T(8,128)(2,1)}, bf16[1280,2048]{1,0:T(8,128)(2,1)}, bf16[1280,2048]{1,0:T(8,128)(2,1)}) custom-call(bf16[4,184,2048]{2,1,0:T(8,128)(2,1)} %bitcast.342, bf16[1280,4096]{1,0:T(8,128)(2,1)} %shard_map.189.k_ref.v_ref.refs_1_.refs_2_, bf16[1280,4096]{1,0:T(8,128)(2,1)} %shard_map.189.k_ref.v_ref.refs_1_.refs_2_, ...), custom_call_target="tpu_custom_call" | custom-call | flops 12540968960 | bytes 36044800 | tf_op jit(solution)/shard_map/attend_back/pallas_call | solution.py:240
  1032.3 16.7 %convolution_convert_fusion.1 = bf16[2048,2048]{1,0:T(8,128)(2,1)} fusion(bf16[1280,2048]{1,0:T(8,128)(2,1)} %get-tuple-element.117.x_ref, bf16[1280,2048]{1,0:T(8,128)(2,1)} %get-tuple-element.55), kind=kOutput, calls=%fused_computation.19 | convolution fusion | flops 10741612544 | bytes 18874368 | tf_op jit(solution)/shard_map/dot_general | solution.py:72
  1050.8 20.7 %copy.44 = f32[704,1,3,2048]{3,1,2,0:T(1,128)} copy(f32[704,1,3,2048]{3,0,2,1:T(8,128)} %maximum_bitcast_fusion) | data formatting | bytes 34603008
  1074.1 16.8 %convolution_convert_fusion = bf16[2048,2048]{1,0:T(8,128)(2,1)} fusion(bf16[1280,2048]{1,0:T(8,128)(2,1)} %get-tuple-element.117.x_ref, bf16[1280,2048]{1,0:T(8,128)(2,1)} %get-tuple-element.56), kind=kOutput, calls=%fused_computation.18 | convolution fusion | flops 10741612544 | bytes 18874368 | tf_op jit(solution)/shard_map/dot_general | solution.py:72
  1105.6 11.2 bitcast_convert_fusion
  1118.5 11.0 fusion.16
  1129.5 11.1 fusion.145
  1175.7 12.1 fusion.146
  1194.7 20.9 %collective-permute-done.34 = bf16[320,1024]{1,0:T(8,128)(2,1)S(1)} collective-permute-done((bf16[320,1024]{1,0:T(8,128)(2,1)S(1)}, bf16[320,1024]{1,0:T(8,128)(2,1)S(1)}, u32[]{:S(2)}, u32[]{:S(2)}) %collective-permute-start.34) | collective-permute-done | bytes 655392 | tf_op jit(solution)/shard_map/ppermute | solution.py:649
  1229.0 28.1 %collective-permute-done.31 = bf16[320,1024]{1,0:T(8,128)(2,1)} collective-permute-done((bf16[320,1024]{1,0:T(8,128)(2,1)}, bf16[320,1024]{1,0:T(8,128)(2,1)}, u32[]{:S(2)}, u32[]{:S(2)}) %collective-permute-start.31) | collective-permute-done | bytes 655392 | tf_op jit(solution)/shard_map/ppermute | solution.py:649
  1298.5 21.0 %collective-permute-done.45 = bf16[256,2048]{1,0:T(8,128)(2,1)} collective-permute-done((bf16[256,2048]{1,0:T(8,128)(2,1)}, bf16[256,2048]{1,0:T(8,128)(2,1)}, u32[]{:S(2)}, u32[]{:S(2)}) %collective-permute-start.45) | collective-permute-done | bytes 1048608 | tf_op jit(solution)/shard_map/ppermute | solution.py:676
  1343.1 19.6 %collective-permute-done.49 = bf16[256,2048]{1,0:T(8,128)(2,1)} collective-permute-done((bf16[256,2048]{1,0:T(8,128)(2,1)}, bf16[256,2048]{1,0:T(8,128)(2,1)}, u32[]{:S(2)}, u32[]{:S(2)}) %collective-permute-start.49) | collective-permute-done | bytes 1048608 | tf_op jit(solution)/shard_map/ppermute | solution.py:676
  1414.3 14.4 all-to-all-done.3
  (492 shorter events, 435.4 us)
Async XLA Ops:
  7.2 171.0 %all-gather.12.cloned.1.call-start = ((), (), s32[]{:S(2)}) async-start(), calls=%async_computation.9 | async-start | bytes 18874368 | tf_op jit(solution)/shard_map/all_gather | solution.py:723
  48.2 182.8 %all-gather.26.cloned.1.call-start = ((), (), s32[]{:S(2)}) async-start(), calls=%async_computation.21 | async-start | bytes 9437184 | tf_op jit(solution)/shard_map/all_gather | solution.py:725
  49.0 227.1 %all-gather.28.cloned.1.call-start = ((), (), s32[]{:S(2)}) async-start(), calls=%async_computation.22 | async-start | bytes 9437184 | tf_op jit(solution)/shard_map/all_gather | solution.py:726
  50.4 117.8 %all-to-all-start = ((bf16[32,1,128]{2,1,0:T(2,128)(2,1)}), bf16[32,1,128]{2,1,0:T(2,128)(2,1)S(1)}, u32[]{:S(2)}, u32[]{:S(2)}) async-start(bf16[32,1,128]{2,1,0:T(2,128)(2,1)} %broadcast_in_dim.143), calls=%async_computation | async-start | bytes 32768 | tf_op jit(solution)/shard_map/all_to_all | solution.py:691
  55.2 400.9 %all-gather.16.cloned.1.call-start = ((), (), s32[]{:S(2)}) async-start(), calls=%async_computation.11 | async-start | bytes 7077888 | tf_op jit(solution)/shard_map/all_gather | solution.py:790
  152.7 63.6 %collective-permute-start.5 = (bf16[184,2048]{1,0:T(8,128)(2,1)}, bf16[184,2048]{1,0:T(8,128)(2,1)S(1)}, u32[]{:S(2)}, u32[]{:S(2)}) collective-permute-start(bf16[184,2048]{1,0:T(8,128)(2,1)} %get-tuple-element.135), channel_id=1, source_target_pairs={{0,3},{1,0},{2,1},{3,2},{4,7},{5,4},{6,5},{7,6},{8,11},{9,8},{10,9... | collective-permute-start | bytes 2261000 | tf_op jit(solution)/shard_map/ppermute | solution.py:685
  155.0 62.4 %collective-permute-start.4 = (bf16[184,2048]{1,0:T(8,128)(2,1)}, bf16[184,2048]{1,0:T(8,128)(2,1)S(1)}, u32[]{:S(2)}, u32[]{:S(2)}) collective-permute-start(bf16[184,2048]{1,0:T(8,128)(2,1)} %get-tuple-element.136), channel_id=1, source_target_pairs={{0,2},{1,3},{2,0},{3,1},{4,6},{5,7},{6,4},{7,5},{8,10},{9,11},{10,... | collective-permute-start | bytes 2261000 | tf_op jit(solution)/shard_map/ppermute | solution.py:685
  155.0 62.4 %collective-permute-start.3 = (bf16[184,2048]{1,0:T(8,128)(2,1)S(1)}, bf16[184,2048]{1,0:T(8,128)(2,1)S(1)}, u32[]{:S(2)}, u32[]{:S(2)}) collective-permute-start(bf16[184,2048]{1,0:T(8,128)(2,1)S(1)} %get-tuple-element.137), channel_id=1, source_target_pairs={{0,1},{1,2},{2,3},{3,0},{4,5},{5,6},{6,7},{7,4},{8,9},{9,10},{10,1... | collective-permute-start | bytes 2261000 | tf_op jit(solution)/shard_map/ppermute | solution.py:685
  288.9 73.4 %all-to-all-start.1 = ((bf16[4,184,2048]{2,1,0:T(8,128)(2,1)}), bf16[4,184,2048]{2,1,0:T(8,128)(2,1)}, u32[]{:S(2)}, u32[]{:S(2)}) async-start(bf16[4,184,2048]{2,1,0:T(8,128)(2,1)} %bitcast.338), calls=%async_computation.1 | async-start | bytes 6029312 | tf_op jit(solution)/shard_map/all_to_all | solution.py:640
  294.0 162.1 %all-gather.14.cloned.1.call-start = ((), (), s32[]{:S(2)}) async-start(), calls=%async_computation.10 | async-start | bytes 7077888 | tf_op jit(solution)/shard_map/all_gather | solution.py:790
  390.2 131.5 %all-gather.20.cloned.1.call-start = ((), (), s32[]{:S(2)}) async-start(), calls=%async_computation.13 | async-start | bytes 9437184 | tf_op jit(solution)/shard_map/all_gather | solution.py:790
  391.3 176.8 %all-gather.18.cloned.1.call-start = ((), (), s32[]{:S(2)}) async-start(), calls=%async_computation.12 | async-start | bytes 9437184 | tf_op jit(solution)/shard_map/all_gather | solution.py:790
  420.6 236.9 %all-gather.24.cloned.1.call-start = ((), (), s32[]{:S(2)}) async-start(), calls=%async_computation.15 | async-start | bytes 10616832 | tf_op jit(solution)/shard_map/all_gather | solution.py:790
  421.8 295.9 %all-gather.22.cloned.1.call-start = ((), (), s32[]{:S(2)}) async-start(), calls=%async_computation.14 | async-start | bytes 10616832 | tf_op jit(solution)/shard_map/all_gather | solution.py:790
  449.9 834.3 %reduce-scatter.6.cloned.1.call-start = ((), (), s32[]{:S(2)}) async-start(), calls=%async_computation.16 | async-start | bytes 7077888 | tf_op jit(solution)/shard_map/reduce_scatter | solution.py:660
  794.3 531.1 %reduce-scatter.8.cloned.1.call-start = ((), (), s32[]{:S(2)}) async-start(), calls=%async_computation.17 | async-start | bytes 9437184 | tf_op jit(solution)/shard_map/reduce_scatter | solution.py:660
  795.1 542.4 %reduce-scatter.10.cloned.1.call-start = ((), (), s32[]{:S(2)}) async-start(), calls=%async_computation.18 | async-start | bytes 10616832 | tf_op jit(solution)/shard_map/reduce_scatter | solution.py:660
  798.3 53.6 %collective-permute-start.23 = (bf16[48,2048]{1,0:T(8,128)(2,1)S(1)}, bf16[48,2048]{1,0:T(8,128)(2,1)}, u32[]{:S(2)}, u32[]{:S(2)}) collective-permute-start(bf16[48,2048]{1,0:T(8,128)(2,1)S(1)} %get-tuple-element.174), channel_id=1, source_target_pairs={{0,1},{1,2},{2,3},{3,0},{4,5},{5,6},{6,7},{7,4},{8,9},{9,10},{10,1... | collective-permute-start | bytes 589832 | tf_op jit(solution)/shard_map/ppermute | solution.py:685
  799.8 54.8 %collective-permute-start.22 = (bf16[48,2048]{1,0:T(8,128)(2,1)S(1)}, bf16[48,2048]{1,0:T(8,128)(2,1)}, u32[]{:S(2)}, u32[]{:S(2)}) collective-permute-start(bf16[48,2048]{1,0:T(8,128)(2,1)S(1)} %get-tuple-element.175), channel_id=1, source_target_pairs={{0,2},{1,3},{2,0},{3,1},{4,6},{5,7},{6,4},{7,5},{8,10},{9,11},{10,... | collective-permute-start | bytes 589832 | tf_op jit(solution)/shard_map/ppermute | solution.py:685
  802.2 53.5 %collective-permute-start.21 = (bf16[48,2048]{1,0:T(8,128)(2,1)S(1)}, bf16[48,2048]{1,0:T(8,128)(2,1)}, u32[]{:S(2)}, u32[]{:S(2)}) collective-permute-start(bf16[48,2048]{1,0:T(8,128)(2,1)S(1)} %get-tuple-element.176), channel_id=1, source_target_pairs={{0,3},{1,0},{2,1},{3,2},{4,7},{5,4},{6,5},{7,6},{8,11},{9,8},{10,9... | collective-permute-start | bytes 589832 | tf_op jit(solution)/shard_map/ppermute | solution.py:685
  890.2 74.3 %all-to-all-start.2 = ((bf16[4,184,2048]{2,1,0:T(8,128)(2,1)}), bf16[4,184,2048]{2,1,0:T(8,128)(2,1)}, u32[]{:S(2)}, u32[]{:S(2)}) async-start(bf16[4,184,2048]{2,1,0:T(8,128)(2,1)} %multiply_convert_fusion.1), calls=%async_computation.5 | async-start | bytes 6029312 | tf_op jit(solution)/shard_map/all_to_all | solution.py:640
  897.7 495.6 %reduce-scatter.14.cloned.1.call-start = ((), (), s32[]{:S(2)}) async-start(), calls=%async_computation.20 | async-start | bytes 9437184 | tf_op jit(solution)/shard_map/reduce_scatter | solution.py:660
  1049.0 353.8 %reduce-scatter.12.cloned.1.call-start = ((), (), s32[]{:S(2)}) async-start(), calls=%async_computation.19 | async-start | bytes 9437184 | tf_op jit(solution)/shard_map/reduce_scatter | solution.py:660
  1143.3 47.4 %collective-permute-start.33 = (bf16[320,1024]{1,0:T(8,128)(2,1)S(1)}, bf16[320,1024]{1,0:T(8,128)(2,1)S(1)}, u32[]{:S(2)}, u32[]{:S(2)}) collective-permute-start(bf16[320,1024]{1,0:T(8,128)(2,1)S(1)} %get-tuple-element.147), channel_id=1, source_target_pairs={{0,1},{1,2},{2,3},{3,0},{4,5},{5,6},{6,7},{7,4},{8,9},{9,10},{10,1... | collective-permute-start | bytes 1966088 | tf_op jit(solution)/shard_map/ppermute | solution.py:649
  1143.3 47.5 %collective-permute-start.35 = (bf16[320,1024]{1,0:T(8,128)(2,1)S(1)}, bf16[320,1024]{1,0:T(8,128)(2,1)S(1)}, u32[]{:S(2)}, u32[]{:S(2)}) collective-permute-start(bf16[320,1024]{1,0:T(8,128)(2,1)S(1)} %get-tuple-element.148), channel_id=1, source_target_pairs={{0,3},{1,0},{2,1},{3,2},{4,7},{5,4},{6,5},{7,6},{8,11},{9,8},{10,9... | collective-permute-start | bytes 1966088 | tf_op jit(solution)/shard_map/ppermute | solution.py:649
  1147.2 68.4 %collective-permute-start.34 = (bf16[320,1024]{1,0:T(8,128)(2,1)S(1)}, bf16[320,1024]{1,0:T(8,128)(2,1)S(1)}, u32[]{:S(2)}, u32[]{:S(2)}) collective-permute-start(bf16[320,1024]{1,0:T(8,128)(2,1)S(1)} %get-tuple-element.149), channel_id=1, source_target_pairs={{0,2},{1,3},{2,0},{3,1},{4,6},{5,7},{6,4},{7,5},{8,10},{9,11},{10,... | collective-permute-start | bytes 1966088 | tf_op jit(solution)/shard_map/ppermute | solution.py:649
  1161.4 99.0 %collective-permute-start.42 = (bf16[4,256,2048]{2,1,0:T(8,128)(2,1)}, bf16[4,256,2048]{2,1,0:T(8,128)(2,1)}, u32[]{:S(2)}, u32[]{:S(2)}) collective-permute-start(bf16[4,256,2048]{2,1,0:T(8,128)(2,1)} %dynamic-slice_bitcast_fusion.1), channel_id=1, source_target_pairs={{0,4},{4,0},{8,12},{12,8},{16,20},{20,16},{24,28},{28,24},{1,5},{5... | collective-permute-start | bytes 12582920 | tf_op jit(solution)/shard_map/ppermute | solution.py:670
  1163.7 110.4 %collective-permute-start.46 = (bf16[4,256,2048]{2,1,0:T(8,128)(2,1)}, bf16[4,256,2048]{2,1,0:T(8,128)(2,1)}, u32[]{:S(2)}, u32[]{:S(2)}) collective-permute-start(bf16[4,256,2048]{2,1,0:T(8,128)(2,1)} %dynamic-slice_bitcast_fusion), channel_id=1, source_target_pairs={{0,4},{4,0},{8,12},{12,8},{16,20},{20,16},{24,28},{28,24},{1,5},{5... | collective-permute-start | bytes 12582920 | tf_op jit(solution)/shard_map/ppermute | solution.py:670
  1271.2 48.3 %collective-permute-start.45 = (bf16[256,2048]{1,0:T(8,128)(2,1)}, bf16[256,2048]{1,0:T(8,128)(2,1)}, u32[]{:S(2)}, u32[]{:S(2)}) collective-permute-start(bf16[256,2048]{1,0:T(8,128)(2,1)} %get-tuple-element.122), channel_id=1, source_target_pairs={{0,24},{4,28},{8,0},{12,4},{16,8},{20,12},{24,16},{28,20},{1,25},{... | collective-permute-start | bytes 3145736 | tf_op jit(solution)/shard_map/ppermute | solution.py:676
  1281.3 60.9 %collective-permute-start.47 = (bf16[256,2048]{1,0:T(8,128)(2,1)}, bf16[256,2048]{1,0:T(8,128)(2,1)}, u32[]{:S(2)}, u32[]{:S(2)}) collective-permute-start(bf16[256,2048]{1,0:T(8,128)(2,1)} %get-tuple-element.118), channel_id=1, source_target_pairs={{0,8},{4,12},{8,16},{12,20},{16,24},{20,28},{24,0},{28,4},{1,9},{5... | collective-permute-start | bytes 3145736 | tf_op jit(solution)/shard_map/ppermute | solution.py:676
  1281.3 81.4 %collective-permute-start.49 = (bf16[256,2048]{1,0:T(8,128)(2,1)}, bf16[256,2048]{1,0:T(8,128)(2,1)}, u32[]{:S(2)}, u32[]{:S(2)}) collective-permute-start(bf16[256,2048]{1,0:T(8,128)(2,1)} %get-tuple-element.119), channel_id=1, source_target_pairs={{0,24},{4,28},{8,0},{12,4},{16,8},{20,12},{24,16},{28,20},{1,25},{... | collective-permute-start | bytes 3145736 | tf_op jit(solution)/shard_map/ppermute | solution.py:676
  1296.9 65.9 %collective-permute-start.48 = (bf16[256,2048]{1,0:T(8,128)(2,1)}, bf16[256,2048]{1,0:T(8,128)(2,1)}, u32[]{:S(2)}, u32[]{:S(2)}) collective-permute-start(bf16[256,2048]{1,0:T(8,128)(2,1)} %get-tuple-element.120), channel_id=1, source_target_pairs={{0,16},{4,20},{8,24},{12,28},{16,0},{20,4},{24,8},{28,12},{1,17},{... | collective-permute-start | bytes 3145736 | tf_op jit(solution)/shard_map/ppermute | solution.py:676
  (141 other events, 2451.3 us)
Sparse Core Ops, SparseCore 0:
  48.4 89.8 all-gather.11
  140.1 54.2 all-gather.25
  196.4 54.2 all-gather.27
  252.4 45.3 all-gather.15
  390.3 46.3 all-gather.13
  439.0 68.0 all-gather.19
  509.6 58.4 all-gather.17
  570.6 86.7 all-gather.23
  659.9 57.7 all-gather.21
  794.5 61.6 reduce-scatter.5
  859.7 71.5 reduce-scatter.7
  934.6 76.7 reduce-scatter.9
  1049.1 69.5 reduce-scatter.13
  1122.0 71.4 reduce-scatter.11

commit v6 on v4

--- a/solution.py
+++ b/solution.py
@@ -840,8 +840,10 @@
         return jnp.concatenate(back, axis=1).reshape(slot_total, width)
 
     in_back = join(in_parts)
-    grad_mlp = [dot_tn(k, r) for k, r in zip(kept[0], (plane_in[0], plane_in[0], plane_grad[0]))]
-    grad_second = dot_tn(mlp_pick_low, after(in_back, *grad_mlp))
+    grad_mlp = []
+    for j, rows in enumerate((plane_in[0], plane_in[0], plane_grad[0])):
+        grad_mlp.append(dot_tn(kept[0][j], rows))
+    grad_second = dot_tn(mlp_pick_low, in_back)
     cot_f32 = cotangent.astype(f32)
     grad_resid = cot_f32 + rms_back(grad_second, normed_two, scale_two, gain_two)
 
@@ -879,7 +881,7 @@
     grad_keys_w = dot_tn(hidden_all, grad_keys).astype(bf16)
     grad_values_w = dot_tn(hidden_all, grad_values).astype(bf16)
     grad_query = hold(grad_query, grad_keys_w, grad_values_w)
-    grad_kv_w = [plane_sum(grad_keys_w), plane_sum(grad_values_w)]
+    kv_sums = [plane_sum(grad_keys_w), plane_sum(grad_values_w)]
 
     grad_rows = dot_nt(grad_query, query_full).astype(bf16)
     half = width // 2
@@ -904,7 +906,7 @@
     query_term = dot_tn(query_rows, hold(grad_query, grad_h[1])).astype(bf16)
     grad_query_w = chip_sum(query_term, owners)
     grad_kv_w = jnp.concatenate(
-        [hop_sum(part.reshape(experts, -1, features), expert_id, experts) for part in grad_kv_w],
+        [hop_sum(part.reshape(experts, -1, features), expert_id, experts) for part in kv_sums],
         axis=1,
     )
     grad_h = lax.optimization_barrier(tuple(grad_h))
@@ -913,7 +915,6 @@
         for part, low in zip(grad_h, (0, half))
     ]
     grad_gain_two = jnp.sum(grad_second * normed_two, axis=0)
-    first_sum = grad_first[0]
     grad_first = jnp.concatenate(grad_first, axis=1)
     normed_one, scale_one = rms_parts(own_f32)
     grad_input = grad_resid + rms_back(grad_first, normed_one, scale_one, gain_one)
@@ -926,7 +927,7 @@
         axis=1,
     )
     gain_rows = lax.all_to_all(
-        hold(gain_rows, first_sum)[:, None, :], ("dp", "expert"), split_axis=0, concat_axis=0, tiled=True
+        hold(gain_rows, kv_sums[1])[:, None, :], ("dp", "expert"), split_axis=0, concat_axis=0, tiled=True
     )
     gain_rows = jnp.sum(gain_rows, axis=(0, 1))
     grad_gain_attn, grad_gain_mlp = gain_rows[:part_size], gain_rows[part_size:]

time: 1480 us -> 1460 us (0.986)
  waiting for transfers between devices: 463 us -> 439 us
  starting transfers between devices: 88.5 us -> 111 us
    ppermute x12, waiting for transfers between devices: 133 us -> 63.6 us  [hop_sum(): got.append(lax.ppermute(piece, 'expert', ring))]
    all_to_all x1, waiting for transfers between devices: 0.01 us -> 32.8 us  [layer(): lax.all_to_all(hold(gain_rows, kv_sums[1])[:, None, :], ('dp', 'expert'),...]
    all_to_all x1, starting transfers between devices: 4.29 us -> 26.6 us  [layer(): lax.all_to_all(hold(gain_rows, kv_sums[1])[:, None, :], ('dp', 'expert'),...]
    all_gather x4, waiting for transfers between devices: 45.6 us -> 66.5 us  [to_plane(): return lax.all_gather(rows.reshape(-1, width), 'dp', axis=0, tiled=True)]
    unnamed x157 -> x151, local copies, waits for them, and re-layouts: 38 us -> 31.9 us
  transfers between devices with their start and end apart: 56 -> 56, of which waited for: 23 -> 23; matrix products, arithmetic and copies ran while one was open for 24% -> 26% of each run, Pallas kernels for 26% -> 30%
where the time goes in v6:
time: 1460 us; the launch traced here: 1450 us
  Pallas kernels  480 us (33%)
  waiting for transfers between devices  439 us (30%)
  matrix products  236 us (16%)
  starting transfers between devices  111 us (8%)
  local copies, waits for them, and re-layouts  80.7 us (6%)
  other arithmetic  78.2 us (5%)
  between operations  20.9 us (1%)
    pallas_call x2, Pallas kernels, unit_block(): pl.pallas_call(unit_kernel, in_specs=[hbm, hbm, vmem, vmem, vmem], out_sp...  211 us
    dot_general x13, matrix products, dot_tn(): lax.dot_general(left, right, contract_first, preferred_element_type=f32)  147 us
    pallas_call x2, Pallas kernels, line_gather(): pl.pallas_call(line_kernel, in_specs=[hbm] * (1 + len(waits)), out_specs=...  132 us
    ppermute x21, waiting for transfers between devices, hops(): pieces.append(lax.ppermute(rows[hop], 'expert', ring))  100 us
    all_to_all x2, waiting for transfers between devices, exchange(): lax.all_to_all(rows, 'expert', split_axis=0, concat_axis=0, tiled=True)  95.8 us
    ppermute x6, waiting for transfers between devices, chip_sum(): got.append(lax.ppermute(piece, 'dp', ring))  78 us
    all_gather x4, waiting for transfers between devices, to_plane(): return lax.all_gather(rows.reshape(-1, width), 'dp', axis=0, tiled=True)  66.5 us
    ppermute x12, waiting for transfers between devices, hop_sum(): got.append(lax.ppermute(piece, 'expert', ring))  63.6 us
  transfers between devices with their start and end apart: 56, of which 23 were waited for; matrix products, arithmetic and copies ran while one was open for 26% of the time, Pallas kernels for 30%

profile of v6, /device:TPU:0, one launch (start us, length us, event | category | flops | bytes accessed | tf_op | source)
XLA Modules:
  0.0 1445.8 jit_solution(7222641525024510579)
XLA Ops:
  7.2 41.0 %line_gather.2 = bf16[4,64,4096]{2,1,0:T(8,128)(2,1)} custom-call(bf16[64,4096]{1,0:T(8,128)(2,1)} %own_ref.2), custom_call_target="tpu_custom_call" | custom-call | bytes 4194304 | tf_op jit(solution)/shard_map/line_gather/pallas_call | solution.py:616
  55.3 91.4 %line_gather.3 = bf16[4,320,2048]{2,1,0:T(8,128)(2,1)} custom-call(bf16[320,2048]{1,0:T(8,128)(2,1)} %own_ref.3, bf16[256,4096]{1,0:T(8,128)(2,1)} %bitcast.283), custom_call_target="tpu_custom_call" | custom-call | bytes 10485760 | tf_op jit(solution)/shard_map/line_gather/pallas_call | solution.py:616
  173.6 36.2 %shard_map.189.k_ref.v_ref.refs_1_.refs_2_ = bf16[1280,4096]{1,0:T(8,128)(2,1)} custom-call(bf16[1280,2048]{1,0:T(8,128)(2,1)} %get-tuple-element.105.x_ref, bf16[2048,4096]{1,0:T(8,128)(2,1)} %all-gather.10.cloned.1.call-done.w_ref, f32[1280,128]{1,0:T(8,128)} %get-tuple-element.188.cos_ref.refs_10_, f32[1280,128]{1,0:T(8,128)} %get-tuple-element.189.sin_ref.refs_11_), custom_call_target="tpu_custom_call" | custom-call | flops 21474836480 | bytes 32505856 | tf_op jit(solution)/shard_map/pallas_call | solution.py:110
  235.2 12.3 shard_map.188
  247.5 32.7 %attend.1 = (bf16[4,184,2048]{2,1,0:T(8,128)(2,1)}, f32[4,184,2048]{2,1,0:T(8,128)}) custom-call(bf16[4,184,2048]{2,1,0:T(8,128)(2,1)} %bitcast.302, bf16[1280,4096]{1,0:T(8,128)(2,1)} %shard_map.189.k_ref.v_ref.refs_1_.refs_2_, bf16[1280,4096]{1,0:T(8,128)(2,1)} %shard_map.189.k_ref.v_ref.refs_1_.refs_2_, s32[4,184,1]{2,1,0:T(8,128)} %select_add_fusion.place_ref.refs_5_, ...), custom_call_target="tpu_custom_call" | custom-call | flops 5016387584 | bytes 22544384 | tf_op jit(solution)/shard_map/attend/pallas_call | solution.py:166
  280.1 12.0 fusion.24
  300.0 64.9 %all-to-all-done.1 = bf16[4,184,2048]{2,1,0:T(8,128)(2,1)} async-done(((bf16[4,184,2048]{2,1,0:T(8,128)(2,1)}), bf16[4,184,2048]{2,1,0:T(8,128)(2,1)}, u32[]{:S(2)}, u32[]{:S(2)}) %all-to-all-start.1) | async-done | bytes 3014688 | tf_op jit(solution)/shard_map/all_to_all | solution.py:640
  386.2 19.7 %collective-permute-done.1 = bf16[88,2048]{1,0:T(8,128)(2,1)S(1)} collective-permute-done((bf16[88,2048]{1,0:T(8,128)(2,1)S(1)}, bf16[88,2048]{1,0:T(8,128)(2,1)S(1)}, u32[]{:S(2)}, u32[]{:S(2)}) %collective-permute-start.1) | collective-permute-done | bytes 360480 | tf_op jit(solution)/shard_map/ppermute | solution.py:685
  420.9 27.2 %collective-permute-done.7 = bf16[96,2048]{1,0:T(8,128)(2,1)S(1)} collective-permute-done((bf16[96,2048]{1,0:T(8,128)(2,1)S(1)}, bf16[96,2048]{1,0:T(8,128)(2,1)S(1)}, u32[]{:S(2)}, u32[]{:S(2)}) %collective-permute-start.7) | collective-permute-done | bytes 393248 | tf_op jit(solution)/shard_map/ppermute | solution.py:685
  459.2 16.8 %all-gather.12.cloned.1.call-done.x_hbm = bf16[2816,2048]{1,0:T(8,128)(2,1)} async-done(((bf16[352,2048]{1,0:T(8,128)(2,1)}), bf16[2816,2048]{1,0:T(8,128)(2,1)}) %all-gather.12.cloned.1.call-update) | async-done | bytes 11534352 | tf_op jit(solution)/shard_map/all_gather | solution.py:790
  476.0 112.5 %unit_block.2 = (bf16[352,2048]{1,0:T(8,128)(2,1)}, bf16[2816,2048]{1,0:T(8,128)(2,1)}, bf16[2816,704]{1,0:T(8,128)(2,1)}, bf16[2816,704]{1,0:T(8,128)(2,1)}, bf16[2816,704]{1,0:T(8,128)(2,1)}) custom-call(bf16[2816,2048]{1,0:T(8,128)(2,1)} %all-gather.12.cloned.1.call-done.x_hbm, bf16[2816,2048]{1,0:T(8,128)(2,1)} %all-gather.14.cloned.1.call-done.g_hbm, ...), custom_call_target="tpu_custom_call" | custom-call | flops 48721035264 | bytes 55148544 | tf_op jit(solution)/shard_map/unit_block/pallas_call | solution.py:479
  596.4 15.3 %fusion.140 = f32[704,2048]{1,0:T(8,128)} fusion(bf16[2816,704]{1,0:T(8,128)(2,1)} %get-tuple-element.39, bf16[2816,2048]{1,0:T(8,128)(2,1)} %all-gather.14.cloned.1.call-done.g_hbm), kind=kOutput, calls=%fused_computation.274 | convolution fusion | flops 8120172544 | bytes 21266432 | tf_op jit(solution)/shard_map/dot_general | solution.py:72
  611.7 49.8 %all-gather.16.cloned.1.call-done.x_hbm = bf16[3072,2048]{1,0:T(8,128)(2,1)} async-done(((bf16[384,2048]{1,0:T(8,128)(2,1)}), bf16[3072,2048]{1,0:T(8,128)(2,1)}) %all-gather.16.cloned.1.call-update) | async-done | bytes 12582928 | tf_op jit(solution)/shard_map/all_gather | solution.py:790
  661.4 98.6 %unit_block.3 = (bf16[384,2048]{1,0:T(8,128)(2,1)}, bf16[3072,2048]{1,0:T(8,128)(2,1)}, bf16[3072,704]{1,0:T(8,128)(2,1)}, bf16[3072,704]{1,0:T(8,128)(2,1)}, bf16[3072,704]{1,0:T(8,128)(2,1)}) custom-call(bf16[3072,2048]{1,0:T(8,128)(2,1)} %all-gather.16.cloned.1.call-done.x_hbm, bf16[3072,2048]{1,0:T(8,128)(2,1)} %all-gather.18.cloned.1.call-done.g_hbm, ...), custom_call_target="tpu_custom_call" | custom-call | flops 53150220288 | bytes 59375616 | tf_op jit(solution)/shard_map/unit_block/pallas_call | solution.py:479
  760.1 14.4 fusion.138
  774.5 15.8 %fusion.139 = f32[704,2048]{1,0:T(8,128)} fusion(bf16[2816,704]{1,0:T(8,128)(2,1)} %get-tuple-element.37, bf16[2816,2048]{1,0:T(8,128)(2,1)} %all-gather.12.cloned.1.call-done.x_hbm), kind=kOutput, calls=%fused_computation.273 | convolution fusion | flops 8120172544 | bytes 21266432 | tf_op jit(solution)/shard_map/dot_general | solution.py:72
  796.1 14.0 add_bitcast_fusion
  839.4 15.2 %add_bitcast_fusion.1 = f32[704,1,2048]{2,0,1:T(8,128)S(1)} fusion(f32[704,2048]{1,0:T(8,128)} %fusion.139, bf16[3072,704]{1,0:T(8,128)(2,1)} %get-tuple-element.38, bf16[3072,2048]{1,0:T(8,128)(2,1)} %all-gather.16.cloned.1.call-done.x_hbm), kind=kOutput, calls=%fused_computation.23 | convolution fusion | flops 8859811840 | bytes 28442624 | tf_op jit(solution)/shard_map/dot_general | solution.py:72
  854.5 14.5 %add_bitcast_fusion.2 = f32[704,1,2048]{2,0,1:T(8,128)S(1)} fusion(f32[704,2048]{1,0:T(8,128)} %fusion.138, bf16[3072,704]{1,0:T(8,128)(2,1)} %get-tuple-element.36, bf16[3072,2048]{1,0:T(8,128)(2,1)} %all-gather.16.cloned.1.call-done.x_hbm), kind=kOutput, calls=%fused_computation.24 | convolution fusion | flops 8859811840 | bytes 28442624 | tf_op jit(solution)/shard_map/dot_general | solution.py:72
  875.4 30.9 %all-to-all-done.2 = bf16[4,184,2048]{2,1,0:T(8,128)(2,1)S(1)} async-done(((bf16[4,184,2048]{2,1,0:T(8,128)(2,1)}), bf16[4,184,2048]{2,1,0:T(8,128)(2,1)S(1)}, u32[]{:S(2)}, u32[]{:S(2)}) %all-to-all-start.2) | async-done | bytes 3014688 | tf_op jit(solution)/shard_map/all_to_all | solution.py:640
  916.3 55.7 %attend_back.1 = (bf16[4,184,2048]{2,1,0:T(8,128)(2,1)}, bf16[1280,2048]{1,0:T(8,128)(2,1)}, bf16[1280,2048]{1,0:T(8,128)(2,1)}) custom-call(bf16[4,184,2048]{2,1,0:T(8,128)(2,1)} %bitcast.303, bf16[1280,4096]{1,0:T(8,128)(2,1)} %shard_map.189.k_ref.v_ref.refs_1_.refs_2_, bf16[1280,4096]{1,0:T(8,128)(2,1)} %shard_map.189.k_ref.v_ref.refs_1_.refs_2_, ...), custom_call_target="tpu_custom_call" | custom-call | flops 12540968960 | bytes 36044800 | tf_op jit(solution)/shard_map/attend_back/pallas_call | solution.py:240
  972.0 16.7 %convolution_convert_fusion.1 = bf16[2048,2048]{1,0:T(8,128)(2,1)} fusion(bf16[1280,2048]{1,0:T(8,128)(2,1)} %get-tuple-element.105.x_ref, bf16[1280,2048]{1,0:T(8,128)(2,1)} %get-tuple-element.43), kind=kOutput, calls=%fused_computation.19 | convolution fusion | flops 10741612544 | bytes 18874368 | tf_op jit(solution)/shard_map/dot_general | solution.py:72
  988.8 16.8 %convolution_convert_fusion = bf16[2048,2048]{1,0:T(8,128)(2,1)} fusion(bf16[1280,2048]{1,0:T(8,128)(2,1)} %get-tuple-element.105.x_ref, bf16[1280,2048]{1,0:T(8,128)(2,1)} %get-tuple-element.44), kind=kOutput, calls=%fused_computation.18 | convolution fusion | flops 10741612544 | bytes 18874368 | tf_op jit(solution)/shard_map/dot_general | solution.py:72
  1006.9 20.9 %copy.44 = f32[704,1,3,2048]{3,1,2,0:T(1,128)} copy(f32[704,1,3,2048]{3,0,2,1:T(8,128)} %maximum_bitcast_fusion) | data formatting | bytes 34603008
  1147.9 12.6 collective-permute-done.23
  1160.5 28.5 %collective-permute-done.22 = bf16[320,1024]{1,0:T(8,128)(2,1)S(1)} collective-permute-done((bf16[320,1024]{1,0:T(8,128)(2,1)S(1)}, bf16[320,1024]{1,0:T(8,128)(2,1)S(1)}, u32[]{:S(2)}, u32[]{:S(2)}) %collective-permute-start.22) | collective-permute-done | bytes 655392 | tf_op jit(solution)/shard_map/ppermute | solution.py:649
  1205.6 19.9 %collective-permute-done.36 = bf16[256,2048]{1,0:T(8,128)(2,1)S(1)} collective-permute-done((bf16[256,2048]{1,0:T(8,128)(2,1)S(1)}, bf16[256,2048]{1,0:T(8,128)(2,1)S(1)}, u32[]{:S(2)}, u32[]{:S(2)}) %collective-permute-start.36) | collective-permute-done | bytes 1048608 | tf_op jit(solution)/shard_map/ppermute | solution.py:676
  1229.0 22.3 %collective-permute-done.38 = bf16[256,2048]{1,0:T(8,128)(2,1)S(1)} collective-permute-done((bf16[256,2048]{1,0:T(8,128)(2,1)}, bf16[256,2048]{1,0:T(8,128)(2,1)S(1)}, u32[]{:S(2)}, u32[]{:S(2)}) %collective-permute-start.38) | collective-permute-done | bytes 1048608 | tf_op jit(solution)/shard_map/ppermute | solution.py:676
  1251.3 35.8 %collective-permute-done.40 = bf16[256,2048]{1,0:T(8,128)(2,1)S(1)} collective-permute-done((bf16[256,2048]{1,0:T(8,128)(2,1)}, bf16[256,2048]{1,0:T(8,128)(2,1)S(1)}, u32[]{:S(2)}, u32[]{:S(2)}) %collective-permute-start.40) | collective-permute-done | bytes 1048608 | tf_op jit(solution)/shard_map/ppermute | solution.py:676
  1305.1 26.6 %all-to-all-start.3 = ((f32[32,1,128]{2,1,0:T(1,128)}), f32[32,1,128]{2,1,0:T(1,128)S(1)}, u32[]{:S(2)}, u32[]{:S(2)}) async-start(f32[32,1,128]{2,1,0:T(1,128)} %maximum_add_fusion.1), calls=%async_computation.6 | async-start | bytes 32768 | tf_op jit(solution)/shard_map/all_to_all | solution.py:929
  1333.8 32.8 %all-to-all-done.3 = f32[32,1,128]{2,1,0:T(1,128)S(1)} async-done(((f32[32,1,128]{2,1,0:T(1,128)}), f32[32,1,128]{2,1,0:T(1,128)S(1)}, u32[]{:S(2)}, u32[]{:S(2)}) %all-to-all-start.3) | async-done | bytes 16416 | tf_op jit(solution)/shard_map/all_to_all | solution.py:929
  1415.2 15.2 %collective-permute-done.13 = bf16[96,2048]{1,0:T(8,128)(2,1)S(1)} collective-permute-done((bf16[96,2048]{1,0:T(8,128)(2,1)S(1)}, bf16[96,2048]{1,0:T(8,128)(2,1)S(1)}, u32[]{:S(2)}, u32[]{:S(2)}) %collective-permute-start.13) | collective-permute-done | bytes 393248 | tf_op jit(solution)/shard_map/ppermute | solution.py:685
  (393 shorter events, 386.1 us)
Async XLA Ops:
  7.2 166.4 %all-gather.10.cloned.1.call-start = ((), (), s32[]{:S(2)}) async-start(), calls=%async_computation.8 | async-start | bytes 18874368 | tf_op jit(solution)/shard_map/all_gather | solution.py:723
  48.2 186.9 %all-gather.20.cloned.1.call-start = ((), (), s32[]{:S(2)}) async-start(), calls=%async_computation.17 | async-start | bytes 9437184 | tf_op jit(solution)/shard_map/all_gather | solution.py:725
  49.0 231.2 %all-gather.22.cloned.1.call-start = ((), (), s32[]{:S(2)}) async-start(), calls=%async_computation.18 | async-start | bytes 9437184 | tf_op jit(solution)/shard_map/all_gather | solution.py:726
  50.4 112.8 %all-to-all-start = ((bf16[32,1,128]{2,1,0:T(2,128)(2,1)}), bf16[32,1,128]{2,1,0:T(2,128)(2,1)S(1)}, u32[]{:S(2)}, u32[]{:S(2)}) async-start(bf16[32,1,128]{2,1,0:T(2,128)(2,1)} %broadcast_in_dim.143), calls=%async_computation | async-start | bytes 32768 | tf_op jit(solution)/shard_map/all_to_all | solution.py:691
  55.2 404.0 %all-gather.14.cloned.1.call-start = ((), (), s32[]{:S(2)}) async-start(), calls=%async_computation.10 | async-start | bytes 12976128 | tf_op jit(solution)/shard_map/all_gather | solution.py:790
  154.6 62.4 %collective-permute-start.4 = (bf16[184,2048]{1,0:T(8,128)(2,1)}, bf16[184,2048]{1,0:T(8,128)(2,1)S(1)}, u32[]{:S(2)}, u32[]{:S(2)}) collective-permute-start(bf16[184,2048]{1,0:T(8,128)(2,1)} %get-tuple-element.120), channel_id=1, source_target_pairs={{0,2},{1,3},{2,0},{3,1},{4,6},{5,7},{6,4},{7,5},{8,10},{9,11},{10,... | collective-permute-start | bytes 2261000 | tf_op jit(solution)/shard_map/ppermute | solution.py:685
  154.6 62.4 %collective-permute-start.3 = (bf16[184,2048]{1,0:T(8,128)(2,1)S(1)}, bf16[184,2048]{1,0:T(8,128)(2,1)S(1)}, u32[]{:S(2)}, u32[]{:S(2)}) collective-permute-start(bf16[184,2048]{1,0:T(8,128)(2,1)S(1)} %get-tuple-element.121), channel_id=1, source_target_pairs={{0,1},{1,2},{2,3},{3,0},{4,5},{5,6},{6,7},{7,4},{8,9},{9,10},{10,1... | collective-permute-start | bytes 2261000 | tf_op jit(solution)/shard_map/ppermute | solution.py:685
  292.2 72.7 %all-to-all-start.1 = ((bf16[4,184,2048]{2,1,0:T(8,128)(2,1)}), bf16[4,184,2048]{2,1,0:T(8,128)(2,1)}, u32[]{:S(2)}, u32[]{:S(2)}) async-start(bf16[4,184,2048]{2,1,0:T(8,128)(2,1)} %bitcast.299), calls=%async_computation.1 | async-start | bytes 6029312 | tf_op jit(solution)/shard_map/all_to_all | solution.py:640
  296.9 179.1 %all-gather.12.cloned.1.call-start = ((), (), s32[]{:S(2)}) async-start(), calls=%async_computation.9 | async-start | bytes 12976128 | tf_op jit(solution)/shard_map/all_gather | solution.py:790
  407.2 204.5 %all-gather.18.cloned.1.call-start = ((), (), s32[]{:S(2)}) async-start(), calls=%async_computation.12 | async-start | bytes 14155776 | tf_op jit(solution)/shard_map/all_gather | solution.py:790
  408.5 252.9 %all-gather.16.cloned.1.call-start = ((), (), s32[]{:S(2)}) async-start(), calls=%async_computation.11 | async-start | bytes 14155776 | tf_op jit(solution)/shard_map/all_gather | solution.py:790
  449.5 841.0 %reduce-scatter.5.cloned.1.call-start = ((), (), s32[]{:S(2)}) async-start(), calls=%async_computation.13 | async-start | bytes 12976128 | tf_op jit(solution)/shard_map/reduce_scatter | solution.py:660
  591.1 203.5 %collective-permute-start.17 = (bf16[88,2048]{1,0:T(8,128)(2,1)}, bf16[88,2048]{1,0:T(8,128)(2,1)}, u32[]{:S(2)}, u32[]{:S(2)}) collective-permute-start(bf16[88,2048]{1,0:T(8,128)(2,1)} %get-tuple-element.143), channel_id=1, source_target_pairs={{0,1},{1,2},{2,3},{3,0},{4,5},{5,6},{6,7},{7,4},{8,9},{9,10},{10,1... | collective-permute-start | bytes 1081352 | tf_op jit(solution)/shard_map/ppermute | solution.py:685
  592.5 217.6 %collective-permute-start.16 = (bf16[88,2048]{1,0:T(8,128)(2,1)}, bf16[88,2048]{1,0:T(8,128)(2,1)}, u32[]{:S(2)}, u32[]{:S(2)}) collective-permute-start(bf16[88,2048]{1,0:T(8,128)(2,1)} %get-tuple-element.144), channel_id=1, source_target_pairs={{0,2},{1,3},{2,0},{3,1},{4,6},{5,7},{6,4},{7,5},{8,10},{9,11},{10,... | collective-permute-start | bytes 1081352 | tf_op jit(solution)/shard_map/ppermute | solution.py:685
  594.9 215.2 %collective-permute-start.15 = (bf16[88,2048]{1,0:T(8,128)(2,1)}, bf16[88,2048]{1,0:T(8,128)(2,1)}, u32[]{:S(2)}, u32[]{:S(2)}) collective-permute-start(bf16[88,2048]{1,0:T(8,128)(2,1)} %get-tuple-element.145), channel_id=1, source_target_pairs={{0,3},{1,0},{2,1},{3,2},{4,7},{5,4},{6,5},{7,6},{8,11},{9,8},{10,9... | collective-permute-start | bytes 1081352 | tf_op jit(solution)/shard_map/ppermute | solution.py:685
  828.2 78.2 %all-to-all-start.2 = ((bf16[4,184,2048]{2,1,0:T(8,128)(2,1)}), bf16[4,184,2048]{2,1,0:T(8,128)(2,1)S(1)}, u32[]{:S(2)}, u32[]{:S(2)}) async-start(bf16[4,184,2048]{2,1,0:T(8,128)(2,1)} %multiply_convert_fusion.1), calls=%async_computation.4 | async-start | bytes 6029312 | tf_op jit(solution)/shard_map/all_to_all | solution.py:640
  839.4 457.4 %reduce-scatter.11.cloned.1.call-start = ((), (), s32[]{:S(2)}) async-start(), calls=%async_computation.16 | async-start | bytes 9437184 | tf_op jit(solution)/shard_map/reduce_scatter | solution.py:660
  988.7 313.8 %reduce-scatter.9.cloned.1.call-start = ((), (), s32[]{:S(2)}) async-start(), calls=%async_computation.15 | async-start | bytes 9437184 | tf_op jit(solution)/shard_map/reduce_scatter | solution.py:660
  1005.6 390.4 %reduce-scatter.7.cloned.1.call-start = ((), (), s32[]{:S(2)}) async-start(), calls=%async_computation.14 | async-start | bytes 14155776 | tf_op jit(solution)/shard_map/reduce_scatter | solution.py:660
  1068.7 59.7 %collective-permute-start.24 = (bf16[320,1024]{1,0:T(8,128)(2,1)}, bf16[320,1024]{1,0:T(8,128)(2,1)}, u32[]{:S(2)}, u32[]{:S(2)}) collective-permute-start(bf16[320,1024]{1,0:T(8,128)(2,1)} %get-tuple-element.131), channel_id=1, source_target_pairs={{0,1},{1,2},{2,3},{3,0},{4,5},{5,6},{6,7},{7,4},{8,9},{9,10},{10,1... | collective-permute-start | bytes 1966088 | tf_op jit(solution)/shard_map/ppermute | solution.py:649
  1068.7 61.0 %collective-permute-start.26 = (bf16[320,1024]{1,0:T(8,128)(2,1)}, bf16[320,1024]{1,0:T(8,128)(2,1)}, u32[]{:S(2)}, u32[]{:S(2)}) collective-permute-start(bf16[320,1024]{1,0:T(8,128)(2,1)} %get-tuple-element.132), channel_id=1, source_target_pairs={{0,3},{1,0},{2,1},{3,2},{4,7},{5,4},{6,5},{7,6},{8,11},{9,8},{10,9... | collective-permute-start | bytes 1966088 | tf_op jit(solution)/shard_map/ppermute | solution.py:649
  1072.5 59.8 %collective-permute-start.25 = (bf16[320,1024]{1,0:T(8,128)(2,1)}, bf16[320,1024]{1,0:T(8,128)(2,1)}, u32[]{:S(2)}, u32[]{:S(2)}) collective-permute-start(bf16[320,1024]{1,0:T(8,128)(2,1)} %get-tuple-element.133), channel_id=1, source_target_pairs={{0,2},{1,3},{2,0},{3,1},{4,6},{5,7},{6,4},{7,5},{8,10},{9,11},{10,... | collective-permute-start | bytes 1966088 | tf_op jit(solution)/shard_map/ppermute | solution.py:649
  1096.5 97.2 %collective-permute-start.37 = (bf16[4,256,2048]{2,1,0:T(8,128)(2,1)}, bf16[4,256,2048]{2,1,0:T(8,128)(2,1)}, u32[]{:S(2)}, u32[]{:S(2)}) collective-permute-start(bf16[4,256,2048]{2,1,0:T(8,128)(2,1)} %dynamic-slice_bitcast_fusion), channel_id=1, source_target_pairs={{0,4},{4,0},{8,12},{12,8},{16,20},{20,16},{24,28},{28,24},{1,5},{5... | collective-permute-start | bytes 12582920 | tf_op jit(solution)/shard_map/ppermute | solution.py:670
  1141.4 62.6 %collective-permute-start.34 = (bf16[256,2048]{1,0:T(8,128)(2,1)S(1)}, bf16[256,2048]{1,0:T(8,128)(2,1)S(1)}, u32[]{:S(2)}, u32[]{:S(2)}) collective-permute-start(bf16[256,2048]{1,0:T(8,128)(2,1)S(1)} %get-tuple-element.109), channel_id=1, source_target_pairs={{0,8},{4,12},{8,16},{12,20},{16,24},{20,28},{24,0},{28,4},{1,9},{5... | collective-permute-start | bytes 3145736 | tf_op jit(solution)/shard_map/ppermute | solution.py:676
  1201.5 85.6 %collective-permute-start.40 = (bf16[256,2048]{1,0:T(8,128)(2,1)}, bf16[256,2048]{1,0:T(8,128)(2,1)S(1)}, u32[]{:S(2)}, u32[]{:S(2)}) collective-permute-start(bf16[256,2048]{1,0:T(8,128)(2,1)} %get-tuple-element.107), channel_id=1, source_target_pairs={{0,24},{4,28},{8,0},{12,4},{16,8},{20,12},{24,16},{28,20},{1,25},{... | collective-permute-start | bytes 3145736 | tf_op jit(solution)/shard_map/ppermute | solution.py:676
  1204.1 83.0 %collective-permute-start.39 = (bf16[256,2048]{1,0:T(8,128)(2,1)}, bf16[256,2048]{1,0:T(8,128)(2,1)S(1)}, u32[]{:S(2)}, u32[]{:S(2)}) collective-permute-start(bf16[256,2048]{1,0:T(8,128)(2,1)} %get-tuple-element.108), channel_id=1, source_target_pairs={{0,16},{4,20},{8,24},{12,28},{16,0},{20,4},{24,8},{28,12},{1,17},{... | collective-permute-start | bytes 3145736 | tf_op jit(solution)/shard_map/ppermute | solution.py:676
  1292.8 112.9 %collective-permute-start.11 = (bf16[88,2048]{1,0:T(8,128)(2,1)}, bf16[88,2048]{1,0:T(8,128)(2,1)}, u32[]{:S(2)}, u32[]{:S(2)}) collective-permute-start(bf16[88,2048]{1,0:T(8,128)(2,1)} %get-tuple-element.147), channel_id=1, source_target_pairs={{0,1},{1,2},{2,3},{3,0},{4,5},{5,6},{6,7},{7,4},{8,9},{9,10},{10,1... | collective-permute-start | bytes 1081352 | tf_op jit(solution)/shard_map/ppermute | solution.py:685
  1294.3 112.4 %collective-permute-start.10 = (bf16[88,2048]{1,0:T(8,128)(2,1)}, bf16[88,2048]{1,0:T(8,128)(2,1)}, u32[]{:S(2)}, u32[]{:S(2)}) collective-permute-start(bf16[88,2048]{1,0:T(8,128)(2,1)} %get-tuple-element.148), channel_id=1, source_target_pairs={{0,2},{1,3},{2,0},{3,1},{4,6},{5,7},{6,4},{7,5},{8,10},{9,11},{10,... | collective-permute-start | bytes 1081352 | tf_op jit(solution)/shard_map/ppermute | solution.py:685
  1298.7 68.6 %collective-permute-start.27 = (bf16[64,2048]{1,0:T(8,128)(2,1)}, bf16[64,2048]{1,0:T(8,128)(2,1)}, u32[]{:S(2)}, u32[]{:S(2)}) collective-permute-start(bf16[64,2048]{1,0:T(8,128)(2,1)} %get-tuple-element.151), channel_id=1, source_target_pairs={{0,1},{1,2},{2,3},{3,0},{4,5},{5,6},{6,7},{7,4},{8,9},{9,10},{10,1... | collective-permute-start | bytes 786440 | tf_op jit(solution)/shard_map/ppermute | solution.py:649
  1299.2 68.7 %collective-permute-start.29 = (bf16[64,2048]{1,0:T(8,128)(2,1)S(1)}, bf16[64,2048]{1,0:T(8,128)(2,1)}, u32[]{:S(2)}, u32[]{:S(2)}) collective-permute-start(bf16[64,2048]{1,0:T(8,128)(2,1)S(1)} %get-tuple-element.152), channel_id=1, source_target_pairs={{0,3},{1,0},{2,1},{3,2},{4,7},{5,4},{6,5},{7,6},{8,11},{9,8},{10,9... | collective-permute-start | bytes 786440 | tf_op jit(solution)/shard_map/ppermute | solution.py:649
  1302.5 68.6 %collective-permute-start.28 = (bf16[64,2048]{1,0:T(8,128)(2,1)S(1)}, bf16[64,2048]{1,0:T(8,128)(2,1)}, u32[]{:S(2)}, u32[]{:S(2)}) collective-permute-start(bf16[64,2048]{1,0:T(8,128)(2,1)S(1)} %get-tuple-element.153), channel_id=1, source_target_pairs={{0,2},{1,3},{2,0},{3,1},{4,6},{5,7},{6,4},{7,5},{8,10},{9,11},{10,... | collective-permute-start | bytes 786440 | tf_op jit(solution)/shard_map/ppermute | solution.py:649
  1305.1 61.5 %all-to-all-start.3 = ((f32[32,1,128]{2,1,0:T(1,128)}), f32[32,1,128]{2,1,0:T(1,128)S(1)}, u32[]{:S(2)}, u32[]{:S(2)}) async-start(f32[32,1,128]{2,1,0:T(1,128)} %maximum_add_fusion.1), calls=%async_computation.6 | async-start | bytes 32768 | tf_op jit(solution)/shard_map/all_to_all | solution.py:929
  (99 other events, 2319.8 us)
Sparse Core Ops, SparseCore 0:
  48.4 89.8 all-gather.9
  140.1 54.2 all-gather.19
  196.4 54.2 all-gather.21
  252.4 67.5 all-gather.13
  407.3 68.6 all-gather.11
  478.4 107.6 all-gather.17
  588.5 72.9 all-gather.15
  760.2 87.1 reduce-scatter.4
  988.9 71.0 reduce-scatter.10
  1063.2 71.4 reduce-scatter.8
  1138.2 145.9 reduce-scatter.6
